TPU v7x, 32 devices: a whole 2x2x4 slice. The times are simulated.
32 devices in a mesh: dp: 2 (over y), ctx: 4 (over z), tp: 4 (over x, core).
Axes of the slice: x: 2, y: 2, z: 4, core: 2. Of those that a mesh axis runs over, the one named last changes fastest.
Arguments:
- hidden_in: bfloat16 [8192, 2048], P(('dp', 'ctx')), may hold values from -6 to 6
- seq_lengths: int32 [2, 3], P('dp'), may hold values from 1024 to 2048, as said below
- pack_order: int32 [2, 3], P('dp'), may hold values from 0 to 2, each once within a row
- norm_gain: bfloat16 [2048], P('dp'), may hold values from 0.5 to 1.5
- in_x_weight: bfloat16 [2048, 4096], P('dp', 'tp'), may hold values from -0.125 to 0.125
- in_z_weight: bfloat16 [2048, 4096], P('dp', 'tp'), may hold values from -0.125 to 0.125
- conv_weight: bfloat16 [4, 4096], P(None, ('tp', 'dp')), may hold values from -3 to 3
- conv_bias: bfloat16 [4096], P(('tp', 'dp')), may hold values from -0.5 to 0.5
- x_weight: bfloat16 [4096, 160], P(('tp', 'dp')), may hold values from -0.09375 to 0.09375
- dt_weight: bfloat16 [128, 4096], P('dp', 'tp'), may hold values from -0.5 to 0.5
- dt_bias: bfloat16 [4096], P(('tp', 'dp')), may hold values from -9 to -2.296875
- a_log: bfloat16 [4096, 16], P(('tp', 'dp')), may hold values from 0 to 2.765625
- skip_weight: bfloat16 [4096], P(('tp', 'dp')), may hold values from 0.5 to 1.5
- out_weight: bfloat16 [4096, 2048], P('tp', 'dp'), may hold values from -0.09375 to 0.09375
- out_grad: bfloat16 [8192, 2048], P(('dp', 'ctx')), may hold values from -6 to 6
Outputs:
- out: bfloat16 [8192, 2048], P(('dp', 'ctx'))
- grad_input: bfloat16 [8192, 2048], P(('dp', 'ctx'))
- grad_norm_gain: float32 [2048], P('dp')
- grad_in_x: float32 [2048, 4096], P('dp', 'tp')
- grad_in_z: float32 [2048, 4096], P('dp', 'tp')
- grad_conv_weight: float32 [4, 4096], P(None, ('tp', 'dp'))
- grad_conv_bias: float32 [4096], P(('tp', 'dp'))
- grad_x_weight: float32 [4096, 160], P(('tp', 'dp'))
- grad_dt_weight: float32 [128, 4096], P('dp', 'tp')
- grad_dt_bias: float32 [4096], P(('tp', 'dp'))
- grad_a_log: float32 [4096, 16], P(('tp', 'dp'))
- grad_skip: float32 [4096], P(('tp', 'dp'))
- grad_out_weight: float32 [4096, 2048], P('tp', 'dp')
Inputs may be any that keep to these rules, and one draw needn't show every extreme that they name: `seq_lengths`: in each group the 3 lengths sum to 4096; each is 1024 or more, and one is exactly 1024; some group has a sequence of the largest length. `pack_order`: each row is a permutation of 0 to 2.
All inputs are finite; a program needn't handle non-finite values.
Results may differ from a plain program's by a relative error of at most 0.012.
The roundings to bfloat16 on the way count: a program that leaves them out, or rounds other values in their place, can miss the bound.
Values may be sent and summed in bfloat16 or wider, within the bound.
A program may use at most 896 MiB of HBM per device.

v0:
```python
import math

import jax
import jax.numpy as jnp
from jax import lax
from jax.sharding import PartitionSpec as P

N = 16
R = 128
K = 4
ROW = 2048
MICRO = 2


EPSILON = 1e-05
PRECISE = lax.Precision.HIGHEST


def carried_in(value, axis, combine, identity, reverse):
    length, position = (lax.axis_size(axis), lax.axis_index(axis))
    everything = jax.tree.map(lambda part: lax.all_gather(part, axis), value)
    start = jax.tree.map(
        lambda part, zero: jnp.broadcast_to(jnp.asarray(zero, part.dtype), part.shape),
        value,
        identity,
    )

    def lap(k, before):
        at = length - 1 - k if reverse else k
        reached = at > position if reverse else at < position
        new = combine(before, jax.tree.map(lambda part: part[at], everything))
        return jax.tree.map(lambda a, b: jnp.where(reached, a, b), new, before)

    return lax.fori_loop(0, length, lap, start)


def shifted(value, axis, steps):
    count = lax.axis_size(axis)
    leading, last = (max(0, -steps), min(count, count - steps))
    return lax.ppermute(value, axis, [(source, source + steps) for source in range(leading, last)])


def affine_join(earlier, later):
    return (earlier[0] * later[0], later[0] * earlier[1] + later[1])


def contract_last(left, right):
    return lax.dot_general(
        left, right, (((1,), (1,)), ((), ())), preferred_element_type=jnp.float32
    )


def contract_first(left, right):
    return lax.dot_general(
        left, right, (((0,), (0,)), ((), ())), preferred_element_type=jnp.float32
    )


def seq_tables(lengths, arrangement):
    slot_ids = jnp.arange(lengths.shape[0], dtype=jnp.int32)
    ordered = jnp.sum(
        jnp.where(arrangement[:, None] == slot_ids[None, :], lengths[None, :], 0), axis=1
    )
    nat_start = jnp.cumsum(lengths) - lengths
    pack_start = jnp.cumsum(ordered) - ordered
    placed = jnp.sum(
        jnp.where(arrangement[None, :] == slot_ids[:, None], slot_ids[None, :], 0), axis=1
    )
    return (nat_start, pack_start, placed)


def find_slot(positions, starts):
    return jnp.sum((positions[:, None] >= starts[None, 1:]).astype(jnp.int32), axis=1)


def lookup_small(table_row, indices):
    slot_ids = jnp.arange(table_row.shape[0], dtype=jnp.int32)
    return jnp.sum(jnp.where(indices[:, None] == slot_ids[None, :], table_row[None, :], 0), axis=1)


def decay_at(step_part, decay_rate, keep_part):
    return jnp.exp(step_part[..., None, :] * decay_rate) * keep_part[..., None, None]


def forward_states(step_size, decay_rate, b_in, drive_in, keep_mask):
    length, channels = step_size.shape
    state_dim = decay_rate.shape[0]
    block_len = math.gcd(length, 16)
    block_count = length // block_len
    step_b = step_size.reshape(block_count, block_len, channels)
    push_b = (step_size * drive_in).reshape(block_count, block_len, channels)
    b_blocks = b_in.reshape(block_count, block_len, state_dim)
    keep_b = keep_mask.reshape(block_count, block_len)
    carry_state = jnp.zeros((block_count, state_dim, channels), jnp.float32)
    saved_states = []
    for offset in range(block_len):
        carry_state = (
            decay_at(step_b[:, offset], decay_rate, keep_b[:, offset]) * carry_state
            + push_b[:, offset, None, :] * b_blocks[:, offset, :, None]
        )
        saved_states.append(carry_state)
    local_states = jnp.stack(saved_states, axis=1)
    growth = (
        jnp.exp(jnp.cumsum(step_b, axis=1)[..., None, :] * decay_rate)
        * jnp.cumprod(keep_b, axis=1)[..., None, None]
    )
    total_mul, total_add = lax.associative_scan(
        affine_join, (growth[:, -1], local_states[:, -1]), axis=0
    )
    entry_state = carried_in(
        (total_mul[-1], total_add[-1]),
        "ctx",
        affine_join,
        (jnp.ones_like(total_mul[-1]), jnp.zeros_like(total_add[-1])),
        False,
    )[1]
    before_mul = jnp.concatenate([jnp.ones_like(total_mul[:1]), total_mul[:-1]], axis=0)
    before_add = jnp.concatenate([jnp.zeros_like(total_add[:1]), total_add[:-1]], axis=0)
    incoming = before_add + before_mul * entry_state[None]
    states = local_states + growth * incoming[:, None]
    return (states.reshape(length, state_dim, channels), entry_state)


def backward_states(step_size, decay_rate, keep_mask, dy_scan, c_out):
    length, channels = step_size.shape
    state_dim = decay_rate.shape[0]
    block_len = math.gcd(length, 16)
    block_count = length // block_len
    step_b = step_size.reshape(block_count, block_len, channels)
    keep_b = keep_mask.reshape(block_count, block_len)
    dy_blocks = dy_scan.reshape(block_count, block_len, channels)
    c_blocks = c_out.reshape(block_count, block_len, state_dim)
    carry_state = dy_blocks[:, -1, None, :] * c_blocks[:, -1, :, None]
    saved_states = [carry_state]
    for offset in range(block_len - 2, -1, -1):
        carry_state = (
            dy_blocks[:, offset, None, :] * c_blocks[:, offset, :, None]
            + decay_at(step_b[:, offset + 1], decay_rate, keep_b[:, offset + 1]) * carry_state
        )
        saved_states.append(carry_state)
    local_states = jnp.stack(saved_states[::-1], axis=1)
    step_after = jnp.concatenate([step_b[:, 1:], jnp.zeros_like(step_b[:, :1])], axis=1)
    keep_after = jnp.concatenate([keep_b[:, 1:], jnp.ones_like(keep_b[:, :1])], axis=1)
    spent_after = jnp.flip(jnp.cumsum(jnp.flip(step_after, 1), axis=1), 1)
    alive_after = jnp.flip(jnp.cumprod(jnp.flip(keep_after, 1), axis=1), 1)
    reach = jnp.exp(spent_after[..., None, :] * decay_rate) * alive_after[..., None, None]
    whole_mul = (
        jnp.exp(jnp.sum(step_b, axis=1)[:, None, :] * decay_rate)
        * jnp.prod(keep_b, axis=1)[:, None, None]
    )
    leave_add = decay_at(step_b[:, 0], decay_rate, keep_b[:, 0]) * local_states[:, 0]
    total_mul, total_add = lax.associative_scan(
        affine_join, (whole_mul, leave_add), reverse=True, axis=0
    )
    entry_grad = carried_in(
        (total_mul[0], total_add[0]),
        "ctx",
        affine_join,
        (jnp.ones_like(total_mul[0]), jnp.zeros_like(total_add[0])),
        True,
    )[1]
    after_mul = jnp.concatenate([total_mul[1:], jnp.ones_like(total_mul[:1])], axis=0)
    after_add = jnp.concatenate([total_add[1:], jnp.zeros_like(total_add[:1])], axis=0)
    incoming = after_add + after_mul * entry_grad[None]
    grad_state = local_states + reach * incoming[:, None]
    return grad_state.reshape(length, state_dim, channels)


def scan_grads(
    grad_state, states, entry_state, step_size, decay_rate, keep_mask, b_in, drive_in, dy_scan
):
    prior = jnp.concatenate([entry_state[None], states[:-1]], axis=0)
    log_grad = grad_state * prior * decay_at(step_size, decay_rate, keep_mask)
    along_b = jnp.einsum("tne,tn->te", grad_state, b_in, precision=PRECISE)
    d_step = jnp.einsum("tne,ne->te", log_grad, decay_rate, precision=PRECISE) + along_b * drive_in
    d_rate = jnp.einsum("tne,te->ne", log_grad, step_size, precision=PRECISE)
    d_bin = jnp.einsum("tne,te->tn", grad_state, step_size * drive_in, precision=PRECISE)
    d_cout = jnp.einsum("tne,te->tn", states, dy_scan, precision=PRECISE)
    return (d_step, d_rate, d_bin, d_cout, along_b * step_size)


def per_device(
    hidden_in,
    seq_lengths,
    pack_order,
    norm_gain,
    in_x_weight,
    in_z_weight,
    conv_weight,
    conv_bias,
    x_weight,
    dt_weight,
    dt_bias,
    a_log,
    skip_weight,
    out_weight,
    out_grad,
):
    ctx_index = lax.axis_index("ctx")
    natural_rows = hidden_in.shape[0]
    row_part = natural_rows // MICRO
    nat_start, pack_start, placed = seq_tables(seq_lengths[0], pack_order[0])
    whole_in, whole_grad = (
        lax.all_gather(hidden_in, "ctx", axis=0, tiled=True),
        lax.all_gather(out_grad, "ctx", axis=0, tiled=True),
    )
    totals = None
    out_blocks = []
    grad_blocks = []
    for micro_index in range(MICRO):
        weights_now = (
            lax.all_gather(norm_gain, "dp", axis=0, tiled=True),
            lax.all_gather(in_x_weight, "dp", axis=0, tiled=True),
            lax.all_gather(in_z_weight, "dp", axis=0, tiled=True),
            lax.all_gather(conv_weight, "dp", axis=1, tiled=True),
            lax.all_gather(conv_bias, "dp", axis=0, tiled=True),
            lax.all_gather(x_weight, "dp", axis=0, tiled=True),
            lax.all_gather(dt_weight, "dp", axis=0, tiled=True),
            lax.all_gather(dt_bias, "dp", axis=0, tiled=True),
            lax.all_gather(a_log, "dp", axis=0, tiled=True),
            lax.all_gather(skip_weight, "dp", axis=0, tiled=True),
            lax.all_gather(out_weight, "dp", axis=1, tiled=True),
        )
        (
            gain_vec,
            w_inx,
            w_inz,
            conv_taps,
            conv_shift,
            w_proj,
            w_step,
            step_bias,
            rate_log,
            skip_vec,
            w_out,
        ) = weights_now
        row_begin = micro_index * ROW
        positions = row_begin + ctx_index * row_part + jnp.arange(row_part, dtype=jnp.int32)
        slot_now = find_slot(positions, pack_start)
        source = (
            lookup_small(nat_start, lookup_small(pack_order[0], slot_now))
            + positions
            - lookup_small(pack_start, slot_now)
        )
        rows_in = jnp.take(whole_in, source, axis=0).astype(jnp.float32)
        rows_grad = jnp.take(whole_grad, source, axis=0)
        tap_masks = []
        for tap_index in range(K):
            earlier = positions - (K - 1 - tap_index)
            tap_masks.append(
                ((earlier >= row_begin) & (find_slot(earlier, pack_start) == slot_now)).astype(
                    jnp.float32
                )
            )
        keep_mask = tap_masks[K - 2]
        gain_full = gain_vec.astype(jnp.float32)
        inv_rms = lax.rsqrt(jnp.mean(rows_in * rows_in, axis=1, keepdims=True) + EPSILON)
        scaled = rows_in * inv_rms
        normed = (scaled * gain_full).astype(jnp.bfloat16)
        inner_x = jnp.dot(normed, w_inx, preferred_element_type=jnp.float32).astype(jnp.bfloat16)
        gate_z = jnp.dot(normed, w_inz, preferred_element_type=jnp.float32)
        halo_rows = shifted(inner_x[row_part - (K - 1) :], "ctx", 1)
        extended = jnp.concatenate([halo_rows, inner_x], axis=0).astype(jnp.float32)
        taps_full = conv_taps.astype(jnp.float32)
        conv_pre = conv_shift.astype(jnp.float32)[None, :]
        for tap_index in range(K):
            conv_pre = (
                conv_pre
                + taps_full[tap_index]
                * extended[tap_index : tap_index + row_part]
                * tap_masks[tap_index][:, None]
            )
        activated = jax.nn.silu(conv_pre).astype(jnp.bfloat16)
        drive_in = activated.astype(jnp.float32)
        projected = lax.psum(jnp.dot(activated, w_proj, preferred_element_type=jnp.float32), "tp")
        step_low = projected[:, :R].astype(jnp.bfloat16)
        b_in = projected[:, R : R + N]
        c_out = projected[:, R + N :]
        step_pre = jnp.dot(step_low, w_step, preferred_element_type=jnp.float32) + step_bias.astype(
            jnp.float32
        )
        step_size = jax.nn.softplus(step_pre)
        decay_rate = -jnp.exp(rate_log.astype(jnp.float32)).T
        states, entry_state = forward_states(step_size, decay_rate, b_in, drive_in, keep_mask)
        skip_full = skip_vec.astype(jnp.float32)
        scan_out = jnp.einsum("tne,tn->te", states, c_out, precision=PRECISE) + skip_full * drive_in
        gate_sig = jax.nn.sigmoid(gate_z)
        gated_out = (scan_out * gate_z * gate_sig).astype(jnp.bfloat16)
        branch = lax.psum(
            jnp.dot(gated_out, w_out, preferred_element_type=jnp.float32).astype(jnp.bfloat16), "tp"
        ).astype(jnp.float32)
        out_blocks.append((rows_in + branch).astype(jnp.bfloat16))
        d_gated = contract_last(rows_grad, w_out)
        g_out = contract_first(gated_out, rows_grad)
        dy_scan = d_gated * gate_z * gate_sig
        d_gate = (d_gated * scan_out * gate_sig * (1.0 + gate_z * (1.0 - gate_sig))).astype(
            jnp.bfloat16
        )
        g_skip = jnp.sum(dy_scan * drive_in, axis=0)
        grad_state = backward_states(step_size, decay_rate, keep_mask, dy_scan, c_out)
        d_step, d_rate, d_bin, d_cout, d_drive = scan_grads(
            grad_state,
            states,
            entry_state,
            step_size,
            decay_rate,
            keep_mask,
            b_in,
            drive_in,
            dy_scan,
        )
        d_pre = (d_step * jax.nn.sigmoid(step_pre)).astype(jnp.bfloat16)
        g_bias = jnp.sum(d_pre.astype(jnp.float32), axis=0)
        g_step = contract_first(step_low, d_pre)
        d_proj = lax.psum(
            jnp.concatenate([contract_last(d_pre, w_step), d_bin, d_cout], axis=1), "tp"
        ).astype(jnp.bfloat16)
        g_proj = contract_first(activated, d_proj)
        d_total = d_drive + dy_scan * skip_full + contract_last(d_proj, w_proj)
        conv_sig = jax.nn.sigmoid(conv_pre)
        d_conv = d_total * conv_sig * (1.0 + conv_pre * (1.0 - conv_sig))
        g_shift = jnp.sum(d_conv, axis=0)
        g_taps = jnp.stack(
            [
                jnp.sum(
                    d_conv
                    * tap_masks[tap_index][:, None]
                    * extended[tap_index : tap_index + row_part],
                    axis=0,
                )
                for tap_index in range(K)
            ],
            axis=0,
        )
        d_extended = jnp.zeros((row_part + K - 1, d_conv.shape[1]), jnp.float32)
        for tap_index in range(K):
            d_extended = d_extended + jnp.pad(
                d_conv * tap_masks[tap_index][:, None] * taps_full[tap_index],
                ((tap_index, K - 1 - tap_index), (0, 0)),
            )
        returned = shifted(d_extended[: K - 1], "ctx", -1)
        d_inner = (
            d_extended[K - 1 :] + jnp.pad(returned, ((row_part - (K - 1), 0), (0, 0)))
        ).astype(jnp.bfloat16)
        g_inx = contract_first(normed, d_inner)
        g_inz = contract_first(normed, d_gate)
        d_normed = lax.psum(contract_last(d_inner, w_inx) + contract_last(d_gate, w_inz), "tp")
        g_gain = jnp.sum(d_normed * scaled, axis=0)
        d_hat = d_normed * gain_full
        d_rows = inv_rms * (
            d_hat - scaled * jnp.mean(d_hat * scaled, axis=1, keepdims=True)
        ) + rows_grad.astype(jnp.float32)
        grad_blocks.append(d_rows.astype(jnp.bfloat16))
        new_terms = (
            g_gain,
            g_inx,
            g_inz,
            g_taps,
            g_shift,
            g_proj,
            g_step,
            g_bias,
            (d_rate * decay_rate).T,
            g_skip,
            g_out,
        )
        totals = new_terms if totals is None else jax.tree.map(jnp.add, totals, new_terms)
    both_out, both_grad = (
        lax.all_gather(jnp.concatenate(out_blocks, axis=0), "ctx", axis=0, tiled=True),
        lax.all_gather(jnp.concatenate(grad_blocks, axis=0), "ctx", axis=0, tiled=True),
    )
    natural = ctx_index * natural_rows + jnp.arange(natural_rows, dtype=jnp.int32)
    seq_index = find_slot(natural, nat_start)
    slot_index = lookup_small(placed, seq_index)
    packed = lookup_small(pack_start, slot_index) + natural - lookup_small(nat_start, seq_index)
    gather_index = (
        packed % ROW // row_part * (MICRO * row_part) + packed // ROW * row_part + packed % row_part
    )
    out_natural = jnp.take(both_out, gather_index, axis=0)
    grad_natural = jnp.take(both_grad, gather_index, axis=0)
    pieces_back = (
        lax.psum_scatter(totals[0], ("dp", "ctx"), scatter_dimension=0, tiled=True),
        lax.psum_scatter(totals[1], ("dp", "ctx"), scatter_dimension=0, tiled=True),
        lax.psum_scatter(totals[2], ("dp", "ctx"), scatter_dimension=0, tiled=True),
        lax.psum_scatter(totals[3], ("dp", "ctx"), scatter_dimension=1, tiled=True),
        lax.psum_scatter(totals[4], ("dp", "ctx"), scatter_dimension=0, tiled=True),
        lax.psum_scatter(totals[5], ("dp", "ctx"), scatter_dimension=0, tiled=True),
        lax.psum_scatter(totals[6], ("dp", "ctx"), scatter_dimension=0, tiled=True),
        lax.psum_scatter(totals[7], ("dp", "ctx"), scatter_dimension=0, tiled=True),
        lax.psum_scatter(totals[8], ("dp", "ctx"), scatter_dimension=0, tiled=True),
        lax.psum_scatter(totals[9], ("dp", "ctx"), scatter_dimension=0, tiled=True),
        lax.psum_scatter(totals[10], ("dp", "ctx"), scatter_dimension=1, tiled=True),
    )
    full_grads = (
        lax.all_gather(pieces_back[0], "ctx", axis=0, tiled=True),
        lax.all_gather(pieces_back[1], "ctx", axis=0, tiled=True),
        lax.all_gather(pieces_back[2], "ctx", axis=0, tiled=True),
        lax.all_gather(pieces_back[3], "ctx", axis=1, tiled=True),
        lax.all_gather(pieces_back[4], "ctx", axis=0, tiled=True),
        lax.all_gather(pieces_back[5], "ctx", axis=0, tiled=True),
        lax.all_gather(pieces_back[6], "ctx", axis=0, tiled=True),
        lax.all_gather(pieces_back[7], "ctx", axis=0, tiled=True),
        lax.all_gather(pieces_back[8], "ctx", axis=0, tiled=True),
        lax.all_gather(pieces_back[9], "ctx", axis=0, tiled=True),
        lax.all_gather(pieces_back[10], "ctx", axis=1, tiled=True),
    )
    return (
        out_natural,
        grad_natural,
        full_grads[0],
        full_grads[1],
        full_grads[2],
        full_grads[3],
        full_grads[4],
        full_grads[5],
        full_grads[6],
        full_grads[7],
        full_grads[8],
        full_grads[9],
        full_grads[10],
    )


def solution(mesh):
    in_specs = (
        P(("dp", "ctx"), None),
        P("dp", None),
        P("dp", None),
        P("dp"),
        P("dp", "tp"),
        P("dp", "tp"),
        P(None, ("tp", "dp")),
        P(("tp", "dp")),
        P(("tp", "dp"), None),
        P("dp", "tp"),
        P(("tp", "dp")),
        P(("tp", "dp"), None),
        P(("tp", "dp")),
        P("tp", "dp"),
        P(("dp", "ctx"), None),
    )
    out_specs = (
        P(("dp", "ctx"), None),
        P(("dp", "ctx"), None),
        P("dp"),
        P("dp", "tp"),
        P("dp", "tp"),
        P(None, ("tp", "dp")),
        P(("tp", "dp")),
        P(("tp", "dp"), None),
        P("dp", "tp"),
        P(("tp", "dp")),
        P(("tp", "dp"), None),
        P(("tp", "dp")),
        P("tp", "dp"),
    )
    return jax.shard_map(
        per_device, mesh=mesh, in_specs=in_specs, out_specs=out_specs, check_vma=False
    )
```

profile of v0, /device:TPU:0, one launch (start us, length us, event | category | flops | bytes accessed | tf_op | source)
XLA Modules:
  0.0 4203.3 jit_solution(16205488290459818443)
XLA Ops:
  66.1 233.0 %all-gather.18.cloned.1.call-done = bf16[4096,2048]{1,0:T(8,128)(2,1)} async-done(((bf16[1024,2048]{1,0:T(8,128)(2,1)}), bf16[4096,2048]{1,0:T(8,128)(2,1)}) %all-gather.18.cloned.1.call-update) | async-done | bytes 16777232 | tf_op jit(solution)/shard_map/all_gather | solution.py:204
  312.3 43.4 %all-gather.20.cloned.1.call-done = bf16[2048,1024]{1,0:T(8,128)(2,1)} async-done(((bf16[1024,1024]{1,0:T(8,128)(2,1)}), bf16[2048,1024]{1,0:T(8,128)(2,1)}) %all-gather.20.cloned.1.call-update) | async-done | bytes 4194320 | tf_op jit(solution)/shard_map/all_gather | solution.py:213
  363.8 14.8 gather_fusion.1
  387.4 256.6 %all-gather.28.cloned.1.call-done = bf16[4096,2048]{1,0:T(8,128)(2,1)} async-done(((bf16[1024,2048]{1,0:T(8,128)(2,1)}), bf16[4096,2048]{1,0:T(8,128)(2,1)}) %all-gather.28.cloned.1.call-update) | async-done | bytes 16777232 | tf_op jit(solution)/shard_map/all_gather | solution.py:205
  670.9 29.5 all-gather.24.cloned.1.call-done
  712.5 46.1 %all-gather.22.cloned.1.call-done = bf16[2048,1024]{1,0:T(8,128)(2,1)} async-done(((bf16[1024,1024]{1,0:T(8,128)(2,1)}), bf16[2048,1024]{1,0:T(8,128)(2,1)}) %all-gather.22.cloned.1.call-update) | async-done | bytes 4194320 | tf_op jit(solution)/shard_map/all_gather | solution.py:214
  806.5 21.0 all-reduce.118.cloned.1.call-done
  1130.8 15.1 add_dynamic-update-slice_fusion.1
  1168.6 22.6 exponential_multiply_fusion.1
  1506.2 13.8 all_gather.134
  1526.6 14.1 all_gather.133
  1564.1 13.9 all_gather.132
  1584.5 13.9 all_gather.131
  1972.4 13.9 all_gather.128
  1986.3 13.9 all_gather.127
  2018.3 13.9 all_gather.123
  2032.2 13.9 all_gather.122
  2057.1 46.7 %fusion.11 = (f32[512,16,1024]{2,1,0:T(8,128)}, f32[512,16,1024]{2,1,0:T(8,128)}) fusion(f32[32,16,16,1024]{3,2,1,0:T(8,128)} %copy-done.11, f32[32,16,1024]{2,1,0:T(8,128)S(1)} %multiply_add_fusion.46, f32[512]{0:T(512)S(1)} %copy-done.611, f32[16,1024]{1,0:T(8,128)S(1)} %fusion.149, f32[512,1024]{1,0:T(8,128)S(1)} %bitcast.668, ...), kind=kLoop, calls=%fused_computation.31 | loop fusion | flops 67108864 | bytes 142675968 | tf_op jit(solution)/shard_map/add | solution.py:120
  2103.7 22.8 slice.2179
  2126.6 23.0 fusion.239
  2149.6 22.8 slice.2249
  2172.5 23.4 fusion.241
  2200.2 74.3 %multiply_reduce_fusion = (f32[1024,16]{0,1:T(8,128)S(1)}, f32[1024,16]{0,1:T(8,128)S(1)}, f32[512,16,1024]{2,1,0:T(8,128)}, f32[512,16,1024]{2,1,0:T(8,128)}) fusion(f32[1024,512]{0,1:T(8,128)S(1)} %bitcast.657, f32[512]{0:T(512)S(1)} %copy-done.494, f32[16,1024]{1,0:T(8,128)S(1)} %fusion.149, f32[512,1024]{1,0:T(8,128)S(1)} %copy-done.4, ...), kind=kLoop, calls=%fused_computation.32 | loop fusion | flops 184516608 | bytes 218308608 | tf_op jit(solution)/shard_map/tne,te->ne/dot_general | solution.py:176
  2275.2 23.0 fusion.245
  2298.2 49.3 %multiply_reduce_fusion.3 = (f32[1024,512]{0,1:T(8,128)}, f32[1024,512]{0,1:T(8,128)}) fusion(f32[1024,16]{0,1:T(8,128)S(1)} %get-tuple-element.989, f32[512]{0:T(512)S(1)} %copy-done.491, f32[16,1024]{1,0:T(8,128)S(1)} %fusion.149, f32[512,1024]{1,0:T(8,128)S(1)} %copy-done.1, f32[512,16,1024]{2,1,0:T(8,128)} %get-tuple-element.665, ...), kind=kLoop, calls=%fused_computation.35 | loop fusion | flops 116391936 | bytes 142741504 | tf_op jit(solution)/shard_map/tne,ne->te/dot_general | solution.py:175
  2347.6 22.5 fusion.242
  2403.0 41.4 fusion.64
  2444.6 41.5 fusion.60
  2486.2 41.7 fusion.62
  2528.0 42.1 %fusion.66 = f32[512,1,16]{2,1,0:T(1,128)} fusion(f32[512,16,1024]{2,1,0:T(8,128)} %get-tuple-element.665, f32[512,1024,1]{1,0,2:T(8,128)} %bitcast.658), kind=kOutput, calls=%fused_computation.131 | convolution fusion | flops 100663296 | bytes 35684352 | tf_op jit(solution)/shard_map/tne,te->tn/dot_general | solution.py:177
  2572.9 17.1 all-reduce.121
  2659.4 33.5 reduce-scatter.12.cloned.1.call-done
  2693.0 151.6 %reduce-scatter.10.cloned.1.call-done = f32[256,1024]{1,0:T(8,128)} async-done(((f32[2048,1024]{1,0:T(8,128)}), f32[256,1024]{1,0:T(8,128)}) %reduce-scatter.10.cloned.1.call-update) | async-done | bytes 1048592 | tf_op jit(solution)/shard_map/reduce_scatter | solution.py:383
  2844.8 155.9 %all-reduce.116.cloned.1.call-done = (f32[512,2048]{1,0:T(8,128)}, f32[512,2048]{1,0:T(8,128)}) async-done(((f32[512,2048]{1,0:T(8,128)}, f32[512,2048]{1,0:T(8,128)}), (f32[512,2048]{1,0:T(8,128)}, f32[512,2048]{1,0:T(8,128)})) %all-reduce.116.cloned.1.call-update) | async-done | bytes 8388624 | tf_op jit(solution)/shard_map/psum | solution.py:347
  3004.2 85.5 %all-reduce.120.cloned.1.call-done = (bf16[512,2048]{1,0:T(8,128)(2,1)}, bf16[512,2048]{1,0:T(8,128)(2,1)}) async-done(((bf16[512,2048]{1,0:T(8,128)(2,1)}, bf16[512,2048]{1,0:T(8,128)(2,1)}), (bf16[512,2048]{1,0:T(8,128)(2,1)}, bf16[512,2048]{1,0:T(8,128)(2,1)})) %all-reduce.120.cloned.1.call-update) | async-done | bytes 4194320 | tf_op jit(solution)/shard_map/psum | solution.py:289
  3112.2 42.8 %reduce-scatter.22.cloned.1.call-done = f32[128,4]{1,0:T(8,128)} async-done(((f32[1024,4]{1,0:T(8,128)}), f32[128,4]{1,0:T(8,128)}) %reduce-scatter.22.cloned.1.call-update) | async-done | bytes 2064
  3167.7 43.4 %reduce-scatter.18.cloned.1.call-done = f32[128,16]{0,1:T(8,128)} async-done(((f32[1024,16]{0,1:T(8,128)}), f32[128,16]{0,1:T(8,128)}) %reduce-scatter.18.cloned.1.call-update) | async-done | bytes 8208 | tf_op jit(solution)/shard_map/reduce_scatter | solution.py:390
  3224.4 51.1 %reduce-scatter.16.cloned.1.call-done = f32[16,1024]{1,0:T(8,128)} async-done(((f32[128,1024]{1,0:T(8,128)}), f32[16,1024]{1,0:T(8,128)}) %reduce-scatter.16.cloned.1.call-update) | async-done | bytes 65552 | tf_op jit(solution)/shard_map/reduce_scatter | solution.py:388
  3275.6 14.6 all_gather.142
  3290.2 50.3 %reduce-scatter.14.cloned.1.call-done = f32[128,160]{0,1:T(8,128)} async-done(((f32[1024,160]{0,1:T(8,128)}), f32[128,160]{0,1:T(8,128)}) %reduce-scatter.14.cloned.1.call-update) | async-done | bytes 81936 | tf_op jit(solution)/shard_map/reduce_scatter | solution.py:387
  3340.5 15.1 all_gather.141
  3355.7 37.5 all-reduce.106
  3428.4 76.3 %all-gather.34.cloned.1.call-done = f32[1024,1024]{1,0:T(8,128)} async-done(((f32[256,1024]{1,0:T(8,128)}), f32[1024,1024]{1,0:T(8,128)}) %all-gather.34.cloned.1.call-update) | async-done | bytes 4194320 | tf_op jit(solution)/shard_map/all_gather | solution.py:397
  3504.7 80.8 %all-gather.32.cloned.1.call-done = f32[1024,1024]{1,0:T(8,128)} async-done(((f32[256,1024]{1,0:T(8,128)}), f32[1024,1024]{1,0:T(8,128)}) %all-gather.32.cloned.1.call-update) | async-done | bytes 4194320 | tf_op jit(solution)/shard_map/all_gather | solution.py:396
  3585.5 287.6 %all-gather.30.cloned.1.call-done = bf16[4096,2048]{1,0:T(8,128)(2,1)} async-done(((bf16[1024,2048]{1,0:T(8,128)(2,1)}), bf16[4096,2048]{1,0:T(8,128)(2,1)}) %all-gather.30.cloned.1.call-update) | async-done | bytes 16777232 | tf_op jit(solution)/shard_map/all_gather | solution.py:370
  3873.1 16.7 gather_fusion.5
  3889.8 270.3 %all-gather.26.cloned.1.call-done = bf16[4096,2048]{1,0:T(8,128)(2,1)} async-done(((bf16[1024,2048]{1,0:T(8,128)(2,1)}), bf16[4096,2048]{1,0:T(8,128)(2,1)}) %all-gather.26.cloned.1.call-update) | async-done | bytes 16777232 | tf_op jit(solution)/shard_map/all_gather | solution.py:369
  4160.1 16.7 gather_fusion.2
  (2201 shorter events, 1462.5 us)
Async XLA Ops:
  7.2 291.9 %all-gather.18.cloned.1.call-start = ((), (), s32[]{:S(2)}) async-start(), calls=%async_computation.7 | async-start | bytes 20971520 | tf_op jit(solution)/shard_map/all_gather | solution.py:204
  7.9 347.7 %all-gather.20.cloned.1.call-start = ((), (), s32[]{:S(2)}) async-start(), calls=%async_computation.8 | async-start | bytes 6291456 | tf_op jit(solution)/shard_map/all_gather | solution.py:213
  8.7 635.3 %all-gather.28.cloned.1.call-start = ((), (), s32[]{:S(2)}) async-start(), calls=%async_computation.12 | async-start | bytes 20971520 | tf_op jit(solution)/shard_map/all_gather | solution.py:205
  9.5 691.0 %all-gather.24.cloned.1.call-start = ((), (), s32[]{:S(2)}) async-start(), calls=%async_computation.10 | async-start | bytes 6291456 | tf_op jit(solution)/shard_map/all_gather | solution.py:222
  10.1 748.5 %all-gather.22.cloned.1.call-start = ((), (), s32[]{:S(2)}) async-start(), calls=%async_computation.9 | async-start | bytes 6291456 | tf_op jit(solution)/shard_map/all_gather | solution.py:214
  10.7 48.8 %copy-start.276 = (bf16[64,1024]{1,0:T(8,128)(2,1)S(1)}, bf16[64,1024]{1,0:T(8,128)(2,1)}, u32[]{:S(2)}) copy-start(bf16[64,1024]{1,0:T(8,128)(2,1)} %param.36) | copy-start | bytes 393220
  10.7 816.9 %all-reduce.118.cloned.1.call-start = ((), (), s32[]{:S(2)}) async-start(), calls=%async_computation.25 | async-start | bytes 1310720 | tf_op jit(solution)/shard_map/psum | solution.py:275
  13.6 770.9 %copy-start.490 = (f32[512]{0:T(512)}, f32[512]{0:T(512)S(1)}, u32[]{:S(2)}) copy-start(f32[512]{0:T(512)S(1)} %get-tuple-element.685) | copy-start | bytes 6148
  14.5 744.1 %copy-start.493 = (f32[512]{0:T(512)}, f32[512]{0:T(512)S(1)}, u32[]{:S(2)}) copy-start(f32[512]{0:T(512)S(1)} %get-tuple-element.689) | copy-start | bytes 6148
  27.5 804.4 %copy-start.482 = (f32[2,1,512]{2,1,0:T(1,128)}, f32[2,1,512]{2,1,0:T(1,128)S(1)}, u32[]{:S(2)}) copy-start(f32[2,1,512]{2,1,0:T(1,128)S(1)} %convert_element_type.318) | copy-start | bytes 12292
  36.8 747.8 %copy-start.208 = (f32[2048]{0:T(1024)}, f32[2048]{0:T(1024)S(1)}, u32[]{:S(2)}) copy-start(f32[2048]{0:T(1024)S(1)} %convert_element_type.260) | copy-start | bytes 24580
  36.9 721.7 %copy-start.484 = (pred[512]{0:T(512)(128)(4,1)}, pred[512]{0:T(512)(128)(4,1)S(1)}, u32[]{:S(2)}) copy-start(pred[512]{0:T(512)(128)(4,1)S(1)} %get-tuple-element.691) | copy-start | bytes 1540
  36.9 747.6 %copy-start.487 = (pred[512]{0:T(512)(128)(4,1)}, pred[512]{0:T(512)(128)(4,1)S(1)}, u32[]{:S(2)}) copy-start(pred[512]{0:T(512)(128)(4,1)S(1)} %get-tuple-element.687) | copy-start | bytes 1540
  65.1 766.8 %copy-start.80 = (bf16[128,1024]{1,0:T(8,128)(2,1)}, bf16[128,1024]{1,0:T(8,128)(2,1)S(1)}, u32[]{:S(2)}) copy-start(bf16[128,1024]{1,0:T(8,128)(2,1)S(1)} %all_gather.119) | copy-start | bytes 786436
  311.5 48.7 %copy-start.8 = (bf16[512,2048]{1,0:T(8,128)(2,1)}, bf16[512,2048]{1,0:T(8,128)(2,1)S(1)}, u32[]{:S(2)}) copy-start(bf16[512,2048]{1,0:T(8,128)(2,1)S(1)} %gather_fusion) | copy-start | bytes 6291460
  312.2 472.4 %copy-start.478 = (f32[512]{0:T(512)}, f32[512]{0:T(512)S(1)}, u32[]{:S(2)}) copy-start(f32[512]{0:T(512)S(1)} %add_rsqrt_fusion.1) | copy-start | bytes 6148
  360.2 424.0 %collective-permute-start = (bf16[3,1024]{1,0:T(4,128)(2,1)S(1)}, bf16[3,1024]{1,0:T(4,128)(2,1)S(1)}, u32[]{:S(2)}, u32[]{:S(2)}) collective-permute-start(bf16[3,1024]{1,0:T(4,128)(2,1)S(1)} %slice.1894), channel_id=1, source_target_pairs={{0,4},{4,8},{8,12},{1,5},{5,9},{9,13},{2,6},{6,10},{10,14},{3,7},{... | collective-permute-start | bytes 18440 | tf_op jit(solution)/shard_map/ppermute | solution.py:40
  378.6 380.0 %copy-start.5 = (bf16[512,2048]{1,0:T(8,128)(2,1)}, bf16[512,2048]{1,0:T(8,128)(2,1)S(1)}, u32[]{:S(2)}) copy-start(bf16[512,2048]{1,0:T(8,128)(2,1)S(1)} %gather_fusion.1) | copy-start | bytes 6291460
  379.3 379.3 %copy-start.480 = (f32[512]{0:T(512)}, f32[512]{0:T(512)S(1)}, u32[]{:S(2)}) copy-start(f32[512]{0:T(512)S(1)} %add_rsqrt_fusion) | copy-start | bytes 6148
  383.9 326.9 %collective-permute-start.1 = (bf16[3,1024]{1,0:T(4,128)(2,1)S(1)}, bf16[3,1024]{1,0:T(4,128)(2,1)S(1)}, u32[]{:S(2)}, u32[]{:S(2)}) collective-permute-start(bf16[3,1024]{1,0:T(4,128)(2,1)S(1)} %slice.2004), channel_id=1, source_target_pairs={{0,4},{4,8},{8,12},{1,5},{5,9},{9,13},{2,6},{6,10},{10,14},{3,7},{... | collective-permute-start | bytes 18440 | tf_op jit(solution)/shard_map/ppermute | solution.py:40
  710.8 47.8 %copy-start.640 = (f32[1,1024]{1,0:T(1,128)S(1)}, f32[1,1024]{1,0:T(1,128)}, u32[]{:S(2)}) copy-start(f32[1,1024]{1,0:T(1,128)} %get-tuple-element.996) | copy-start | bytes 12292
  710.8 47.8 %copy-start.642 = (f32[1,1024]{1,0:T(1,128)S(1)}, f32[1,1024]{1,0:T(1,128)}, u32[]{:S(2)}) copy-start(f32[1,1024]{1,0:T(1,128)} %get-tuple-element.997) | copy-start | bytes 12292
  710.8 47.8 %copy-start.644 = (f32[1,1024]{1,0:T(1,128)S(1)}, f32[1,1024]{1,0:T(1,128)}, u32[]{:S(2)}) copy-start(f32[1,1024]{1,0:T(1,128)} %get-tuple-element.998) | copy-start | bytes 12292
  710.8 47.8 %copy-start.646 = (f32[1,1024]{1,0:T(1,128)S(1)}, f32[1,1024]{1,0:T(1,128)}, u32[]{:S(2)}) copy-start(f32[1,1024]{1,0:T(1,128)} %get-tuple-element.999) | copy-start | bytes 12292
  770.1 61.7 %copy-start.20 = (bf16[512,1024]{1,0:T(8,128)(2,1)}, bf16[512,1024]{1,0:T(8,128)(2,1)S(1)}, u32[]{:S(2)}) copy-start(bf16[512,1024]{1,0:T(8,128)(2,1)S(1)} %get-tuple-element.669) | copy-start | bytes 3145732
  793.5 1865.4 %reduce-scatter.20.cloned.1.call-start = ((), (), s32[]{:S(2)}) async-start(), calls=%async_computation.21 | async-start | bytes 9437184 | tf_op jit(solution)/shard_map/reduce_scatter | solution.py:392
  838.0 321.7 %copy-start = (f32[512,1024]{1,0:T(8,128)}, f32[512,1024]{1,0:T(8,128)S(1)}, u32[]{:S(2)}) copy-start(f32[512,1024]{1,0:T(8,128)S(1)} %get-tuple-element.682) | copy-start | bytes 6291460
  856.5 289.3 %copy-start.238 = (f32[32,1,16]{2,0,1:T(8,128)}, f32[32,1,16]{2,0,1:T(8,128)S(1)}, u32[]{:S(2)}) copy-start(f32[32,1,16]{2,0,1:T(8,128)S(1)} %copy.849) | copy-start | bytes 6148
  2200.2 74.3 %copy-start.241 = (bf16[1024,16]{0,1:T(8,128)(2,1)S(1)}, bf16[1024,16]{0,1:T(8,128)(2,1)}, u32[]{:S(2)}) copy-start(bf16[1024,16]{0,1:T(8,128)(2,1)} %copy-done.240) | copy-start | bytes 98308
  2200.2 75.0 %copy-start.176 = (f32[512,16,1]{1,2,0:T(1,128)S(1)}, f32[512,16,1]{1,2,0:T(1,128)}, u32[]{:S(2)}) copy-start(f32[512,16,1]{1,2,0:T(1,128)} %copy.758) | copy-start | bytes 98308
  2298.2 49.3 %copy-start.175 = (f32[512,16,1]{1,2,0:T(1,128)S(1)}, f32[512,16,1]{1,2,0:T(1,128)}, u32[]{:S(2)}) copy-start(f32[512,16,1]{1,2,0:T(1,128)} %copy.746) | copy-start | bytes 98308
  2381.1 190.1 %copy-start.37 = (bf16[512,1024]{1,0:T(8,128)(2,1)}, bf16[512,1024]{1,0:T(8,128)(2,1)S(1)}, u32[]{:S(2)}) copy-start(bf16[512,1024]{1,0:T(8,128)(2,1)S(1)} %get-tuple-element.676) | copy-start | bytes 3145732
  2391.3 301.7 %reduce-scatter.12.cloned.1.call-start = ((), (), s32[]{:S(2)}) async-start(), calls=%async_computation.16 | async-start | bytes 9437184 | tf_op jit(solution)/shard_map/reduce_scatter | solution.py:384
  2403.0 441.7 %reduce-scatter.10.cloned.1.call-start = ((), (), s32[]{:S(2)}) async-start(), calls=%async_computation.14 | async-start | bytes 9437184 | tf_op jit(solution)/shard_map/reduce_scatter | solution.py:383
  2528.0 43.1 %copy-start.81 = (bf16[128,1024]{1,0:T(8,128)(2,1)S(1)}, bf16[128,1024]{1,0:T(8,128)(2,1)}, u32[]{:S(2)}) copy-start(bf16[128,1024]{1,0:T(8,128)(2,1)} %copy-done.80) | copy-start | bytes 786436
  2599.0 10.0 collective-permute-start.3
  2607.5 7.7 collective-permute-start.2
  2621.3 379.4 %all-reduce.116.cloned.1.call-start = ((), (), s32[]{:S(2)}) async-start(), calls=%async_computation.24 | async-start | bytes 16777216 | tf_op jit(solution)/shard_map/psum | solution.py:347
  2639.1 450.6 %all-reduce.120.cloned.1.call-start = ((), (), s32[]{:S(2)}) async-start(), calls=%async_computation.26 | async-start | bytes 8388608 | tf_op jit(solution)/shard_map/psum | solution.py:289
  2650.0 504.9 %reduce-scatter.22.cloned.1.call-start = ((), (), s32[]{:S(2)}) async-start(), calls=%async_computation.23 | async-start | bytes 589824
  2651.8 559.3 %reduce-scatter.18.cloned.1.call-start = ((), (), s32[]{:S(2)}) async-start(), calls=%async_computation.20 | async-start | bytes 73728 | tf_op jit(solution)/shard_map/reduce_scatter | solution.py:390
  2653.2 622.4 %reduce-scatter.16.cloned.1.call-start = ((), (), s32[]{:S(2)}) async-start(), calls=%async_computation.19 | async-start | bytes 589824 | tf_op jit(solution)/shard_map/reduce_scatter | solution.py:388
  2655.9 684.6 %reduce-scatter.14.cloned.1.call-start = ((), (), s32[]{:S(2)}) async-start(), calls=%async_computation.18 | async-start | bytes 737280 | tf_op jit(solution)/shard_map/reduce_scatter | solution.py:387
  2658.8 769.6 %all-gather.36.cloned.1.call-start = ((), (), s32[]{:S(2)}) async-start(), calls=%async_computation.22 | async-start | bytes 5242880 | tf_op jit(solution)/shard_map/all_gather | solution.py:405
  2659.4 845.3 %all-gather.34.cloned.1.call-start = ((), (), s32[]{:S(2)}) async-start(), calls=%async_computation.17 | async-start | bytes 5242880 | tf_op jit(solution)/shard_map/all_gather | solution.py:397
  2693.0 892.5 %all-gather.32.cloned.1.call-start = ((), (), s32[]{:S(2)}) async-start(), calls=%async_computation.15 | async-start | bytes 5242880 | tf_op jit(solution)/shard_map/all_gather | solution.py:396
  2844.7 1028.4 %all-gather.30.cloned.1.call-start = ((), (), s32[]{:S(2)}) async-start(), calls=%async_computation.13 | async-start | bytes 20971520 | tf_op jit(solution)/shard_map/all_gather | solution.py:370
  3103.4 1056.7 %all-gather.26.cloned.1.call-start = ((), (), s32[]{:S(2)}) async-start(), calls=%async_computation.11 | async-start | bytes 20971520 | tf_op jit(solution)/shard_map/all_gather | solution.py:369
  (715 other events, 5850.5 us)
Sparse Core Ops, SparseCore 0:
  9.6 289.4 all-gather.17
  300.6 54.9 all-gather.19
  357.2 286.7 all-gather.27
  645.4 54.9 all-gather.23
  701.8 56.7 all-gather.21
  793.6 33.9 all-reduce.117
  2391.4 149.4 reduce-scatter.19
  2544.9 147.9 reduce-scatter.11
  2696.6 148.0 reduce-scatter.9
  2848.4 152.1 all-reduce.115
  3003.8 85.8 all-reduce.119
  3092.9 62.0 reduce-scatter.21
  3158.4 52.6 reduce-scatter.17
  3214.7 60.8 reduce-scatter.15
  3278.7 61.7 reduce-scatter.13
  3342.0 81.6 all-gather.35
  3425.2 79.4 all-gather.33
  3506.2 79.2 all-gather.31
  3587.7 285.2 all-gather.29
  3875.1 284.9 all-gather.25
where the time goes:
time: 4220 us; the launch traced here: 4200 us
  waiting for transfers between devices  1970 us (47%)
  other arithmetic  784 us (19%)
  local copies, waits for them, and re-layouts  738 us (17%)
  matrix products  382 us (9%)
  blocking collectives  295 us (7%)
    unnamed x60, other arithmetic  354 us
    all_gather x1, waiting for transfers between devices, per_device(): lax.all_gather(jnp.concatenate(grad_blocks, axis=0), 'ctx', axis=0, tiled...  288 us
    all_gather x1, waiting for transfers between devices, per_device(): lax.all_gather(jnp.concatenate(out_blocks, axis=0), 'ctx', axis=0, tiled=...  270 us
    all_gather x1, waiting for transfers between devices, per_device(): lax.all_gather(out_grad, 'ctx', axis=0, tiled=True)  257 us
    all_gather x1, waiting for transfers between devices, per_device(): lax.all_gather(hidden_in, 'ctx', axis=0, tiled=True)  233 us
    psum x1, waiting for transfers between devices, per_device(): lax.psum(contract_last(d_inner, w_inx) + contract_last(d_gate, w_inz), 'tp')  156 us
    reduce_scatter x1, waiting for transfers between devices, per_device(): lax.psum_scatter(totals[1], ('dp', 'ctx'), scatter_dimension=0, tiled=True)  152 us
    unnamed x1577, local copies, waits for them, and re-layouts  146 us
  transfers between devices with their start and end apart: 24, of which 19 were waited for; matrix products, arithmetic and copies ran while one was open for 10% of the time, Pallas kernels for 0%

commit v1 on v0

v1 whole, which is shorter than its diff:
```python
import jax
import jax.numpy as jnp
from jax import lax
from jax.experimental import pallas as pl
from jax.experimental.pallas import tpu as pltpu
from jax.sharding import PartitionSpec as P

N = 16
R = 128
K = 4
ROW = 2048
MICRO = 2
EPSILON = 1e-05

LANES = 128
SEGS = 8
FAR = 1e30
LOG2E = 1.4426950408889634
LN2 = 0.6931471805599453
F32 = jnp.float32
BF16 = jnp.bfloat16


def contract_last(left, right):
    return lax.dot_general(left, right, (((1,), (1,)), ((), ())), preferred_element_type=F32)


def contract_first(left, right):
    return lax.dot_general(left, right, (((0,), (0,)), ((), ())), preferred_element_type=F32)


def shifted(value, axis, steps):
    count = lax.axis_size(axis)
    leading, last = (max(0, -steps), min(count, count - steps))
    return lax.ppermute(value, axis, [(source, source + steps) for source in range(leading, last)])


def piece_starts(lengths, arrangement):
    count = lengths.shape[0]
    ids = jnp.arange(count, dtype=jnp.int32)
    ordered = jnp.sum(jnp.where(arrangement[:, None] == ids[None, :], lengths[None, :], 0), axis=1)
    nat_start = jnp.cumsum(lengths) - lengths
    pack_start = jnp.cumsum(ordered) - ordered
    rows = jnp.arange(1, MICRO, dtype=jnp.int32) * ROW
    slot = jnp.sum((rows[:, None] >= pack_start[None, 1:]).astype(jnp.int32), axis=1)
    in_slot = slot[:, None] == ids[None, :]
    sequence = jnp.sum(jnp.where(in_slot, arrangement[None, :], 0), axis=1)
    begun = jnp.sum(jnp.where(in_slot, pack_start[None, :], 0), axis=1)
    source = (
        jnp.sum(jnp.where(sequence[:, None] == ids[None, :], nat_start[None, :], 0), axis=1)
        + rows
        - begun
    )
    return jnp.concatenate([nat_start, source])


def exact_parts(value):
    high = value.astype(BF16)
    rest = value - high.astype(F32)
    mid = rest.astype(BF16)
    return high, mid, (rest - mid.astype(F32)).astype(BF16)


def spread_columns(table_ref, out_ref, extra_ref, turned_ref, groups, steps):
    rows_of = SEGS * steps
    row = lax.broadcasted_iota(jnp.int32, (2 * LANES, 2 * LANES), 0) % LANES
    side = lax.broadcasted_iota(jnp.int32, (2 * LANES, 2 * LANES), 1) // LANES
    for g in range(groups):

        def one(i, _):
            turned_ref[pl.ds(pl.multiple_of(i * SEGS, SEGS), SEGS), :] = table_ref[
                pl.ds(g * rows_of + i, SEGS, stride=steps), :
            ]
            return 0

        lax.fori_loop(0, steps, one, 0, unroll=8)
        high, mid, low = exact_parts(turned_ref[0:rows_of, :])
        most = jnp.concatenate([high, mid], axis=1)
        for n in range(0, 2 * N + 1, 2):
            pick = (row == n + side).astype(F32).astype(BF16)
            value = jnp.dot(most, pick, preferred_element_type=F32)
            value = value + jnp.dot(low, pick[:LANES], preferred_element_type=F32)
            first = value[:, :LANES].reshape(steps, SEGS, LANES)
            if n < 2 * N:
                out_ref[g * steps : (g + 1) * steps, n] = first
                out_ref[g * steps : (g + 1) * steps, n + 1] = value[:, LANES:].reshape(
                    steps, SEGS, LANES
                )
            else:
                extra_ref[g * steps : (g + 1) * steps] = first


def totals_kernel(
    groups,
    steps,
    step_ref,
    act_ref,
    dy_ref,
    rate_ref,
    table_ref,
    seg_s_ref,
    seg_h_ref,
    seg_c_ref,
    whole_ref,
    bc_s,
    keep_s,
    act_s,
):
    rows_of = SEGS * steps

    @pl.when(pl.program_id(0) == 0)
    def _():
        spread_columns(table_ref, bc_s, keep_s, act_s, groups, steps)

    act_s[...] = act_ref[...].astype(F32)
    half = N
    zero = jnp.zeros((SEGS, LANES), F32)
    for g in range(groups):
        for lo in range(0, N, half):
            rates = [
                jnp.broadcast_to(rate_ref[lo + n : lo + n + 1, :], (SEGS, LANES))
                for n in range(half)
            ]

            def one(i, carry):
                total, state, reach, back = carry
                state, reach, back = list(state), list(reach), list(back)
                at = pl.ds(g * rows_of + i, SEGS, stride=steps)
                step, act, dy = step_ref[at, :], act_s[at, :], dy_ref[at, :]
                gone = step + keep_s[g * steps + i]
                push = step * act
                for n in range(half):
                    decay = jnp.exp2(gone * rates[n])
                    state[n] = decay * state[n] + push * bc_s[g * steps + i, lo + n]
                    reach[n] = reach[n] * decay
                    back[n] = back[n] + reach[n] * (dy * bc_s[g * steps + i, N + lo + n])
                return (total + gone, tuple(state), tuple(reach), tuple(back))

            total, state, _, back = lax.fori_loop(
                0,
                steps,
                one,
                (zero, (zero,) * half, (jnp.ones((SEGS, LANES), F32),) * half, (zero,) * half),
                unroll=8,
            )
            if lo == 0:
                seg_s_ref[g * SEGS : (g + 1) * SEGS, :] = total
            for n in range(half):
                first = (g * N + lo + n) * SEGS
                seg_h_ref[first : first + SEGS, :] = state[n]
                seg_c_ref[first : first + SEGS, :] = back[n]
    rate = rate_ref[...]
    h = jnp.zeros((N, LANES), F32)
    c = jnp.zeros((N, LANES), F32)
    order = [(g, s) for g in range(groups) for s in range(SEGS)]
    gone = jnp.zeros((1, LANES), F32)
    for g, s in order:
        at = pl.ds(g * N * SEGS + s, N, stride=SEGS)
        spent = seg_s_ref[g * SEGS + s : g * SEGS + s + 1, :]
        h = jnp.exp2(rate * spent) * h + seg_h_ref[at, :]
        gone = gone + spent
    for g, s in order[::-1]:
        at = pl.ds(g * N * SEGS + s, N, stride=SEGS)
        spent = seg_s_ref[g * SEGS + s : g * SEGS + s + 1, :]
        c = jnp.exp2(rate * spent) * c + seg_c_ref[at, :]
    whole_ref[0:N, :] = h
    whole_ref[N : 2 * N, :] = c
    whole_ref[2 * N : 2 * N + SEGS, :] = jnp.broadcast_to(gone, (SEGS, LANES))


def grads_kernel(
    groups,
    steps,
    blocks,
    step_ref,
    act_ref,
    dy_ref,
    rate_ref,
    table_ref,
    seg_s_ref,
    seg_h_ref,
    seg_c_ref,
    h_in_ref,
    c_in_ref,
    y_ref,
    d_step_ref,
    d_act_ref,
    d_rate_ref,
    d_bc_ref,
    bc_s,
    keep_s,
    act_s,
    enter_h,
    enter_c,
    decay_s,
    prior_s,
    sum_b,
    sum_c,
):
    g, j = pl.program_id(0), pl.program_id(1)

    @pl.when(j == 0)
    def _():
        spread_columns(table_ref, bc_s, keep_s, act_s, 1, steps)
        sum_b[...] = jnp.zeros_like(sum_b)
        sum_c[...] = jnp.zeros_like(sum_c)

    rate = rate_ref[...]

    @pl.when(g == 0)
    def _():
        h = h_in_ref[...]
        c = c_in_ref[...]
        order = [(a, s) for a in range(groups) for s in range(SEGS)]
        for a, s in order:
            at = pl.ds(a * N * SEGS + s, N, stride=SEGS)
            spent = seg_s_ref[a * SEGS + s : a * SEGS + s + 1, :]
            enter_h.at[j][at, :] = h
            h = jnp.exp2(rate * spent) * h + seg_h_ref[at, :]
        for a, s in order[::-1]:
            at = pl.ds(a * N * SEGS + s, N, stride=SEGS)
            spent = seg_s_ref[a * SEGS + s : a * SEGS + s + 1, :]
            enter_c.at[j][at, :] = c
            c = jnp.exp2(rate * spent) * c + seg_c_ref[at, :]

    act_s[...] = act_ref[...].astype(F32)
    first = g * N * SEGS

    def rate_row(n):
        return jnp.broadcast_to(rate_ref[n : n + 1, :], (SEGS, LANES))

    def ahead(i, state):
        state = list(state)
        at = pl.ds(i, SEGS, stride=steps)
        step, act, dy = step_ref[at, :], act_s[at, :], dy_ref[at, :]
        gone = step + keep_s[i]
        push = step * act
        y = jnp.zeros((SEGS, LANES), F32)
        for n in range(N):
            decay = jnp.exp2(gone * rate_row(n))
            prior = decay * state[n]
            state[n] = prior + push * bc_s[i, n]
            decay_s[i, n] = decay
            prior_s[i, n] = prior
            y = y + state[n] * bc_s[i, N + n]
            sum_c[i, n] += state[n] * dy
        y_ref[at, :] = y
        return tuple(state)

    def enter(ref, n):
        return ref[j, pl.ds(pl.multiple_of(first + n * SEGS, SEGS), SEGS), :]

    lax.fori_loop(0, steps, ahead, tuple(enter(enter_h, n) for n in range(N)), unroll=8)

    def back(k, carry):
        i = steps - 1 - k
        carried, d_rate = list(carry[0]), list(carry[1])
        at = pl.ds(i, SEGS, stride=steps)
        step, act, dy = step_ref[at, :], act_s[at, :], dy_ref[at, :]
        push = step * act
        along = jnp.zeros((SEGS, LANES), F32)
        d_step = jnp.zeros((SEGS, LANES), F32)
        for n in range(N):
            grad = dy * bc_s[i, N + n] + carried[n]
            along = along + grad * bc_s[i, n]
            log_grad = grad * prior_s[i, n]
            d_step = d_step + log_grad * rate_row(n)
            d_rate[n] = d_rate[n] + log_grad * step
            carried[n] = grad * decay_s[i, n]
            sum_b[i, n] += grad * push
        d_step_ref[at, :] = d_step * LN2 + along * act
        d_act_ref[at, :] = along * step
        return (tuple(carried), tuple(d_rate))

    zero = jnp.zeros((SEGS, LANES), F32)
    _, d_rate = lax.fori_loop(
        0, steps, back, (tuple(enter(enter_c, n) for n in range(N)), (zero,) * N), unroll=8
    )
    for n in range(N):
        d_rate_ref[0, n : n + 1, :] = jnp.sum(d_rate[n], axis=0, keepdims=True)

    @pl.when(j == blocks - 1)
    def _():
        column = lax.broadcasted_iota(jnp.int32, (2 * LANES, LANES), 1)
        total = jnp.zeros((steps * SEGS, LANES), F32)
        for n in range(N):
            for ref, at in ((sum_b, n), (sum_c, N + n)):
                pick = (column == at).astype(F32).astype(BF16)
                value = exact_parts(ref[:, n].reshape(steps * SEGS, LANES))
                total = total + jnp.dot(
                    jnp.concatenate(value[:2], axis=1), pick, preferred_element_type=F32
                )
        act_s[...] = total

        def put(i, _):
            d_bc_ref[pl.ds(i, SEGS, stride=steps), :] = act_s[
                pl.ds(pl.multiple_of(i * SEGS, SEGS), SEGS), :
            ]
            return 0

        lax.fori_loop(0, steps, put, 0, unroll=8)


def scan_totals(step_size, activated, dy_scan, rate2, table, groups, begin, channels):
    length = step_size.shape[0]
    steps = length // (groups * SEGS)
    blocks = channels // LANES
    skip = begin // LANES
    body = lambda *refs: totals_kernel(groups, steps, *refs)
    tall = pl.BlockSpec((length, LANES), lambda j: (0, j + skip))
    rows = groups * N * SEGS
    return pl.pallas_call(
        body,
        grid=(blocks,),
        in_specs=[
            tall,
            tall,
            tall,
            pl.BlockSpec((N, LANES), lambda j: (0, j + skip)),
            pl.BlockSpec((length, LANES), lambda j: (0, 0)),
        ],
        out_specs=[
            pl.BlockSpec((groups * SEGS, LANES), lambda j: (0, j)),
            pl.BlockSpec((rows, LANES), lambda j: (0, j)),
            pl.BlockSpec((rows, LANES), lambda j: (0, j)),
            pl.BlockSpec((2 * N + SEGS, LANES), lambda j: (0, j)),
        ],
        out_shape=[
            jax.ShapeDtypeStruct((groups * SEGS, channels), F32),
            jax.ShapeDtypeStruct((rows, channels), F32),
            jax.ShapeDtypeStruct((rows, channels), F32),
            jax.ShapeDtypeStruct((2 * N + SEGS, channels), F32),
        ],
        scratch_shapes=[
            pltpu.VMEM((groups * steps, 2 * N, SEGS, LANES), F32),
            pltpu.VMEM((groups * steps, SEGS, LANES), F32),
            pltpu.VMEM((length, LANES), F32),
        ],
        compiler_params=pltpu.CompilerParams(
            dimension_semantics=("arbitrary",), vmem_limit_bytes=40 << 20
        ),
        cost_estimate=pl.CostEstimate(
            flops=length * channels * N * 6000,
            bytes_accessed=length * channels * 10,
            transcendentals=length * channels * N,
        ),
        name="scan_totals",
    )(step_size, activated, dy_scan, rate2, table)


def scan_grads(step_size, activated, dy_scan, rate2, table, segs, enter, groups, begin, channels):
    length = step_size.shape[0]
    steps = length // (groups * SEGS)
    blocks = channels // LANES
    skip = begin // LANES
    body = lambda *refs: grads_kernel(groups, steps, blocks, *refs)
    tall = pl.BlockSpec((length // groups, LANES), lambda g, j: (g, j + skip))
    short = pl.BlockSpec((length // groups, LANES), lambda g, j: (g, j))
    rows = groups * N * SEGS
    grid_spec = pl.GridSpec(
        grid=(groups, blocks),
        in_specs=[
            tall,
            tall,
            tall,
            pl.BlockSpec((N, LANES), lambda g, j: (0, j + skip)),
            pl.BlockSpec((length // groups, LANES), lambda g, j: (g, 0)),
            pl.BlockSpec((groups * SEGS, LANES), lambda g, j: (0, j)),
            pl.BlockSpec((rows, LANES), lambda g, j: (0, j)),
            pl.BlockSpec((rows, LANES), lambda g, j: (0, j)),
            pl.BlockSpec((N, LANES), lambda g, j: (0, j)),
            pl.BlockSpec((N, LANES), lambda g, j: (0, j)),
        ],
        out_specs=[
            short,
            short,
            short,
            pl.BlockSpec((1, N, LANES), lambda g, j: (g, 0, j)),
            pl.BlockSpec((length // groups, LANES), lambda g, j: (g, 0)),
        ],
        scratch_shapes=[
            pltpu.VMEM((steps, 2 * N, SEGS, LANES), F32),
            pltpu.VMEM((steps, SEGS, LANES), F32),
            pltpu.VMEM((length // groups, LANES), F32),
            pltpu.VMEM((blocks, rows, LANES), F32),
            pltpu.VMEM((blocks, rows, LANES), F32),
            pltpu.VMEM((steps, N, SEGS, LANES), F32),
            pltpu.VMEM((steps, N, SEGS, LANES), F32),
            pltpu.VMEM((steps, N, SEGS, LANES), F32),
            pltpu.VMEM((steps, N, SEGS, LANES), F32),
        ],
    )
    return pl.pallas_call(
        body,
        grid_spec=grid_spec,
        out_shape=[
            jax.ShapeDtypeStruct((length, channels), F32),
            jax.ShapeDtypeStruct((length, channels), F32),
            jax.ShapeDtypeStruct((length, channels), F32),
            jax.ShapeDtypeStruct((groups, N, channels), F32),
            jax.ShapeDtypeStruct((length, LANES), F32),
        ],
        compiler_params=pltpu.CompilerParams(
            dimension_semantics=("arbitrary", "arbitrary"), vmem_limit_bytes=48 << 20
        ),
        cost_estimate=pl.CostEstimate(
            flops=length * channels * N * 12000,
            bytes_accessed=length * channels * 22,
            transcendentals=length * channels * N,
        ),
        name="scan_grads",
    )(step_size, activated, dy_scan, rate2, table, *segs, *enter)


MESH = pl.DeviceIdType.MESH
CHUNK = 256


def finish_kernel(
    parts,
    gated_hbm,
    normed_hbm,
    d_gate_hbm,
    d_inner_hbm,
    w_inx_hbm,
    w_inz_hbm,
    x_hbm,
    dy_hbm,
    rms_ref,
    gain_ref,
    small_send_ref,
    small_keep_ref,
    sums_hbm,
    small_ref,
    grad_hbm,
    left,
    right,
    w_x,
    w_z,
    x_cols,
    y_out,
    y_in,
    a_in,
    b_in,
    line,
    first,
    total,
    core_out,
    core_in,
    kept,
    x_out,
    x_in,
    rows_x,
    rows_dy,
    final,
    gain_sum,
    gain_core,
    gain_x,
    gain_out,
    s_out,
    s_in,
    s_a,
    s_b,
    s_line,
    load_sem,
    w_sem,
    y_sem,
    a_sem,
    b_sem,
    c_sem,
    out_sem,
    tp_sem,
    gain_sem,
    final_sem,
    small_sem,
):
    rows, width = x_hbm.shape
    half = width // 2
    dp, z, tp = lax.axis_index("dp"), lax.axis_index("ctx"), lax.axis_index("tp")
    core, x_bit = tp % 2, tp // 2
    near, across, diagonal = tp + 1 - 2 * core, (tp + 2) % 4, 3 - tp
    ends = (z == 0) | (z == 3)
    middle = (z == 1) | (z == 2)
    inward, twin, outward = z // 2 + 1, 3 - z, (z // 2) * 3

    loads = [
        pltpu.make_async_copy(gated_hbm, left.at[0], load_sem.at[0]),
        pltpu.make_async_copy(dy_hbm.at[:, pl.ds(half, half)], right.at[1], load_sem.at[1]),
        pltpu.make_async_copy(dy_hbm.at[:, pl.ds(0, half)], right.at[0], load_sem.at[2]),
        pltpu.make_async_copy(normed_hbm.at[pl.ds(0, half), :], left.at[1], load_sem.at[3]),
        pltpu.make_async_copy(normed_hbm.at[pl.ds(half, half), :], left.at[2], load_sem.at[4]),
        pltpu.make_async_copy(d_gate_hbm, right.at[2], load_sem.at[5]),
        pltpu.make_async_copy(d_inner_hbm, right.at[3], load_sem.at[6]),
    ]
    quarter = rows // 4
    own_row = pl.multiple_of(core * (rows // 2) + x_bit * quarter, quarter)
    loads.append(pltpu.make_async_copy(x_hbm.at[pl.ds(own_row, quarter), :], rows_x, load_sem.at[7]))
    loads.append(pltpu.make_async_copy(dy_hbm.at[pl.ds(own_row, quarter), :], rows_dy, load_sem.at[8]))
    for load in loads:
        load.start()

    barrier = pltpu.get_barrier_semaphore()
    for peer in ({"tp": near}, {"tp": across}, {"tp": diagonal}, {"dp": 1 - dp}):
        pl.semaphore_signal(barrier, inc=1, device_id=peer, device_id_type=MESH)

    @pl.when(ends)
    def _():
        pl.semaphore_signal(barrier, inc=1, device_id={"ctx": inward}, device_id_type=MESH)
        pl.semaphore_wait(barrier, 5)

    @pl.when(middle)
    def _():
        pl.semaphore_signal(barrier, inc=1, device_id={"ctx": twin}, device_id_type=MESH)
        pl.semaphore_signal(barrier, inc=1, device_id={"ctx": outward}, device_id_type=MESH)
        pl.semaphore_wait(barrier, 6)

    def remote(source, target, sems, at, peer):
        return pltpu.make_async_remote_copy(
            src_ref=source,
            dst_ref=target,
            send_sem=sems.at[0, at],
            recv_sem=sems.at[1, at],
            device_id=peer,
            device_id_type=MESH,
        )

    per_weight = parts // 3

    def chunk(k):
        return k // per_weight, pl.multiple_of(k % per_weight * CHUNK, CHUNK)

    def product(slot_l, slot_r, column):
        return jnp.dot(
            left[slot_l], right[slot_r, :, pl.ds(column, CHUNK)], preferred_element_type=F32
        )

    def y_copy(k):
        return remote(y_out.at[k % 4], y_in.at[k % 6], y_sem, k, {"dp": 1 - dp})

    def a_copy(k):
        return remote(line.at[k % 4], a_in.at[k], a_sem, k, {"ctx": inward})

    def b_copy(k):
        return remote(line.at[k % 4], b_in.at[k % 4], b_sem, k, {"ctx": twin})

    def c_copy(k):
        w, column = chunk(k)
        return remote(
            total.at[k % 4], sums_hbm.at[w, :, pl.ds(column, CHUNK)], c_sem, k, {"ctx": outward}
        )

    def own_copy(k):
        w, column = chunk(k)
        return pltpu.make_async_copy(
            total.at[k % 4], sums_hbm.at[w, :, pl.ds(column, CHUNK)], out_sem.at[k]
        )

    def send_y(k):
        w, column = chunk(k)
        up = (w + 1) // 2

        @pl.when(k >= 4)
        def _():
            y_copy(k - 4).wait_send()

        y_out[k % 4] = product(2 * up, w + 1, column).astype(BF16)
        y_copy(k).start()

    def take_y(k):
        w, column = chunk(k)
        up = (w + 1) // 2
        value = product(up, w + up, column)
        y_copy(k).wait_recv()
        value = value + y_in[k % 6].astype(F32)

        @pl.when(ends)
        def _():
            @pl.when(k >= 4)
            def _():
                a_copy(k - 4).wait_send()

            line[k % 4] = value.astype(BF16)
            a_copy(k).start()

        @pl.when(middle)
        def _():
            first[k % 2] = value

    def take_a(k):
        @pl.when(middle)
        def _():
            @pl.when(k >= 4)
            def _():
                b_copy(k - 4).wait_send()

            a_copy(k).wait_recv()
            line[k % 4] = (first[k % 2] + a_in[k].astype(F32)).astype(BF16)
            b_copy(k).start()

    def take_b(k):
        @pl.when(middle)
        def _():
            @pl.when(k >= 4)
            def _():
                c_copy(k - 4).wait_send()
                own_copy(k - 4).wait()

            b_copy(k).wait_recv()
            total[k % 4] = (line[k % 4].astype(F32) + b_in[k % 4].astype(F32)).astype(BF16)
            c_copy(k).start()
            own_copy(k).start()

    def tick(k, _):
        @pl.when(k + 2 < parts)
        def _():
            send_y(k + 2)

        @pl.when((k >= 1) & (k < parts + 1))
        def _():
            take_a(k - 1)

        @pl.when(k < parts)
        def _():
            take_y(k)

        @pl.when((k >= 2) & (k < parts + 2))
        def _():
            take_b(k - 2)

        return 0

    def ticks(begin, end):
        lax.fori_loop(begin, end, tick, 0)

    for load in loads[:2]:
        load.wait()
    send_y(0)
    send_y(1)
    for load in loads[2:7]:
        load.wait()

    block = w_x.shape[0]
    send_row = pl.multiple_of((1 - core) * (rows // 2), rows // 2)
    keep_row = pl.multiple_of(core * (rows // 2), rows // 2)

    def columns(d, _):
        at = pl.multiple_of(d * block, block)
        copies = [
            pltpu.make_async_copy(w_inx_hbm.at[pl.ds(at, block), :], w_x, w_sem.at[0]),
            pltpu.make_async_copy(w_inz_hbm.at[pl.ds(at, block), :], w_z, w_sem.at[1]),
            pltpu.make_async_copy(x_hbm.at[:, pl.ds(at, block)], x_cols, w_sem.at[2]),
        ]
        for copy in copies:
            copy.start()
        for copy in copies:
            copy.wait()
        sums = jnp.zeros((SEGS, block), F32)
        for row, keep in ((send_row, False), (keep_row, True)):
            span = pl.ds(row, rows // 2)
            value = contract_last(right[3, span, :], w_x[...])
            value = value + contract_last(right[2, span, :], w_z[...])
            hat = x_cols[span, :].astype(F32) * rms_ref[span, :]
            sums = sums + jnp.sum((value * hat).reshape(rows // 2 // SEGS, SEGS, block), axis=0)
            if keep:
                kept[:, pl.ds(at, block)] = value
            else:
                core_out[:, pl.ds(at, block)] = value.astype(BF16)
        gain_sum[:, pl.ds(at, block)] = sums
        return 0

    lax.fori_loop(0, width // block, columns, 0)
    core_copy = remote(core_out, core_in, tp_sem, 0, {"tp": near})
    core_copy.start()
    gain_copy = remote(gain_sum, gain_core, gain_sem, 0, {"tp": near})
    gain_copy.start()

    ticks(0, 1)

    core_copy.wait_recv()
    give = pl.multiple_of((1 - x_bit) * quarter, quarter)
    have = pl.multiple_of(x_bit * quarter, quarter)
    x_out[...] = (
        kept[pl.ds(give, quarter), :] + core_in[pl.ds(give, quarter), :].astype(F32)
    ).astype(BF16)
    x_copy = remote(x_out, x_in, tp_sem, 1, {"tp": across})
    x_copy.start()
    gain_copy.wait_recv()
    gain_out[...] = gain_sum[...] + gain_core[...]
    gain_across = remote(gain_out, gain_x, gain_sem, 1, {"tp": across})
    gain_across.start()

    ticks(1, 2)

    small_rows = small_send_ref.shape[0]
    gain_across.wait_recv()
    both = gain_out[...] + gain_x[...]
    quarter_w = half // 2
    s_out[0:small_rows, :] = small_send_ref[...].astype(BF16)
    s_out[small_rows:, :] = jnp.concatenate(
        [both[:, half : half + quarter_w], both[:, half + quarter_w :]], axis=0
    ).astype(BF16)
    small_y = remote(s_out, s_in, small_sem, 0, {"dp": 1 - dp})
    small_y.start()

    ticks(2, 4)

    x_copy.wait_recv()
    r_own = rms_ref[pl.ds(own_row, quarter), :]
    d_normed = (
        kept[pl.ds(have, quarter), :]
        + core_in[pl.ds(have, quarter), :].astype(F32)
        + x_in[...].astype(F32)
    )
    hat = rows_x_wait(loads, rows_x) * r_own
    d_hat = d_normed * gain_ref[...]
    mean = jnp.sum(d_hat * hat, axis=1, keepdims=True) * (1.0 / width)
    final[...] = (rows_dy[...].astype(F32) + r_own * (d_hat - hat * mean)).astype(BF16)
    gathers = []
    for side in range(2):
        place = pl.multiple_of((dp + side - 2 * dp * side) * half, half)
        spot = grad_hbm.at[pl.ds(own_row, quarter), pl.ds(place, half)]
        source = final.at[:, pl.ds(side * half, half)]
        for p, peer in enumerate((near, across, diagonal)):
            gathers.append(remote(source, spot, final_sem, 2 * p + side, {"tp": peer}))
        local = pltpu.make_async_copy(source, spot, load_sem.at[9 + side])
        local.start()
        loads.append(local)
    for copy in gathers:
        copy.start()

    small_y.wait_recv()
    s_keep = jnp.concatenate(
        [
            small_keep_ref[...],
            both[:, :quarter_w],
            both[:, quarter_w:half],
        ],
        axis=0,
    ) + s_in[...].astype(F32)
    small_a = remote(s_line, s_a, small_sem, 1, {"ctx": inward})
    small_b = remote(s_line, s_b, small_sem, 2, {"ctx": twin})
    small_c = remote(small_ref, small_ref, small_sem, 3, {"ctx": outward})

    @pl.when(ends)
    def _():
        s_line[...] = s_keep.astype(BF16)
        small_a.start()

    @pl.when(middle)
    def _():
        small_a.wait_recv()
        s_line[...] = (s_keep + s_a[...].astype(F32)).astype(BF16)
        small_b.start()

    ticks(4, 6)

    @pl.when(middle)
    def _():
        small_b.wait_recv()
        small_ref[...] = (s_line[...].astype(F32) + s_b[...].astype(F32)).astype(BF16)
        small_c.start()

    ticks(6, parts + 2)

    for k in range(parts - 4, parts):
        y_copy(k).wait_send()

    @pl.when(ends)
    def _():
        for k in range(parts - 4, parts):
            a_copy(k).wait_send()
        for k in range(parts):
            c_copy(k).wait_recv()
        small_a.wait_send()
        small_c.wait_recv()

    @pl.when(middle)
    def _():
        for k in range(parts - 4, parts):
            b_copy(k).wait_send()
            c_copy(k).wait_send()
            own_copy(k).wait()
        small_b.wait_send()
        small_c.wait_send()

    core_copy.wait_send()
    x_copy.wait_send()
    gain_copy.wait_send()
    gain_across.wait_send()
    small_y.wait_send()
    for copy in gathers:
        copy.wait()
    for local in loads[9:]:
        local.wait()


def rows_x_wait(loads, ref):
    loads[7].wait()
    loads[8].wait()
    return ref[...].astype(F32)


def finish(gated, normed, d_gate, d_inner, w_inx, w_inz, x_all, dy_all, rms, gain, small_send, small_keep):
    rows, width = x_all.shape
    channels = w_inx.shape[1]
    parts = 3 * (channels // CHUNK)
    half = width // 2
    small = small_send.shape[0] + 2 * SEGS
    block = 512
    hbm = pl.BlockSpec(memory_space=pl.ANY)
    vmem = pl.BlockSpec(memory_space=pltpu.VMEM)
    dma = pltpu.SemaphoreType.DMA
    piece = (half, CHUNK)
    quarter = rows // 4
    return pl.pallas_call(
        lambda *refs: finish_kernel(parts, *refs),
        in_specs=[hbm] * 8 + [vmem] * 4,
        out_specs=[hbm, vmem, hbm],
        out_shape=[
            jax.ShapeDtypeStruct((3, half, channels), BF16),
            jax.ShapeDtypeStruct((small, small_send.shape[1]), BF16),
            jax.ShapeDtypeStruct((rows, width), BF16),
        ],
        scratch_shapes=[
            pltpu.VMEM((3, half, rows), BF16),
            pltpu.VMEM((4, rows, channels), BF16),
            pltpu.VMEM((block, channels), BF16),
            pltpu.VMEM((block, channels), BF16),
            pltpu.VMEM((rows, block), BF16),
            pltpu.VMEM((4,) + piece, BF16),
            pltpu.VMEM((6,) + piece, BF16),
            pltpu.VMEM((parts,) + piece, BF16),
            pltpu.VMEM((4,) + piece, BF16),
            pltpu.VMEM((4,) + piece, BF16),
            pltpu.VMEM((2,) + piece, F32),
            pltpu.VMEM((4,) + piece, BF16),
            pltpu.VMEM((rows // 2, width), BF16),
            pltpu.VMEM((rows // 2, width), BF16),
            pltpu.VMEM((rows // 2, width), F32),
            pltpu.VMEM((quarter, width), BF16),
            pltpu.VMEM((quarter, width), BF16),
            pltpu.VMEM((quarter, width), BF16),
            pltpu.VMEM((quarter, width), BF16),
            pltpu.VMEM((quarter, width), BF16),
            pltpu.VMEM((SEGS, width), F32),
            pltpu.VMEM((SEGS, width), F32),
            pltpu.VMEM((SEGS, width), F32),
            pltpu.VMEM((SEGS, width), F32),
            pltpu.VMEM((small, small_send.shape[1]), BF16),
            pltpu.VMEM((small, small_send.shape[1]), BF16),
            pltpu.VMEM((small, small_send.shape[1]), BF16),
            pltpu.VMEM((small, small_send.shape[1]), BF16),
            pltpu.VMEM((small, small_send.shape[1]), BF16),
            dma((11,)),
            dma((3,)),
            dma((2, parts)),
            dma((2, parts)),
            dma((2, parts)),
            dma((2, parts)),
            dma((parts,)),
            dma((2, 2)),
            dma((2, 2)),
            dma((2, 6)),
            dma((2, 4)),
        ],
        compiler_params=pltpu.CompilerParams(
            collective_id=0, has_side_effects=True, vmem_limit_bytes=63000 << 10
        ),
        cost_estimate=pl.CostEstimate(
            flops=150_000_000_000, bytes_accessed=60_000_000, transcendentals=0
        ),
        name="finish",
    )(gated, normed, d_gate, d_inner, w_inx, w_inz, x_all, dy_all, rms, gain, small_send, small_keep)


def swap_pairs(value, axis, distance):
    count = lax.axis_size(axis)
    return lax.ppermute(value, axis, [(i, i ^ distance) for i in range(count)])


def ordered(mine, other, bit, axis=0):
    return jnp.where(
        bit == 0,
        jnp.concatenate([mine, other], axis=axis),
        jnp.concatenate([other, mine], axis=axis),
    )


def half_of(value, index, axis=0):
    size = value.shape[axis] // 2
    return lax.dynamic_slice_in_dim(value, index * size, size, axis)


def tp_sum(value):
    distance = 1
    while distance < lax.axis_size("tp"):
        value = value + swap_pairs(value, "tp", distance)
        distance *= 2
    return value


def tp_scatter(value):
    index, distance = lax.axis_index("tp"), 1
    while distance < lax.axis_size("tp"):
        mine = (index // distance) % 2
        got = swap_pairs(half_of(value, 1 - mine).astype(BF16), "tp", distance)
        value = half_of(value, mine).astype(F32) + got.astype(F32)
        distance *= 2
    return value


def tp_rows():
    index, distance, at, size = lax.axis_index("tp"), 1, 0, lax.axis_size("tp")
    while distance < lax.axis_size("tp"):
        size //= 2
        at = at + (index // distance) % 2 * size
        distance *= 2
    return at


def per_device(
    hidden_in,
    seq_lengths,
    pack_order,
    norm_gain,
    in_x_weight,
    in_z_weight,
    conv_weight,
    conv_bias,
    x_weight,
    dt_weight,
    dt_bias,
    a_log,
    skip_weight,
    out_weight,
    out_grad,
):
    length, width = hidden_in.shape
    channels = in_x_weight.shape[1]
    tp_count, dp_count, ctx_count = (lax.axis_size(a) for a in ("tp", "dp", "ctx"))
    dp_index, ctx_index, tp_index = (lax.axis_index(a) for a in ("dp", "ctx", "tp"))
    paired = dp_count == 2
    half = width // dp_count
    groups, splits = 2, 1
    fused = paired and ctx_count == 4 and tp_count == 4 and half == channels == length

    def turned(value, axis):
        if not paired:
            return value
        return jnp.concatenate(
            [half_of(value, dp_index, axis), half_of(value, 1 - dp_index, axis)], axis=axis
        )

    def joined(value, axis):
        if not paired:
            return lax.all_gather(value, "dp", axis=axis, tiled=True)
        other = swap_pairs(value, "dp", 1)
        return jnp.where(
            dp_index == 0,
            jnp.concatenate([value, other], axis=axis),
            jnp.concatenate([other, value], axis=axis),
        )

    def weight(own, axis, after):
        if not paired:
            return lax.all_gather(own, "dp", axis=axis, tiled=True), None
        bit = ctx_index % 2
        piece = half_of(own, bit)
        if after is not None:
            piece, _ = lax.optimization_barrier((piece, after))
        near = swap_pairs(piece, "dp", 1)
        far = swap_pairs(near, "ctx", 1)
        return jnp.concatenate([own, ordered(near, far, bit)], axis=axis), near

    small = jnp.concatenate(
        [conv_weight, conv_bias[None], dt_bias[None], skip_weight[None], a_log.T], axis=0
    )
    small = joined(small, 1).astype(F32)
    gain_full = joined(norm_gain, 0).astype(F32)
    w_proj = joined(x_weight, 0)
    w_step = joined(dt_weight, 0)
    w_inx, sent = weight(in_x_weight, 0, small)
    w_inz, sent = weight(in_z_weight, 0, sent)
    w_out, sent = weight(out_weight, 1, sent)
    gain_full = turned(gain_full, 0)
    taps_full = small[:K]
    conv_shift, step_bias, skip_full = small[K], small[K + 1], small[K + 2]
    decay_rate = -jnp.exp(small[K + 3 :])

    starts = piece_starts(seq_lengths[0], pack_order[0])
    positions = ctx_index * length + jnp.arange(length, dtype=jnp.int32)

    def piece(at):
        return jnp.sum((at[:, None] >= starts[None, :]).astype(jnp.int32), axis=1)

    piece_now = piece(positions)
    masks = [(piece(positions - back) == piece_now).astype(F32) for back in (3, 2, 1)]
    blocked = (1.0 - masks[2]) * FAR

    rows_all = turned(hidden_in, 1)
    grad_all = turned(out_grad, 1)
    rows_in = rows_all.astype(F32)
    inv_rms = lax.rsqrt(jnp.mean(rows_in * rows_in, axis=1, keepdims=True) + EPSILON)
    normed = (rows_in * inv_rms * gain_full).astype(BF16)
    inner_x = jnp.dot(normed, w_inx, preferred_element_type=F32).astype(BF16)
    halo = shifted(inner_x[length - (K - 1) :], "ctx", 1)
    extended = jnp.concatenate([halo, inner_x], axis=0).astype(F32)
    conv_pre = conv_shift[None, :] + taps_full[K - 1] * extended[K - 1 :]
    for tap in range(K - 1):
        conv_pre = conv_pre + taps_full[tap] * extended[tap : tap + length] * masks[tap][:, None]
    activated = jax.nn.silu(conv_pre).astype(BF16)
    projected = tp_sum(jnp.dot(activated, w_proj, preferred_element_type=F32))
    gate_z = jnp.dot(normed, w_inz, preferred_element_type=F32)
    d_gated = contract_last(grad_all, w_out)
    gate_sig = jax.nn.sigmoid(gate_z)
    dy_scan = d_gated * gate_z * gate_sig

    step_low = projected[:, :R].astype(BF16)
    step_pre = jnp.dot(step_low, w_step, preferred_element_type=F32) + step_bias
    step_size = jax.nn.softplus(step_pre)
    table = jnp.concatenate(
        [
            projected[:, R:],
            blocked[:, None],
            jnp.zeros((length, LANES - 2 * N - 1), F32),
        ],
        axis=1,
    )
    rate2 = decay_rate * LOG2E
    share = channels // splits

    def entering(whole, rate):
        state, back, spent = whole[:N], whole[N : 2 * N], whole[2 * N : 2 * N + 1]
        h_in = jnp.zeros_like(state)
        c_in = jnp.zeros_like(back)
        below = jnp.zeros_like(spent)
        above = jnp.zeros_like(spent)
        distance = 1
        while distance < ctx_count:
            got = swap_pairs(jnp.concatenate([state, back, jnp.broadcast_to(spent, (8,) + spent.shape[1:])], axis=0), "ctx", distance)
            o_state, o_back, o_spent = got[:N], got[N : 2 * N], got[2 * N : 2 * N + 1]
            upper = (ctx_index // distance) % 2 == 1
            h_in = jnp.where(upper, jnp.exp2(rate * below) * o_state + h_in, h_in)
            c_in = jnp.where(upper, c_in, jnp.exp2(rate * above) * o_back + c_in)
            below = jnp.where(upper, below + o_spent, below)
            above = jnp.where(upper, above, above + o_spent)
            mine, other = jnp.exp2(rate * spent), jnp.exp2(rate * o_spent)
            state, back = (
                jnp.where(upper, mine * o_state + state, other * state + o_state),
                jnp.where(upper, o_back + other * back, back + mine * o_back),
            )
            spent = spent + o_spent
            distance *= 2
        return h_in, c_in

    totals = [
        scan_totals(step_size, activated, dy_scan, rate2, table, groups, k * share, share)
        for k in range(splits)
    ]
    drive_in = activated.astype(F32)

    def input_sum(cotangent):
        value = contract_first(normed, cotangent)
        if paired:
            value = turned(value, 0)
        value = lax.psum_scatter(value.astype(BF16), "dp", scatter_dimension=0, tiled=True)
        return lax.psum(value, "ctx").astype(F32)

    def output_sum(gated):
        value = contract_first(gated, grad_all)
        if paired:
            value = turned(value, 1)
        value = lax.psum_scatter(value.astype(BF16), "dp", scatter_dimension=1, tiled=True)
        return lax.psum(value, "ctx").astype(F32)

    branch, d_low = None, None
    gates, pres, acts, rates_d, gateds = [], [], [], [], []
    for k in range(splits):
        cut = slice(k * share, (k + 1) * share)
        seg_s, seg_h, seg_c, whole = totals[k]
        scan, d_step, d_act, d_rate, d_bc = scan_grads(
            step_size,
            activated,
            dy_scan,
            rate2,
            table,
            (seg_s, seg_h, seg_c),
            entering(whole, rate2[:, cut]),
            groups,
            k * share,
            share,
        )
        sig, z = gate_sig[:, cut], gate_z[:, cut]
        scan_out = scan + skip_full[cut] * drive_in[:, cut]
        gated = (scan_out * z * sig).astype(BF16)
        d_gate = (d_gated[:, cut] * scan_out * sig * (1.0 + z * (1.0 - sig))).astype(BF16)
        d_pre = (d_step * jax.nn.sigmoid(step_pre[:, cut])).astype(BF16)
        low = jnp.concatenate([contract_last(d_pre, w_step[:, cut]), d_bc[:, : 2 * N]], axis=1)
        product = jnp.dot(gated, w_out[cut], preferred_element_type=F32)
        gateds.append(gated)
        branch = product if branch is None else branch + product
        d_low = low if d_low is None else d_low + low
        gates.append(d_gate)
        pres.append(d_pre)
        acts.append(d_act)
        rates_d.append(d_rate)
    d_gate, d_pre, d_act, d_rate, gated_out = (
        jnp.concatenate(v, axis=-1) for v in (gates, pres, acts, rates_d, gateds)
    )
    d_proj = tp_sum(d_low).astype(BF16)

    quarter = length // tp_count
    own_row = tp_rows() * quarter
    own_in = lax.dynamic_slice_in_dim(rows_all, own_row, quarter, 0).astype(F32)
    own_grad = lax.dynamic_slice_in_dim(grad_all, own_row, quarter, 0).astype(F32)
    own_rms = lax.rsqrt(jnp.mean(own_in * own_in, axis=1, keepdims=True) + EPSILON)
    own_hat = own_in * own_rms

    def whole_rows(value):
        distance = tp_count // 2
        while distance >= 1:
            value = ordered(value, swap_pairs(value, "tp", distance), (tp_index // distance) % 2)
            distance //= 2
        if not paired:
            return value
        return ordered(value[:, :half], value[:, half:], dp_index, axis=1)

    out_natural = whole_rows((own_in + tp_scatter(branch)).astype(BF16))

    g_skip = jnp.sum(dy_scan * drive_in, axis=0)
    g_bias = jnp.sum(d_pre.astype(F32), axis=0)
    g_step = contract_first(step_low, d_pre)
    g_log = jnp.sum(d_rate, axis=0) * decay_rate

    g_proj = contract_first(d_proj, activated)
    d_total = d_act + dy_scan * skip_full + contract_last(d_proj, w_proj)
    conv_sig = jax.nn.sigmoid(conv_pre)
    d_conv = d_total * conv_sig * (1.0 + conv_pre * (1.0 - conv_sig))
    g_shift = jnp.sum(d_conv, axis=0)
    g_taps = jnp.stack(
        [
            jnp.sum(d_conv * masks[tap][:, None] * extended[tap : tap + length], axis=0)
            for tap in range(K - 1)
        ]
        + [jnp.sum(d_conv * extended[K - 1 :], axis=0)],
        axis=0,
    )
    d_extended = jnp.pad(d_conv * taps_full[K - 1], ((K - 1, 0), (0, 0)))
    for tap in range(K - 1):
        d_extended = d_extended + jnp.pad(
            d_conv * masks[tap][:, None] * taps_full[tap], ((tap, K - 1 - tap), (0, 0))
        )
    returned = shifted(d_extended[: K - 1], "ctx", -1)
    d_inner = (
        d_extended[K - 1 :] + jnp.pad(returned, ((length - (K - 1), 0), (0, 0)))
    ).astype(BF16)
    packed = jnp.concatenate(
        [g_taps, g_shift[None], g_bias[None], g_skip[None], g_log, g_proj], axis=0
    )
    if fused:

        def side(index):
            piece = half_of(packed, index, 1)
            steps = half_of(g_step, index)
            cut = piece.shape[1]
            rows = [piece, steps[:, :cut], steps[:, cut:]]
            count = sum(r.shape[0] for r in rows)
            rows.append(jnp.zeros((-count % 16, cut), F32))
            return jnp.concatenate(rows, axis=0)

        small_send, small_keep = side(1 - dp_index), side(dp_index)
        sums, small_sum, grad_natural = finish(
            gated_out.T,
            normed.T,
            d_gate,
            d_inner,
            w_inx,
            w_inz,
            rows_all,
            grad_all,
            inv_rms,
            gain_full[None],
            small_send,
            small_keep,
        )
        sums = sums.astype(F32)
        small_sum = small_sum.astype(F32)
        count, high, cut = packed.shape[0], g_step.shape[0] // 2, packed.shape[1] // 2
        at = small_send.shape[0]
        g_out, g_inz, g_inx = sums[0], sums[1], sums[2]
        g_gain = jnp.concatenate(
            [
                jnp.sum(small_sum[at : at + SEGS], axis=0),
                jnp.sum(small_sum[at + SEGS :], axis=0),
            ]
        )
        packed = small_sum[:count]
        g_step = jnp.concatenate(
            [small_sum[count : count + high], small_sum[count + high : count + 2 * high]], axis=1
        )
    else:
        g_inx, g_inz, g_out = input_sum(d_inner), input_sum(d_gate), output_sum(gated_out)
        d_normed = tp_scatter(contract_last(d_inner, w_inx) + contract_last(d_gate, w_inz))
        g_gain = jnp.sum(d_normed * own_hat, axis=0)
        d_hat = d_normed * gain_full
        d_rows = own_grad + own_rms * (
            d_hat - own_hat * jnp.mean(d_hat * own_hat, axis=1, keepdims=True)
        )
        grad_natural = whole_rows(d_rows.astype(BF16))
        g_gain = turned(lax.psum(g_gain, ("ctx", "tp")), 0)
        g_gain = lax.psum_scatter(g_gain, "dp", scatter_dimension=0, tiled=True)
        packed = lax.psum(lax.psum_scatter(packed, "dp", scatter_dimension=1, tiled=True), "ctx")
        g_step = lax.psum(lax.psum_scatter(g_step, "dp", scatter_dimension=0, tiled=True), "ctx")
    return (
        out_natural,
        grad_natural,
        g_gain,
        g_inx,
        g_inz,
        packed[:K],
        packed[K],
        packed[K + 3 + N :].T,
        g_step,
        packed[K + 1],
        packed[K + 3 : K + 3 + N].T,
        packed[K + 2],
        g_out,
    )


def solution(mesh):
    in_specs = (
        P(("dp", "ctx"), None),
        P("dp", None),
        P("dp", None),
        P("dp"),
        P("dp", "tp"),
        P("dp", "tp"),
        P(None, ("tp", "dp")),
        P(("tp", "dp")),
        P(("tp", "dp"), None),
        P("dp", "tp"),
        P(("tp", "dp")),
        P(("tp", "dp"), None),
        P(("tp", "dp")),
        P("tp", "dp"),
        P(("dp", "ctx"), None),
    )
    out_specs = (
        P(("dp", "ctx"), None),
        P(("dp", "ctx"), None),
        P("dp"),
        P("dp", "tp"),
        P("dp", "tp"),
        P(None, ("tp", "dp")),
        P(("tp", "dp")),
        P(("tp", "dp"), None),
        P("dp", "tp"),
        P(("tp", "dp")),
        P(("tp", "dp"), None),
        P(("tp", "dp")),
        P("tp", "dp"),
    )
    return jax.shard_map(
        per_device, mesh=mesh, in_specs=in_specs, out_specs=out_specs, check_vma=False
    )
```

time: 4220 us -> 700 us (0.17)
  waiting for transfers between devices: 1970 us -> 98.1 us
  other arithmetic: 784 us -> 88.1 us
  local copies, waits for them, and re-layouts: 738 us -> 62.7 us
  Pallas kernels: 0 us -> 345 us
  matrix products: 382 us -> 68.3 us
  blocking collectives: 295 us -> 0 us
    all_gather x10 -> x0, waiting for transfers between devices: 1320 us -> none  [the longest x1 288 us: per_device(): lax.all_gather(jnp.concatenate(grad_blocks, axis=0), 'ctx', axis=0, tiled...]
    unnamed x60 -> x0, other arithmetic: 354 us -> none
    pallas_call x0 -> x3, Pallas kernels: none -> 345 us  [the longest x1 216 us: finish(): pl.pallas_call(lambda *refs: finish_kernel(parts, *refs), in_specs=[hbm]...]
    reduce_scatter x6 -> x0, waiting for transfers between devices: 330 us -> none  [the longest x1 152 us: per_device(): lax.psum_scatter(totals[1], ('dp', 'ctx'), scatter_dimension=0, tiled=True)]
    dot_general x18 -> x5, matrix products: 306 us -> 37.6 us  [the longest x1 21 us: per_device(): gate_z = jnp.dot(normed, w_inz, preferred_element_type=F32)]
    psum x3 -> x0, waiting for transfers between devices: 262 us -> none  [the longest x1 156 us: per_device(): lax.psum(contract_last(d_inner, w_inx) + contract_last(d_gate, w_inz), 'tp')]
    pad x64 -> x0, local copies, waits for them, and re-layouts: 259 us -> none  [the longest x32 133 us: forward_states(): lax.associative_scan(affine_join, (growth[:, -1], local_states[:, -1]), a...]
    all_gather x24 -> x0, blocking collectives: 240 us -> none  [the longest x8 111 us: carried_in(): everything = jax.tree.map(lambda part: lax.all_gather(part, axis), value)]
  transfers between devices with their start and end apart: 24 -> 22, of which waited for: 19 -> 11; matrix products, arithmetic and copies ran while one was open for 10% -> 24% of each run, Pallas kernels for 0% -> 31%
where the time goes in v1:
time: 700 us; the launch traced here: 694 us
  Pallas kernels  345 us (49%)
  waiting for transfers between devices  98.1 us (14%)
  other arithmetic  88.1 us (13%)
  matrix products  68.3 us (10%)
  local copies, waits for them, and re-layouts  62.7 us (9%)
  starting transfers between devices  28.6 us (4%)
    pallas_call x1, Pallas kernels, finish(): pl.pallas_call(lambda *refs: finish_kernel(parts, *refs), in_specs=[hbm]...  216 us
    pallas_call x1, Pallas kernels, scan_grads(): pl.pallas_call(body, grid_spec=grid_spec, out_shape=[jax.ShapeDtypeStruct...  89.3 us
    ppermute x20, waiting for transfers between devices, swap_pairs(): return lax.ppermute(value, axis, [(i, i ^ distance) for i in range(count)])  80 us
    pallas_call x1, Pallas kernels, scan_totals(): pl.pallas_call(body, grid=(blocks,), in_specs=[tall, tall, tall, pl.Block...  38.9 us
    dot_general x3, matrix products, contract_last(): lax.dot_general(left, right, (((1,), (1,)), ((), ())), preferred_element_...  27.9 us
    ppermute x20, starting transfers between devices, swap_pairs(): return lax.ppermute(value, axis, [(i, i ^ distance) for i in range(count)])  24.4 us
    dot_general x1, matrix products, per_device(): gate_z = jnp.dot(normed, w_inz, preferred_element_type=F32)  21 us
    select_n x6, other arithmetic, ordered(): jnp.where(bit == 0, jnp.concatenate([mine, other], axis=axis), jnp.concat...  20.7 us
  transfers between devices with their start and end apart: 22, of which 11 were waited for; matrix products, arithmetic and copies ran while one was open for 24% of the time, Pallas kernels for 31%

profile of v1, /device:TPU:0, one launch (start us, length us, event | category | flops | bytes accessed | tf_op | source)
XLA Modules:
  0.0 693.5 jit_solution(9519631953886758963)
XLA Ops:
  4.3 3.0 collective-permute-start
  19.9 16.7 %collective-permute-done.2 = bf16[512,1024]{1,0:T(8,128)(2,1)S(1)} collective-permute-done((bf16[512,1024]{1,0:T(8,128)(2,1)S(1)}, bf16[512,1024]{1,0:T(8,128)(2,1)S(1)}, u32[]{:S(2)}, u32[]{:S(2)}) %collective-permute-start.2) | collective-permute-done | bytes 1048608 | tf_op jit(solution)/shard_map/ppermute | solution.py:878
  37.6 2.8 constant_dynamic-slice_fusion.10
  45.5 14.4 %collective-permute-done.9 = bf16[512,1024]{1,0:T(8,128)(2,1)} collective-permute-done((bf16[512,1024]{1,0:T(8,128)(2,1)S(1)}, bf16[512,1024]{1,0:T(8,128)(2,1)}, u32[]{:S(2)}, u32[]{:S(2)}) %collective-permute-start.9) | collective-permute-done | bytes 1048608 | tf_op jit(solution)/shard_map/ppermute | solution.py:878
  61.3 2.5 constant_dynamic-slice_fusion.6
  65.2 3.2 collective-permute-done.3
  68.4 2.5 maximum_select_fusion.2
  70.9 11.8 %collective-permute-done.10 = bf16[512,1024]{1,0:T(8,128)(2,1)} collective-permute-done((bf16[512,1024]{1,0:T(8,128)(2,1)}, bf16[512,1024]{1,0:T(8,128)(2,1)}, u32[]{:S(2)}, u32[]{:S(2)}) %collective-permute-start.10) | collective-permute-done | bytes 1048608 | tf_op jit(solution)/shard_map/ppermute | solution.py:878
  84.0 4.6 convolution_convert_fusion
  88.6 2.9 collective-permute-start.4
  92.1 18.1 %collective-permute-done.4 = bf16[3,1024]{1,0:T(4,128)(2,1)S(1)} collective-permute-done((bf16[3,1024]{1,0:T(4,128)(2,1)S(1)}, bf16[3,1024]{1,0:T(4,128)(2,1)S(1)}, u32[]{:S(2)}, u32[]{:S(2)}) %collective-permute-start.4) | collective-permute-done | bytes 6176 | tf_op jit(solution)/shard_map/ppermute | solution.py:35
  110.2 2.7 maximum_convert_fusion
  112.9 4.0 maximum_select_fusion.4
  116.9 2.5 maximum_select_fusion.3
  119.5 6.5 fusion.7
  126.1 21.0 %fusion.4 = (f32[1024]{0:T(1024)}, f32[1024,1024]{1,0:T(8,128)}, bf16[1024,1024]{1,0:T(8,128)(2,1)S(1)}, f32[1024,1024]{1,0:T(8,128)}, f32[1024,1024]{1,0:T(8,128)}) fusion(f32[1024,1024]{1,0:T(8,128)} %fusion.7, f32[1024]{0:T(1024)S(1)} %get-tuple-element.61, f32[1027,1024]{1,0:T(8,128)} %maximum_convert_fusion, f32[1024]{0:T(1024)S(1)} %bitcast.90, ...), kind=kOutput, calls=%fused_computation.13 | convolution fusion | flops 4343200768 | bytes 44089344 | tf_op jit(solution)/shard_map/dot_general | solution.py:1013
  153.7 2.5 pad_maximum_fusion.refs_6_
  159.0 4.8 pad_maximum_fusion.2.refs_7_
  165.2 4.0 collective-permute-done.7
  169.3 2.4 copy.59
  173.4 5.6 compare_select_fusion
  179.0 38.9 %scan_totals.1 = (f32[16,1024]{1,0:T(8,128)S(1)}, f32[256,1024]{1,0:T(8,128)S(1)}, f32[256,1024]{1,0:T(8,128)S(1)}, f32[40,1024]{1,0:T(8,128)S(1)}) custom-call(f32[1024,1024]{1,0:T(8,128)S(1)} %get-tuple-element.110.refs_0_, bf16[1024,1024]{1,0:T(8,128)(2,1)S(1)} %get-tuple-element.56.refs_1_, f32[1024,1024]{1,0:T(8,128)S(1)} %copy-done.1, ...), custom_call_target="tpu_custom_call" | custom-call | flops 100663296000 | bytes 10485760 | tf_op jit(solution)/shard_map/scan_totals/pallas_call | solution.py:312
  218.9 2.5 collective-permute-start.13
  221.5 3.7 collective-permute-done.13
  225.3 2.6 collective-permute-start.14
  227.9 2.8 fusion.34
  230.7 6.4 copy.63.refs_1_
  239.6 89.3 %scan_grads.1 = (f32[1024,1024]{1,0:T(8,128)}, f32[1024,1024]{1,0:T(8,128)}, f32[1024,1024]{1,0:T(8,128)}, f32[2,16,1024]{2,1,0:T(8,128)S(1)}, f32[1024,128]{1,0:T(8,128)S(1)}) custom-call(f32[1024,1024]{1,0:T(8,128)} %copy-done, bf16[1024,1024]{1,0:T(8,128)(2,1)S(1)} %get-tuple-element.56.refs_1_, f32[1024,1024]{1,0:T(8,128)} %get-tuple-element.55.refs_2_, ...), custom_call_target="tpu_custom_call" | custom-call | flops 201326592000 | bytes 23068672 | tf_op jit(solution)/shard_map/scan_grads/pallas_call | solution.py:393
  329.0 5.5 multiply_convert_fusion.1
  334.5 4.5 fusion.6
  340.7 3.3 copy-done.22
  349.8 4.8 pad_maximum_fusion.1.refs_4_
  354.6 2.4 pad_maximum_fusion.4.refs_5_
  357.0 3.9 copy.62.refs_0_
  363.8 2.2 fusion.10
  366.8 12.4 %collective-permute-done.20 = f32[1024,160]{0,1:T(8,128)S(1)} collective-permute-done((f32[1024,160]{0,1:T(8,128)S(1)}, f32[1024,160]{0,1:T(8,128)S(1)}, u32[]{:S(2)}, u32[]{:S(2)}) %collective-permute-start.20) | collective-permute-done | bytes 655392 | tf_op jit(solution)/shard_map/ppermute | solution.py:878
  379.4 3.5 convert_add_fusion
  387.6 19.6 %multiply_reduce_fusion = (f32[1024]{0:T(1024)S(1)}, f32[1024]{0:T(1024)S(1)}, f32[1024]{0:T(1024)S(1)}, f32[1024]{0:T(1024)S(1)}, f32[1024]{0:T(1024)S(1)}, /*i...) fusion(f32[1027,1024]{1,0:T(8,128)} %maximum_convert_fusion, ...), kind=kOutput, calls=%fused_computation.26 | convolution fusion | flops 365325312 | bytes 46845952 | tf_op jit(solution)/shard_map/dot_general | solution.py:25
  410.9 2.8 add_convert_fusion
  415.7 5.6 pad_add_fusion
  421.4 2.2 maximum_maximum_fusion.1
  425.5 12.4 %collective-permute-done.17 = bf16[256,2048]{1,0:T(8,128)(2,1)} collective-permute-done((bf16[256,2048]{1,0:T(8,128)(2,1)S(1)}, bf16[256,2048]{1,0:T(8,128)(2,1)}, u32[]{:S(2)}, u32[]{:S(2)}) %collective-permute-start.17) | collective-permute-done | bytes 1048608 | tf_op jit(solution)/shard_map/ppermute | solution.py:878
  437.9 3.9 maximum_select_fusion.5
  441.8 216.4 %finish.1 = (bf16[3,1024,1024]{2,1,0:T(8,128)(2,1)}, bf16[336,512]{1,0:T(8,128)(2,1)}, bf16[1024,2048]{1,0:T(8,128)(2,1)}) custom-call(bf16[1024,1024]{1,0:T(8,128)(2,1)} %copy.62.refs_0_, bf16[2048,1024]{1,0:T(8,128)(2,1)} %copy.63.refs_1_, bf16[1024,1024]{1,0:T(8,128)(2,1)} %get-tuple-element.65.refs_2_, bf16[1024,1024]{1,0:T(8,128)(2,1)} %fusion.5.refs_3_, ...), custom_call_target="tpu_custom_call" | custom-call | flops 149999992832 | bytes 60000000 | tf_op jit(solution)/shard_map/finish/pallas_call | solution.py:815
  660.5 8.9 %convert_element_type.150 = f32[3,1024,1024]{2,1,0:T(8,128)} convert(bf16[3,1024,1024]{2,1,0:T(8,128)(2,1)} %get-tuple-element.42) | non-fusion elementwise | flops 3145728 | bytes 18874368 | tf_op jit(solution)/shard_map/convert_element_type | solution.py:1186
  672.8 10.1 %slice_bitcast_fusion = (f32[1024,1024]{1,0:T(8,128)}, f32[1024,1024]{1,0:T(8,128)}, f32[1024,1024]{1,0:T(8,128)}) fusion(f32[3,1024,1024]{2,1,0:T(8,128)} %convert_element_type.150), kind=kLoop, calls=%fused_computation.14 | loop fusion | bytes 25165824 | tf_op jit(solution)/shard_map/squeeze | solution.py:1190
  682.9 4.7 maximum_select_fusion
  688.2 3.0 maximum_select_fusion.1
  (243 shorter events, 73.4 us)
Async XLA Ops:
  0.6 19.2 %copy-start.62 = (s32[1,3]{1,0:T(1,128)S(1)}, s32[1,3]{1,0:T(1,128)}, u32[]{:S(2)}) copy-start(s32[1,3]{1,0:T(1,128)} %param.16) | copy-start | bytes 40
  4.3 8.2 %collective-permute-start = (bf16[23,512]{1,0:T(8,128)(2,1)S(1)}, bf16[23,512]{1,0:T(8,128)(2,1)S(1)}, u32[]{:S(2)}, u32[]{:S(2)}) collective-permute-start(bf16[23,512]{1,0:T(8,128)(2,1)S(1)} %concatenate.114), channel_id=1, source_target_pairs={{0,16},{16,0},{1,17},{17,1},{2,18},{18,2},{3,19},{19,3},{4,20},{20... | collective-permute-start | bytes 70664 | tf_op jit(solution)/shard_map/ppermute | solution.py:878
  7.3 56.6 %collective-permute-start.1 = (bf16[1024]{0:T(1024)(128)(2,1)}, bf16[1024]{0:T(1024)(128)(2,1)S(1)}, u32[]{:S(2)}, u32[]{:S(2)}) collective-permute-start(bf16[1024]{0:T(1024)(128)(2,1)} %param.18), channel_id=1, source_target_pairs={{0,16},{16,0},{1,17},{17,1},{2,18},{18,2},{3,19},{19,3},{4,20},{20... | collective-permute-start | bytes 6152 | tf_op jit(solution)/shard_map/ppermute | solution.py:878
  7.4 139.7 %collective-permute-start.5 = (bf16[512,160]{0,1:T(8,128)(2,1)}, bf16[512,160]{0,1:T(8,128)(2,1)}, u32[]{:S(2)}, u32[]{:S(2)}) collective-permute-start(bf16[512,160]{0,1:T(8,128)(2,1)} %param.23), channel_id=1, source_target_pairs={{0,16},{16,0},{1,17},{17,1},{2,18},{18,2},{3,19},{19,3},{4,20},{20... | collective-permute-start | bytes 491528 | tf_op jit(solution)/shard_map/ppermute | solution.py:878
  12.5 224.6 %copy-start.35 = (f32[23,1024]{1,0:T(8,128)}, f32[23,1024]{1,0:T(8,128)S(1)}, u32[]{:S(2)}) copy-start(f32[23,1024]{1,0:T(8,128)S(1)} %fusion.13) | copy-start | bytes 282628
  12.5 24.1 %collective-permute-start.2 = (bf16[512,1024]{1,0:T(8,128)(2,1)S(1)}, bf16[512,1024]{1,0:T(8,128)(2,1)S(1)}, u32[]{:S(2)}, u32[]{:S(2)}) collective-permute-start(bf16[512,1024]{1,0:T(8,128)(2,1)S(1)} %constant_dynamic-slice_fusion.7), channel_id=1, source_target_pairs={{0,16},{16,0},{1,17},{17,1},{2,18},{18,2},{3,19},{19,3},{4,20},{20... | collective-permute-start | bytes 3145736 | tf_op jit(solution)/shard_map/ppermute | solution.py:878
  36.6 23.2 %collective-permute-start.9 = (bf16[512,1024]{1,0:T(8,128)(2,1)S(1)}, bf16[512,1024]{1,0:T(8,128)(2,1)}, u32[]{:S(2)}, u32[]{:S(2)}) collective-permute-start(bf16[512,1024]{1,0:T(8,128)(2,1)S(1)} %constant_dynamic-slice_fusion.3), channel_id=1, source_target_pairs={{0,16},{16,0},{1,17},{17,1},{2,18},{18,2},{3,19},{19,3},{4,20},{20... | collective-permute-start | bytes 3145736 | tf_op jit(solution)/shard_map/ppermute | solution.py:878
  40.4 43.5 %copy-start.6 = (bf16[1024,1024]{1,0:T(8,128)(2,1)}, bf16[1024,1024]{1,0:T(8,128)(2,1)S(1)}, u32[]{:S(2)}) copy-start(bf16[1024,1024]{1,0:T(8,128)(2,1)S(1)} %get-tuple-element.75) | copy-start | bytes 6291460
  40.4 20.9 %copy-start.28 = (bf16[1024,2048]{1,0:T(8,128)(2,1)S(1)}, bf16[1024,2048]{1,0:T(8,128)(2,1)}, u32[]{:S(2)}) copy-start(bf16[1024,2048]{1,0:T(8,128)(2,1)} %param.29) | copy-start | bytes 12582916
  40.5 85.6 %copy-start.59 = (f32[1024]{0:T(1024)}, f32[1024]{0:T(1024)S(1)}, u32[]{:S(2)}) copy-start(f32[1024]{0:T(1024)S(1)} %get-tuple-element.61) | copy-start | bytes 12292
  42.8 25.6 %collective-permute-start.3 = (bf16[512,1024]{1,0:T(8,128)(2,1)S(1)}, bf16[512,1024]{1,0:T(8,128)(2,1)}, u32[]{:S(2)}, u32[]{:S(2)}) collective-permute-start(bf16[512,1024]{1,0:T(8,128)(2,1)S(1)} %collective-permute-done.2), channel_id=1, source_target_pairs={{0,4},{4,0},{8,12},{12,8},{1,5},{5,1},{9,13},{13,9},{2,6},{6,2},{1... | collective-permute-start | bytes 3145736 | tf_op jit(solution)/shard_map/ppermute | solution.py:878
  59.9 22.9 %collective-permute-start.10 = (bf16[512,1024]{1,0:T(8,128)(2,1)}, bf16[512,1024]{1,0:T(8,128)(2,1)}, u32[]{:S(2)}, u32[]{:S(2)}) collective-permute-start(bf16[512,1024]{1,0:T(8,128)(2,1)} %constant_dynamic-slice_fusion.4), channel_id=1, source_target_pairs={{0,16},{16,0},{1,17},{17,1},{2,18},{18,2},{3,19},{19,3},{4,20},{20... | collective-permute-start | bytes 3145736 | tf_op jit(solution)/shard_map/ppermute | solution.py:878
  61.3 64.8 %copy-start.55 = (f32[1024]{0:T(1024)}, f32[1024]{0:T(1024)S(1)}, u32[]{:S(2)}) copy-start(f32[1024]{0:T(1024)S(1)} %get-tuple-element.105) | copy-start | bytes 12292
  61.3 64.8 %copy-start.57 = (f32[1024]{0:T(1024)}, f32[1024]{0:T(1024)S(1)}, u32[]{:S(2)}) copy-start(f32[1024]{0:T(1024)S(1)} %get-tuple-element.106) | copy-start | bytes 12292
  63.9 20.1 %copy-start.10 = (bf16[1024,1024]{1,0:T(8,128)(2,1)S(1)}, bf16[1024,1024]{1,0:T(8,128)(2,1)}, u32[]{:S(2)}) copy-start(bf16[1024,1024]{1,0:T(8,128)(2,1)} %copy-done.9) | copy-start | bytes 6291460
  63.9 20.1 %copy-start.23 = (bf16[1024,1024]{1,0:T(8,128)(2,1)S(1)}, bf16[1024,1024]{1,0:T(8,128)(2,1)}, u32[]{:S(2)}) copy-start(bf16[1024,1024]{1,0:T(8,128)(2,1)} %param.19) | copy-start | bytes 6291460
  63.9 164.0 %copy-start.41 = (f32[2048]{0:T(1024)}, f32[2048]{0:T(1024)S(1)}, u32[]{:S(2)}) copy-start(f32[2048]{0:T(1024)S(1)} %pad_maximum_fusion.11) | copy-start | bytes 24580
  63.9 49.0 %collective-permute-start.12 = (bf16[512,1024]{1,0:T(8,128)(2,1)}, bf16[512,1024]{1,0:T(8,128)(2,1)S(1)}, u32[]{:S(2)}, u32[]{:S(2)}) collective-permute-start(bf16[512,1024]{1,0:T(8,128)(2,1)} %collective-permute-done.9), channel_id=1, source_target_pairs={{0,4},{4,0},{8,12},{12,8},{1,5},{5,1},{9,13},{13,9},{2,6},{6,2},{1... | collective-permute-start | bytes 3145736 | tf_op jit(solution)/shard_map/ppermute | solution.py:878
  70.9 17.6 %copy-start.19 = (bf16[1024,1024]{1,0:T(8,128)(2,1)}, bf16[1024,1024]{1,0:T(8,128)(2,1)S(1)}, u32[]{:S(2)}) copy-start(bf16[1024,1024]{1,0:T(8,128)(2,1)S(1)} %maximum_select_fusion.2) | copy-start | bytes 6291460
  82.7 34.2 %collective-permute-start.11 = (bf16[512,1024]{1,0:T(8,128)(2,1)}, bf16[512,1024]{1,0:T(8,128)(2,1)S(1)}, u32[]{:S(2)}, u32[]{:S(2)}) collective-permute-start(bf16[512,1024]{1,0:T(8,128)(2,1)} %collective-permute-done.10), channel_id=1, source_target_pairs={{0,4},{4,0},{8,12},{12,8},{1,5},{5,1},{9,13},{13,9},{2,6},{6,2},{1... | collective-permute-start | bytes 3145736 | tf_op jit(solution)/shard_map/ppermute | solution.py:878
  88.6 21.6 %collective-permute-start.4 = (bf16[3,1024]{1,0:T(4,128)(2,1)S(1)}, bf16[3,1024]{1,0:T(4,128)(2,1)S(1)}, u32[]{:S(2)}, u32[]{:S(2)}) collective-permute-start(bf16[3,1024]{1,0:T(4,128)(2,1)S(1)} %slice.212), channel_id=1, source_target_pairs={{0,4},{4,8},{8,12},{1,5},{5,9},{9,13},{2,6},{6,10},{10,14},{3,7},{... | collective-permute-start | bytes 18440 | tf_op jit(solution)/shard_map/ppermute | solution.py:35
  92.1 34.0 %copy-start.47 = (f32[1,1024]{1,0:T(1,128)}, f32[1,1024]{1,0:T(1,128)S(1)}, u32[]{:S(2)}) copy-start(f32[1,1024]{1,0:T(1,128)S(1)} %get-tuple-element.98) | copy-start | bytes 12292
  92.1 34.0 %copy-start.49 = (f32[1,1024]{1,0:T(1,128)}, f32[1,1024]{1,0:T(1,128)S(1)}, u32[]{:S(2)}) copy-start(f32[1,1024]{1,0:T(1,128)S(1)} %get-tuple-element.99) | copy-start | bytes 12292
  92.1 34.0 %copy-start.51 = (f32[1,1024]{1,0:T(1,128)}, f32[1,1024]{1,0:T(1,128)S(1)}, u32[]{:S(2)}) copy-start(f32[1,1024]{1,0:T(1,128)S(1)} %get-tuple-element.100) | copy-start | bytes 12292
  92.1 34.0 %copy-start.53 = (f32[1,1024]{1,0:T(1,128)}, f32[1,1024]{1,0:T(1,128)S(1)}, u32[]{:S(2)}) copy-start(f32[1,1024]{1,0:T(1,128)S(1)} %get-tuple-element.101) | copy-start | bytes 12292
  92.1 81.2 %copy-start.43 = (f32[1,1024]{1,0:T(1,128)}, f32[1,1024]{1,0:T(1,128)S(1)}, u32[]{:S(2)}) copy-start(f32[1,1024]{1,0:T(1,128)S(1)} %get-tuple-element.97) | copy-start | bytes 12292
  126.1 21.0 %copy-start.63 = (bf16[512,160]{0,1:T(8,128)(2,1)S(1)}, bf16[512,160]{0,1:T(8,128)(2,1)}, u32[]{:S(2)}) copy-start(bf16[512,160]{0,1:T(8,128)(2,1)} %param.23) | copy-start | bytes 491524
  149.1 2.2 collective-permute-start.6
  149.2 24.2 %collective-permute-start.8 = (bf16[64,1024]{1,0:T(8,128)(2,1)S(1)}, bf16[64,1024]{1,0:T(8,128)(2,1)}, u32[]{:S(2)}, u32[]{:S(2)}) collective-permute-start(bf16[64,1024]{1,0:T(8,128)(2,1)S(1)} %copy-done.65), channel_id=1, source_target_pairs={{0,16},{16,0},{1,17},{17,1},{2,18},{18,2},{3,19},{19,3},{4,20},{20... | collective-permute-start | bytes 393224 | tf_op jit(solution)/shard_map/ppermute | solution.py:878
  152.2 17.1 %collective-permute-start.7 = (f32[1024,160]{0,1:T(8,128)}, f32[1024,160]{0,1:T(8,128)}, u32[]{:S(2)}, u32[]{:S(2)}) collective-permute-start(f32[1024,160]{0,1:T(8,128)} %add.266), channel_id=1, source_target_pairs={{0,2},{1,3},{2,0},{3,1},{4,6},{5,7},{6,4},{7,5},{8,10},{9,11},{10,... | collective-permute-start | bytes 1966088 | tf_op jit(solution)/shard_map/ppermute | solution.py:878
  179.0 38.9 %copy-start = (f32[1024,1024]{1,0:T(8,128)}, f32[1024,1024]{1,0:T(8,128)S(1)}, u32[]{:S(2)}) copy-start(f32[1024,1024]{1,0:T(8,128)S(1)} %get-tuple-element.110.refs_0_) | copy-start | bytes 12582916
  179.0 48.9 %copy-start.8 = (bf16[1024,1024]{1,0:T(8,128)(2,1)S(1)}, bf16[1024,1024]{1,0:T(8,128)(2,1)}, u32[]{:S(2)}) copy-start(bf16[1024,1024]{1,0:T(8,128)(2,1)} %copy-done.6) | copy-start | bytes 6291460
  179.0 48.9 %copy-start.12 = (bf16[1024,1024]{1,0:T(8,128)(2,1)S(1)}, bf16[1024,1024]{1,0:T(8,128)(2,1)}, u32[]{:S(2)}) copy-start(bf16[1024,1024]{1,0:T(8,128)(2,1)} %copy-done.9) | copy-start | bytes 6291460
  218.9 6.2 collective-permute-start.13
  225.3 11.8 %collective-permute-start.14 = (f32[40,1024]{1,0:T(8,128)S(1)}, f32[40,1024]{1,0:T(8,128)S(1)}, u32[]{:S(2)}, u32[]{:S(2)}) collective-permute-start(f32[40,1024]{1,0:T(8,128)S(1)} %pad_maximum_fusion.10), channel_id=1, source_target_pairs={{0,8},{4,12},{8,0},{12,4},{1,9},{5,13},{9,1},{13,5},{2,10},{6,14},... | collective-permute-start | bytes 491528 | tf_op jit(solution)/shard_map/ppermute | solution.py:878
  239.6 89.3 %copy-start.25 = (f32[1024,1024]{1,0:T(8,128)S(1)}, f32[1024,1024]{1,0:T(8,128)}, u32[]{:S(2)}) copy-start(f32[1024,1024]{1,0:T(8,128)} %fusion.7) | copy-start | bytes 12582916
  239.6 89.3 %copy-start.26 = (f32[1024,1024]{1,0:T(8,128)S(1)}, f32[1024,1024]{1,0:T(8,128)}, u32[]{:S(2)}) copy-start(f32[1024,1024]{1,0:T(8,128)} %get-tuple-element.109) | copy-start | bytes 12582916
  239.6 89.3 %copy-start.42 = (f32[1,1024]{1,0:T(1,128)S(1)}, f32[1,1024]{1,0:T(1,128)}, u32[]{:S(2)}) copy-start(f32[1,1024]{1,0:T(1,128)} %get-tuple-element.96) | copy-start | bytes 12292
  334.5 9.5 %copy-start.31 = (f32[1024,1024]{1,0:T(8,128)S(1)}, f32[1024,1024]{1,0:T(8,128)}, u32[]{:S(2)}) copy-start(f32[1024,1024]{1,0:T(8,128)} %get-tuple-element.37) | copy-start | bytes 12582916
  340.7 38.7 %collective-permute-start.15 = (bf16[512,2048]{1,0:T(8,128)(2,1)}, bf16[512,2048]{1,0:T(8,128)(2,1)}, u32[]{:S(2)}, u32[]{:S(2)}) collective-permute-start(bf16[512,2048]{1,0:T(8,128)(2,1)} %dynamic-slice_convert_fusion), channel_id=1, source_target_pairs={{0,1},{1,0},{2,3},{3,2},{4,5},{5,4},{6,7},{7,6},{8,9},{9,8},{10,11... | collective-permute-start | bytes 6291464 | tf_op jit(solution)/shard_map/ppermute | solution.py:878
  349.8 11.2 %collective-permute-start.19 = (f32[1024,160]{0,1:T(8,128)}, f32[1024,160]{0,1:T(8,128)}, u32[]{:S(2)}, u32[]{:S(2)}) collective-permute-start(f32[1024,160]{0,1:T(8,128)} %pad_maximum_fusion.7), channel_id=1, source_target_pairs={{0,1},{1,0},{2,3},{3,2},{4,5},{5,4},{6,7},{7,6},{8,9},{9,8},{10,11... | collective-permute-start | bytes 1966088 | tf_op jit(solution)/shard_map/ppermute | solution.py:878
  362.2 17.0 %collective-permute-start.20 = (f32[1024,160]{0,1:T(8,128)S(1)}, f32[1024,160]{0,1:T(8,128)S(1)}, u32[]{:S(2)}, u32[]{:S(2)}) collective-permute-start(f32[1024,160]{0,1:T(8,128)S(1)} %fusion.32), channel_id=1, source_target_pairs={{0,2},{1,3},{2,0},{3,1},{4,6},{5,7},{6,4},{7,5},{8,10},{9,11},{10,... | collective-permute-start | bytes 1966088 | tf_op jit(solution)/shard_map/ppermute | solution.py:878
  379.3 8.2 %copy-start.48 = (f32[1,1024]{1,0:T(1,128)S(1)}, f32[1,1024]{1,0:T(1,128)}, u32[]{:S(2)}) copy-start(f32[1,1024]{1,0:T(1,128)} %copy-done.47) | copy-start | bytes 12292
  386.0 24.9 %collective-permute-start.16 = (bf16[256,2048]{1,0:T(8,128)(2,1)}, bf16[256,2048]{1,0:T(8,128)(2,1)}, u32[]{:S(2)}, u32[]{:S(2)}) collective-permute-start(bf16[256,2048]{1,0:T(8,128)(2,1)} %dynamic-slice_convert_fusion.1), channel_id=1, source_target_pairs={{0,2},{1,3},{2,0},{3,1},{4,6},{5,7},{6,4},{7,5},{8,10},{9,11},{10,... | collective-permute-start | bytes 3145736 | tf_op jit(solution)/shard_map/ppermute | solution.py:878
  408.0 15.6 %collective-permute-start.21 = (f32[3,1024]{1,0:T(4,128)S(1)}, f32[3,1024]{1,0:T(4,128)S(1)}, u32[]{:S(2)}, u32[]{:S(2)}) collective-permute-start(f32[3,1024]{1,0:T(4,128)S(1)} %pad_add_fusion.1), channel_id=1, source_target_pairs={{4,0},{8,4},{12,8},{5,1},{9,5},{13,9},{6,2},{10,6},{14,10},{7,3},{... | collective-permute-start | bytes 36872 | tf_op jit(solution)/shard_map/ppermute | solution.py:35
  413.7 24.2 %collective-permute-start.17 = (bf16[256,2048]{1,0:T(8,128)(2,1)S(1)}, bf16[256,2048]{1,0:T(8,128)(2,1)}, u32[]{:S(2)}, u32[]{:S(2)}) collective-permute-start(bf16[256,2048]{1,0:T(8,128)(2,1)S(1)} %add_convert_fusion), channel_id=1, source_target_pairs={{0,2},{1,3},{2,0},{3,1},{4,6},{5,7},{6,4},{7,5},{8,10},{9,11},{10,... | collective-permute-start | bytes 3145736 | tf_op jit(solution)/shard_map/ppermute | solution.py:878
  441.8 241.2 %collective-permute-start.18 = (bf16[512,2048]{1,0:T(8,128)(2,1)}, bf16[512,2048]{1,0:T(8,128)(2,1)}, u32[]{:S(2)}, u32[]{:S(2)}) collective-permute-start(bf16[512,2048]{1,0:T(8,128)(2,1)} %maximum_select_fusion.5), channel_id=1, source_target_pairs={{0,1},{1,0},{2,3},{3,2},{4,5},{5,4},{6,7},{7,6},{8,9},{9,8},{10,11... | collective-permute-start | bytes 6291464 | tf_op jit(solution)/shard_map/ppermute | solution.py:878
  660.5 9.6 %copy-start.37 = (bf16[336,512]{1,0:T(8,128)(2,1)S(1)}, bf16[336,512]{1,0:T(8,128)(2,1)}, u32[]{:S(2)}) copy-start(bf16[336,512]{1,0:T(8,128)(2,1)} %get-tuple-element.41) | copy-start | bytes 1032196
  (41 other events, 208.8 us)

commit v2 on v1

--- a/solution.py
+++ b/solution.py
@@ -90,12 +90,25 @@
                 extra_ref[g * steps : (g + 1) * steps] = first
 
 
+def silu_rows(left_ref, gate_ref, out_ref):
+    strip = 128
+
+    def one(r, _):
+        at = pl.ds(pl.multiple_of(r * strip, strip), strip)
+        gate = gate_ref[at, :]
+        out_ref[at, :] = left_ref[at, :] * gate * jax.nn.sigmoid(gate)
+        return 0
+
+    lax.fori_loop(0, out_ref.shape[0] // strip, one, 0)
+
+
 def totals_kernel(
     groups,
     steps,
     step_ref,
     act_ref,
-    dy_ref,
+    d_gated_ref,
+    gate_ref,
     rate_ref,
     table_ref,
     seg_s_ref,
@@ -105,6 +118,7 @@
     bc_s,
     keep_s,
     act_s,
+    dy_s,
 ):
     rows_of = SEGS * steps
 
@@ -113,6 +127,7 @@
         spread_columns(table_ref, bc_s, keep_s, act_s, groups, steps)
 
     act_s[...] = act_ref[...].astype(F32)
+    silu_rows(d_gated_ref, gate_ref, dy_s)
     half = N
     zero = jnp.zeros((SEGS, LANES), F32)
     for g in range(groups):
@@ -126,7 +141,7 @@
                 total, state, reach, back = carry
                 state, reach, back = list(state), list(reach), list(back)
                 at = pl.ds(g * rows_of + i, SEGS, stride=steps)
-                step, act, dy = step_ref[at, :], act_s[at, :], dy_ref[at, :]
+                step, act, dy = step_ref[at, :], act_s[at, :], dy_s[at, :]
                 gone = step + keep_s[g * steps + i]
                 push = step * act
                 for n in range(half):
@@ -173,8 +188,11 @@
     steps,
     blocks,
     step_ref,
+    pre_ref,
     act_ref,
-    dy_ref,
+    d_gated_ref,
+    gate_ref,
+    skip_ref,
     rate_ref,
     table_ref,
     seg_s_ref,
@@ -182,9 +200,11 @@
     seg_c_ref,
     h_in_ref,
     c_in_ref,
-    y_ref,
-    d_step_ref,
-    d_act_ref,
+    gated_t_ref,
+    gated_ref,
+    d_gate_ref,
+    d_pre_ref,
+    drive_ref,
     d_rate_ref,
     d_bc_ref,
     bc_s,
@@ -196,6 +216,10 @@
     prior_s,
     sum_b,
     sum_c,
+    dy_s,
+    y_s,
+    d_step_s,
+    d_act_s,
 ):
     g, j = pl.program_id(0), pl.program_id(1)
 
@@ -224,6 +248,7 @@
             c = jnp.exp2(rate * spent) * c + seg_c_ref[at, :]
 
     act_s[...] = act_ref[...].astype(F32)
+    silu_rows(d_gated_ref, gate_ref, dy_s)
     first = g * N * SEGS
 
     def rate_row(n):
@@ -232,7 +257,7 @@
     def ahead(i, state):
         state = list(state)
         at = pl.ds(i, SEGS, stride=steps)
-        step, act, dy = step_ref[at, :], act_s[at, :], dy_ref[at, :]
+        step, act, dy = step_ref[at, :], act_s[at, :], dy_s[at, :]
         gone = step + keep_s[i]
         push = step * act
         y = jnp.zeros((SEGS, LANES), F32)
@@ -244,7 +269,7 @@
             prior_s[i, n] = prior
             y = y + state[n] * bc_s[i, N + n]
             sum_c[i, n] += state[n] * dy
-        y_ref[at, :] = y
+        y_s[at, :] = y
         return tuple(state)
 
     def enter(ref, n):
@@ -256,7 +281,7 @@
         i = steps - 1 - k
         carried, d_rate = list(carry[0]), list(carry[1])
         at = pl.ds(i, SEGS, stride=steps)
-        step, act, dy = step_ref[at, :], act_s[at, :], dy_ref[at, :]
+        step, act, dy = step_ref[at, :], act_s[at, :], dy_s[at, :]
         push = step * act
         along = jnp.zeros((SEGS, LANES), F32)
         d_step = jnp.zeros((SEGS, LANES), F32)
@@ -268,8 +293,8 @@
             d_rate[n] = d_rate[n] + log_grad * step
             carried[n] = grad * decay_s[i, n]
             sum_b[i, n] += grad * push
-        d_step_ref[at, :] = d_step * LN2 + along * act
-        d_act_ref[at, :] = along * step
+        d_step_s[at, :] = d_step * LN2 + along * act
+        d_act_s[at, :] = along * step
         return (tuple(carried), tuple(d_rate))
 
     zero = jnp.zeros((SEGS, LANES), F32)
@@ -278,6 +303,32 @@
     )
     for n in range(N):
         d_rate_ref[0, n : n + 1, :] = jnp.sum(d_rate[n], axis=0, keepdims=True)
+
+    strip = 64
+
+    def close(r, sums):
+        at = pl.ds(pl.multiple_of(r * strip, strip), strip)
+        gate, d_gated, act, dy = gate_ref[at, :], d_gated_ref[at, :], act_s[at, :], dy_s[at, :]
+        skip = skip_ref[...]
+        sig = jax.nn.sigmoid(gate)
+        scan_out = y_s[at, :] + skip * act
+        gated = scan_out * gate * sig
+        y_s[at, :] = gated
+        gated_ref[at, :] = gated.astype(BF16)
+        d_gate_ref[at, :] = (d_gated * scan_out * sig * (1.0 + gate * (1.0 - sig))).astype(BF16)
+        d_pre = (d_step_s[at, :] * jax.nn.sigmoid(pre_ref[at, :])).astype(BF16)
+        d_pre_ref[at, :] = d_pre
+        drive_ref[at, :] = d_act_s[at, :] + dy * skip
+
+        def fold(value):
+            return jnp.sum(value.reshape(strip // SEGS, SEGS, LANES), axis=0)
+
+        return sums[0] + fold(dy * act), sums[1] + fold(d_pre.astype(F32))
+
+    g_skip, g_bias = lax.fori_loop(0, y_s.shape[0] // strip, close, (zero, zero))
+    d_rate_ref[0, N : N + 1, :] = jnp.sum(g_skip, axis=0, keepdims=True)
+    d_rate_ref[0, N + 1 : N + 2, :] = jnp.sum(g_bias, axis=0, keepdims=True)
+    gated_t_ref[...] = y_s[...].T.astype(BF16)
 
     @pl.when(j == blocks - 1)
     def _():
@@ -301,22 +352,21 @@
         lax.fori_loop(0, steps, put, 0, unroll=8)
 
 
-def scan_totals(step_size, activated, dy_scan, rate2, table, groups, begin, channels):
-    length = step_size.shape[0]
+def scan_totals(step_size, activated, d_gated, gate_z, rate2, table, groups):
+    length, channels = step_size.shape
     steps = length // (groups * SEGS)
     blocks = channels // LANES
-    skip = begin // LANES
-    body = lambda *refs: totals_kernel(groups, steps, *refs)
-    tall = pl.BlockSpec((length, LANES), lambda j: (0, j + skip))
+    tall = pl.BlockSpec((length, LANES), lambda j: (0, j))
     rows = groups * N * SEGS
     return pl.pallas_call(
-        body,
+        lambda *refs: totals_kernel(groups, steps, *refs),
         grid=(blocks,),
         in_specs=[
             tall,
             tall,
             tall,
-            pl.BlockSpec((N, LANES), lambda j: (0, j + skip)),
+            tall,
+            pl.BlockSpec((N, LANES), lambda j: (0, j)),
             pl.BlockSpec((length, LANES), lambda j: (0, 0)),
         ],
         out_specs=[
@@ -335,103 +385,121 @@
             pltpu.VMEM((groups * steps, 2 * N, SEGS, LANES), F32),
             pltpu.VMEM((groups * steps, SEGS, LANES), F32),
             pltpu.VMEM((length, LANES), F32),
+            pltpu.VMEM((length, LANES), F32),
         ],
         compiler_params=pltpu.CompilerParams(
             dimension_semantics=("arbitrary",), vmem_limit_bytes=40 << 20
         ),
         cost_estimate=pl.CostEstimate(
-            flops=length * channels * N * 6000,
-            bytes_accessed=length * channels * 10,
+            flops=length * channels * N * 3000,
+            bytes_accessed=length * channels * 14,
             transcendentals=length * channels * N,
         ),
         name="scan_totals",
-    )(step_size, activated, dy_scan, rate2, table)
-
-
-def scan_grads(step_size, activated, dy_scan, rate2, table, segs, enter, groups, begin, channels):
-    length = step_size.shape[0]
+    )(step_size, activated, d_gated, gate_z, rate2, table)
+
+
+def scan_grads(
+    step_size, step_pre, activated, d_gated, gate_z, skip, rate2, table, segs, enter, groups
+):
+    length, channels = step_size.shape
     steps = length // (groups * SEGS)
     blocks = channels // LANES
-    skip = begin // LANES
-    body = lambda *refs: grads_kernel(groups, steps, blocks, *refs)
-    tall = pl.BlockSpec((length // groups, LANES), lambda g, j: (g, j + skip))
-    short = pl.BlockSpec((length // groups, LANES), lambda g, j: (g, j))
+    share = length // groups
+    tall = pl.BlockSpec((share, LANES), lambda g, j: (g, j))
+    one = pl.BlockSpec((share, LANES), lambda g, j: (g, 0))
     rows = groups * N * SEGS
+
+    def wide(height):
+        return pl.BlockSpec((height, LANES), lambda g, j: (0, j))
+
+    def shape(dtype, *dims):
+        return jax.ShapeDtypeStruct(dims, dtype)
+
     grid_spec = pl.GridSpec(
         grid=(groups, blocks),
-        in_specs=[
-            tall,
-            tall,
-            tall,
-            pl.BlockSpec((N, LANES), lambda g, j: (0, j + skip)),
-            pl.BlockSpec((length // groups, LANES), lambda g, j: (g, 0)),
-            pl.BlockSpec((groups * SEGS, LANES), lambda g, j: (0, j)),
-            pl.BlockSpec((rows, LANES), lambda g, j: (0, j)),
-            pl.BlockSpec((rows, LANES), lambda g, j: (0, j)),
-            pl.BlockSpec((N, LANES), lambda g, j: (0, j)),
-            pl.BlockSpec((N, LANES), lambda g, j: (0, j)),
-        ],
-        out_specs=[
-            short,
-            short,
-            short,
-            pl.BlockSpec((1, N, LANES), lambda g, j: (g, 0, j)),
-            pl.BlockSpec((length // groups, LANES), lambda g, j: (g, 0)),
-        ],
+        in_specs=[tall] * 5
+        + [wide(1), wide(N), one]
+        + [wide(groups * SEGS), wide(rows), wide(rows), wide(N), wide(N)],
+        out_specs=[pl.BlockSpec((LANES, share), lambda g, j: (j, g))]
+        + [tall] * 4
+        + [pl.BlockSpec((1, 3 * SEGS, LANES), lambda g, j: (g, 0, j)), one],
         scratch_shapes=[
             pltpu.VMEM((steps, 2 * N, SEGS, LANES), F32),
             pltpu.VMEM((steps, SEGS, LANES), F32),
-            pltpu.VMEM((length // groups, LANES), F32),
+            pltpu.VMEM((share, LANES), F32),
             pltpu.VMEM((blocks, rows, LANES), F32),
             pltpu.VMEM((blocks, rows, LANES), F32),
             pltpu.VMEM((steps, N, SEGS, LANES), F32),
             pltpu.VMEM((steps, N, SEGS, LANES), F32),
             pltpu.VMEM((steps, N, SEGS, LANES), F32),
             pltpu.VMEM((steps, N, SEGS, LANES), F32),
+            pltpu.VMEM((share, LANES), F32),
+            pltpu.VMEM((share, LANES), F32),
+            pltpu.VMEM((share, LANES), F32),
+            pltpu.VMEM((share, LANES), F32),
         ],
     )
     return pl.pallas_call(
-        body,
+        lambda *refs: grads_kernel(groups, steps, blocks, *refs),
         grid_spec=grid_spec,
         out_shape=[
-            jax.ShapeDtypeStruct((length, channels), F32),
-            jax.ShapeDtypeStruct((length, channels), F32),
-            jax.ShapeDtypeStruct((length, channels), F32),
-            jax.ShapeDtypeStruct((groups, N, channels), F32),
-            jax.ShapeDtypeStruct((length, LANES), F32),
+            shape(BF16, channels, length),
+            shape(BF16, length, channels),
+            shape(BF16, length, channels),
+            shape(BF16, length, channels),
+            shape(F32, length, channels),
+            shape(F32, groups, 3 * SEGS, channels),
+            shape(F32, length, LANES),
         ],
         compiler_params=pltpu.CompilerParams(
             dimension_semantics=("arbitrary", "arbitrary"), vmem_limit_bytes=48 << 20
         ),
         cost_estimate=pl.CostEstimate(
-            flops=length * channels * N * 12000,
-            bytes_accessed=length * channels * 22,
+            flops=length * channels * N * 6000,
+            bytes_accessed=length * channels * 30,
             transcendentals=length * channels * N,
         ),
         name="scan_grads",
-    )(step_size, activated, dy_scan, rate2, table, *segs, *enter)
+    )(step_size, step_pre, activated, d_gated, gate_z, skip, rate2, table, *segs, *enter)
 
 
 MESH = pl.DeviceIdType.MESH
-CHUNK = 256
+CHUNK = 128
+AHEAD = 4
+LAG = 2
+WIDE = 256
 
 
 def finish_kernel(
     parts,
+    gated_t_hbm,
     gated_hbm,
     normed_hbm,
     d_gate_hbm,
-    d_inner_hbm,
+    d_pre_hbm,
+    drive_hbm,
+    inner_hbm,
+    halo_hbm,
     w_inx_hbm,
     w_inz_hbm,
+    w_out_hbm,
     x_hbm,
     dy_hbm,
     rms_ref,
     gain_ref,
-    small_send_ref,
-    small_keep_ref,
-    sums_hbm,
+    masks_ref,
+    taps_ref,
+    w_step_ref,
+    w_proj_ref,
+    d_bc_ref,
+    misc_ref,
+    g_step_ref,
+    sums_out,
+    sums_z,
+    sums_x,
     small_ref,
+    out_hbm,
     grad_hbm,
     left,
     right,
@@ -453,6 +521,7 @@
     rows_x,
     rows_dy,
     final,
+    passed,
     gain_sum,
     gain_core,
     gain_x,
@@ -462,6 +531,19 @@
     s_a,
     s_b,
     s_line,
+    p_out,
+    p_in,
+    q_out,
+    q_in,
+    turned_p,
+    drive,
+    inner_low,
+    inner,
+    active,
+    pack,
+    tail,
+    halo_out,
+    halo_in,
     load_sem,
     w_sem,
     y_sem,
@@ -473,46 +555,52 @@
     gain_sem,
     final_sem,
     small_sem,
+    chain_sem,
+    proj_sem,
+    halo_sem,
 ):
     rows, width = x_hbm.shape
     half = width // 2
     dp, z, tp = lax.axis_index("dp"), lax.axis_index("ctx"), lax.axis_index("tp")
     core, x_bit = tp % 2, tp // 2
-    near, across, diagonal = tp + 1 - 2 * core, (tp + 2) % 4, 3 - tp
+    near, across = tp + 1 - 2 * core, (tp + 2) % 4
     ends = (z == 0) | (z == 3)
     middle = (z == 1) | (z == 2)
     inward, twin, outward = z // 2 + 1, 3 - z, (z // 2) * 3
 
-    loads = [
-        pltpu.make_async_copy(gated_hbm, left.at[0], load_sem.at[0]),
-        pltpu.make_async_copy(dy_hbm.at[:, pl.ds(half, half)], right.at[1], load_sem.at[1]),
-        pltpu.make_async_copy(dy_hbm.at[:, pl.ds(0, half)], right.at[0], load_sem.at[2]),
-        pltpu.make_async_copy(normed_hbm.at[pl.ds(0, half), :], left.at[1], load_sem.at[3]),
-        pltpu.make_async_copy(normed_hbm.at[pl.ds(half, half), :], left.at[2], load_sem.at[4]),
-        pltpu.make_async_copy(d_gate_hbm, right.at[2], load_sem.at[5]),
-        pltpu.make_async_copy(d_inner_hbm, right.at[3], load_sem.at[6]),
-    ]
+    def load(source, target, at):
+        copy = pltpu.make_async_copy(source, target, load_sem.at[at])
+        copy.start()
+        return copy
+
     quarter = rows // 4
     own_row = pl.multiple_of(core * (rows // 2) + x_bit * quarter, quarter)
-    loads.append(pltpu.make_async_copy(x_hbm.at[pl.ds(own_row, quarter), :], rows_x, load_sem.at[7]))
-    loads.append(pltpu.make_async_copy(dy_hbm.at[pl.ds(own_row, quarter), :], rows_dy, load_sem.at[8]))
-    for load in loads:
-        load.start()
+    got_pre = load(d_pre_hbm, right.at[3], 0)
+    got_left = load(gated_t_hbm, left.at[0], 1)
+    got_other = load(dy_hbm.at[:, pl.ds(half, half)], right.at[1], 2)
+    others = [
+        load(dy_hbm.at[:, pl.ds(0, half)], right.at[0], 3),
+        load(normed_hbm.at[pl.ds(0, half), :], left.at[1], 4),
+        load(normed_hbm.at[pl.ds(half, half), :], left.at[2], 5),
+        load(d_gate_hbm, right.at[2], 6),
+        load(x_hbm.at[pl.ds(own_row, quarter), :], rows_x, 7),
+        load(dy_hbm.at[pl.ds(own_row, quarter), :], rows_dy, 8),
+    ]
 
     barrier = pltpu.get_barrier_semaphore()
-    for peer in ({"tp": near}, {"tp": across}, {"tp": diagonal}, {"dp": 1 - dp}):
+    for peer in ({"tp": near}, {"tp": across}, {"dp": 1 - dp}):
         pl.semaphore_signal(barrier, inc=1, device_id=peer, device_id_type=MESH)
 
     @pl.when(ends)
     def _():
         pl.semaphore_signal(barrier, inc=1, device_id={"ctx": inward}, device_id_type=MESH)
-        pl.semaphore_wait(barrier, 5)
+        pl.semaphore_wait(barrier, 4)
 
     @pl.when(middle)
     def _():
         pl.semaphore_signal(barrier, inc=1, device_id={"ctx": twin}, device_id_type=MESH)
         pl.semaphore_signal(barrier, inc=1, device_id={"ctx": outward}, device_id_type=MESH)
-        pl.semaphore_wait(barrier, 6)
+        pl.semaphore_wait(barrier, 5)
 
     def remote(source, target, sems, at, peer):
         return pltpu.make_async_remote_copy(
@@ -535,35 +623,49 @@
         )
 
     def y_copy(k):
-        return remote(y_out.at[k % 4], y_in.at[k % 6], y_sem, k, {"dp": 1 - dp})
+        return remote(y_out.at[k % 6], y_in.at[k % 8], y_sem, k, {"dp": 1 - dp})
 
     def a_copy(k):
-        return remote(line.at[k % 4], a_in.at[k], a_sem, k, {"ctx": inward})
+        return remote(line.at[k % 4], a_in.at[k % 10], a_sem, k, {"ctx": inward})
 
     def b_copy(k):
         return remote(line.at[k % 4], b_in.at[k % 4], b_sem, k, {"ctx": twin})
 
-    def c_copy(k):
-        w, column = chunk(k)
-        return remote(
-            total.at[k % 4], sums_hbm.at[w, :, pl.ds(column, CHUNK)], c_sem, k, {"ctx": outward}
-        )
-
-    def own_copy(k):
-        w, column = chunk(k)
-        return pltpu.make_async_copy(
-            total.at[k % 4], sums_hbm.at[w, :, pl.ds(column, CHUNK)], out_sem.at[k]
-        )
+    sums = (sums_out, sums_z, sums_x)
+
+    def far_copy(k, ref):
+        spot = ref.at[:, pl.ds(chunk(k)[1], CHUNK)]
+        return remote(total.at[k % 4], spot, c_sem, k, {"ctx": outward})
+
+    def own_copy(k, ref):
+        spot = ref.at[:, pl.ds(chunk(k)[1], CHUNK)]
+        return pltpu.make_async_copy(total.at[k % 4], spot, out_sem.at[k])
+
+    def give_c(k, start):
+        for w, ref in enumerate(sums):
+
+            @pl.when(k // per_weight == w)
+            def _():
+                far, own = far_copy(k, ref), own_copy(k, ref)
+                if start:
+                    far.start()
+                    own.start()
+                else:
+                    far.wait_send()
+                    own.wait()
+
+    def wait_c(k):
+        far_copy(k, sums_out).wait_recv()
 
     def send_y(k):
         w, column = chunk(k)
         up = (w + 1) // 2
 
-        @pl.when(k >= 4)
+        @pl.when(k >= 6)
         def _():
-            y_copy(k - 4).wait_send()
-
-        y_out[k % 4] = product(2 * up, w + 1, column).astype(BF16)
+            y_copy(k - 6).wait_send()
+
+        y_out[k % 6] = product(2 * up, w + 1, column).astype(BF16)
         y_copy(k).start()
 
     def take_y(k):
@@ -571,13 +673,17 @@
         up = (w + 1) // 2
         value = product(up, w + up, column)
         y_copy(k).wait_recv()
-        value = value + y_in[k % 6].astype(F32)
+        value = value + y_in[k % 8].astype(F32)
 
         @pl.when(ends)
         def _():
             @pl.when(k >= 4)
             def _():
                 a_copy(k - 4).wait_send()
+
+            @pl.when(k >= 10)
+            def _():
+                wait_c(k - 10)
 
             line[k % 4] = value.astype(BF16)
             a_copy(k).start()
@@ -594,7 +700,7 @@
                 b_copy(k - 4).wait_send()
 
             a_copy(k).wait_recv()
-            line[k % 4] = (first[k % 2] + a_in[k].astype(F32)).astype(BF16)
+            line[k % 4] = (first[k % 2] + a_in[k % 10].astype(F32)).astype(BF16)
             b_copy(k).start()
 
     def take_b(k):
@@ -602,46 +708,244 @@
         def _():
             @pl.when(k >= 4)
             def _():
-                c_copy(k - 4).wait_send()
-                own_copy(k - 4).wait()
+                give_c(k - 4, False)
 
             b_copy(k).wait_recv()
             total[k % 4] = (line[k % 4].astype(F32) + b_in[k % 4].astype(F32)).astype(BF16)
-            c_copy(k).start()
-            own_copy(k).start()
+            give_c(k, True)
 
     def tick(k, _):
-        @pl.when(k + 2 < parts)
+        @pl.when((k >= 2 * LAG) & (k < parts + 2 * LAG))
         def _():
-            send_y(k + 2)
-
-        @pl.when((k >= 1) & (k < parts + 1))
+            take_b(k - 2 * LAG)
+
+        @pl.when((k >= LAG) & (k < parts + LAG))
         def _():
-            take_a(k - 1)
+            take_a(k - LAG)
 
         @pl.when(k < parts)
         def _():
             take_y(k)
 
-        @pl.when((k >= 2) & (k < parts + 2))
+        @pl.when(k + AHEAD < parts)
         def _():
-            take_b(k - 2)
+            send_y(k + AHEAD)
 
         return 0
 
     def ticks(begin, end):
         lax.fori_loop(begin, end, tick, 0)
 
-    for load in loads[:2]:
-        load.wait()
-    send_y(0)
-    send_y(1)
-    for load in loads[2:7]:
-        load.wait()
+    got_pre.wait()
+    p_out[:, :LANES] = contract_last(right[3], w_step_ref[...]).astype(BF16)
+    p_out[:, LANES:] = d_bc_ref[...].astype(BF16)
+    p_copy = remote(p_out, p_in, proj_sem, 0, {"tp": near})
+    p_copy.start()
+    got_gated = load(gated_hbm, right.at[3], 0)
+    got_left.wait()
+    got_other.wait()
+    for k in range(AHEAD):
+        send_y(k)
+    p_copy.wait_recv()
+    q_out[...] = (p_out[...].astype(F32) + p_in[...].astype(F32)).astype(BF16)
+    q_copy = remote(q_out, q_in, proj_sem, 1, {"tp": across})
+    q_copy.start()
 
     block = w_x.shape[0]
     send_row = pl.multiple_of((1 - core) * (rows // 2), rows // 2)
     keep_row = pl.multiple_of(core * (rows // 2), rows // 2)
+    give = pl.multiple_of((1 - x_bit) * quarter, quarter)
+    have = pl.multiple_of(x_bit * quarter, quarter)
+
+    got_gated.wait()
+
+    def out_columns(d, _):
+        at = pl.multiple_of(d * block, block)
+        copy = pltpu.make_async_copy(w_out_hbm.at[:, pl.ds(at, block)], x_cols, w_sem.at[0])
+        copy.start()
+        copy.wait()
+        core_out[:, pl.ds(at, block)] = jnp.dot(
+            right[3, pl.ds(send_row, rows // 2), :], x_cols[...], preferred_element_type=F32
+        ).astype(BF16)
+        kept[:, pl.ds(at, block)] = jnp.dot(
+            right[3, pl.ds(keep_row, rows // 2), :], x_cols[...], preferred_element_type=F32
+        ).astype(BF16)
+        return 0
+
+    lax.fori_loop(0, width // block, out_columns, 0)
+    core_copy = remote(core_out, core_in, tp_sem, 0, {"tp": near})
+    core_copy.start()
+
+    def chain_loads(q):
+        at = pl.ds(q * WIDE, WIDE)
+        return (
+            pltpu.make_async_copy(
+                drive_hbm.at[:, at], drive.at[pl.ds(SEGS, rows), :], chain_sem.at[0]
+            ),
+            pltpu.make_async_copy(
+                inner_hbm.at[:, at], inner_low.at[pl.ds(2 * SEGS, rows), :], chain_sem.at[1]
+            ),
+            pltpu.make_async_copy(
+                halo_hbm.at[:, at], inner_low.at[pl.ds(0, 2 * SEGS), :], chain_sem.at[2]
+            ),
+        )
+
+    for copy in chain_loads(0):
+        copy.start()
+    for copy in others:
+        copy.wait()
+
+    ticks(0, 2)
+
+    core_copy.wait_recv()
+
+    def to_across():
+        x_out[...] = (
+            kept[pl.ds(give, quarter), :].astype(F32) + core_in[pl.ds(give, quarter), :].astype(F32)
+        ).astype(BF16)
+
+    to_across()
+    x_copy = remote(x_out, x_in, tp_sem, 1, {"tp": across})
+    x_copy.start()
+
+    q_copy.wait_recv()
+    projected = q_out[...].astype(F32) + q_in[...].astype(F32)
+    p_copy.wait_send()
+    p_out[...] = projected.astype(BF16)
+    turned_p[...] = projected.T.astype(BF16)
+
+    zeros = jnp.zeros((SEGS, WIDE), F32)
+    strip = 64
+    pad = 2 * SEGS
+    drive[0:SEGS, :] = zeros
+    drive[rows + SEGS :, :] = zeros
+
+    def chain(q):
+        cut = slice(q * WIDE, (q + 1) * WIDE)
+        for copy in chain_loads(q):
+            copy.wait()
+        inner[...] = inner_low[...].astype(F32)
+        taps = [taps_ref[i : i + 1, cut] for i in range(K + 1)]
+
+        def down(r, sums):
+            at = pl.multiple_of(r * strip, strip)
+            mask = masks_ref[pl.ds(at + SEGS, strip), :]
+            valid = [mask[:, i : i + 1] for i in range(K - 1)]
+            near_rows = inner[pl.ds(at, strip + pad), :]
+            moved = [near_rows[pad - (K - 1) + i :][:strip] for i in range(K)]
+            moved = [moved[i] * valid[i] for i in range(K - 1)] + moved[K - 1 :]
+            pre = taps[K] + taps[K - 1] * moved[K - 1]
+            for i in range(K - 1):
+                pre = pre + taps[i] * moved[i]
+            sig = jax.nn.sigmoid(pre)
+            active[pl.ds(at, strip), :] = (pre * sig).astype(BF16)
+            whole = drive[pl.ds(at + SEGS, strip), :] + contract_last(
+                p_out[pl.ds(at, strip), :], w_proj_ref[cut, :]
+            )
+            grad = whole * sig * (1.0 + pre * (1.0 - sig))
+            drive[pl.ds(at + SEGS, strip), :] = grad
+
+            def fold(value):
+                return jnp.sum(value.reshape(strip // SEGS, SEGS, WIDE), axis=0)
+
+            terms = [grad * m for m in moved] + [grad]
+            return tuple(s + fold(t) for s, t in zip(sums, terms))
+
+        sums_q = lax.fori_loop(0, rows // strip, down, (zeros,) * (K + 1))
+        for i in range(K + 1):
+            pack[i : i + 1, cut] = jnp.sum(sums_q[i], axis=0, keepdims=True)
+
+        def spread(base, size):
+            grads = drive[pl.ds(base + SEGS, size + SEGS), :]
+            mask = masks_ref[pl.ds(base + SEGS, size + SEGS), :]
+            value = grads[:size] * taps[K - 1]
+            for back in range(1, K):
+                valid = grads * mask[:, K - 1 - back : K - back]
+                value = value + valid[back : back + size] * taps[K - 1 - back]
+            return value
+
+        def up(r, _):
+            at = pl.multiple_of(r * strip, strip)
+            right[3, pl.ds(at, strip), cut] = spread(at, strip).astype(BF16)
+            return 0
+
+        lax.fori_loop(0, rows // strip, up, 0)
+        tail[:, cut] = spread(rows - pad, pad)
+        halo_out[:, cut] = spread(-SEGS, SEGS)
+        pack[4 * SEGS : 4 * SEGS + R + 2 * N, cut] = jnp.dot(
+            turned_p[...], active[...], preferred_element_type=F32
+        )[: R + 2 * N]
+
+    for q in range(rows // WIDE):
+        chain(q)
+        if q + 1 < rows // WIDE:
+            for copy in chain_loads(q + 1):
+                copy.start()
+            ticks(2 * q + 2, 2 * q + 4)
+    halo_copy = remote(halo_out, halo_in, halo_sem, 0, {"ctx": jnp.maximum(z - 1, 0)})
+
+    @pl.when(z > 0)
+    def _():
+        halo_copy.start()
+
+    ticks(8, 10)
+
+    def gather(ref, source, base):
+        copies = []
+        for side in range(2):
+            place = pl.multiple_of((dp + side - 2 * dp * side) * half, half)
+            spot = ref.at[pl.ds(own_row, quarter), pl.ds(place, half)]
+            piece = source.at[:, pl.ds(side * half, half)]
+            for p, peer in enumerate((across, near)):
+                copies.append(remote(piece, spot, final_sem, base + 2 * p + side, {"tp": peer}))
+            copies.append(pltpu.make_async_copy(piece, spot, load_sem.at[9 + base // 2 + side]))
+        for copy in copies:
+            copy.start()
+        return copies
+
+    def forward(ref, copies, base):
+        copies[0].wait_recv()
+        copies[3].wait_recv()
+        row = pl.multiple_of(core * (rows // 2) + (1 - x_bit) * quarter, quarter)
+        spot = ref.at[pl.ds(row, quarter), :]
+        fetch = pltpu.make_async_copy(spot, passed, load_sem.at[15])
+        fetch.start()
+        fetch.wait()
+        copy = remote(passed, spot, final_sem, base + 4, {"tp": near})
+        copy.start()
+        return copy
+
+    def finished(copies, last):
+        for k, copy in enumerate(copies):
+            if k in (0, 3):
+                copy.wait_send()
+            else:
+                copy.wait()
+        last.wait()
+
+    x_copy.wait_recv()
+
+    def summed_rows():
+        return (
+            kept[pl.ds(have, quarter), :].astype(F32)
+            + core_in[pl.ds(have, quarter), :].astype(F32)
+            + x_in[...].astype(F32)
+        )
+
+    final[...] = (rows_x[...].astype(F32) + summed_rows()).astype(BF16)
+    out_copies = gather(out_hbm, final, 0)
+
+    @pl.when(z < 3)
+    def _():
+        halo_copy.wait_recv()
+        tail[SEGS:, :] = tail[SEGS:, :] + halo_in[...]
+
+    right[3, rows - pad :, :] = tail[...].astype(BF16)
+
+    ticks(10, 12)
+
+    core_copy.wait_send()
+    x_copy.wait_send()
 
     def columns(d, _):
         at = pl.multiple_of(d * block, block)
@@ -654,89 +958,81 @@
             copy.start()
         for copy in copies:
             copy.wait()
-        sums = jnp.zeros((SEGS, block), F32)
+        sums_d = jnp.zeros((SEGS, block), F32)
         for row, keep in ((send_row, False), (keep_row, True)):
             span = pl.ds(row, rows // 2)
             value = contract_last(right[3, span, :], w_x[...])
             value = value + contract_last(right[2, span, :], w_z[...])
             hat = x_cols[span, :].astype(F32) * rms_ref[span, :]
-            sums = sums + jnp.sum((value * hat).reshape(rows // 2 // SEGS, SEGS, block), axis=0)
-            if keep:
-                kept[:, pl.ds(at, block)] = value
-            else:
-                core_out[:, pl.ds(at, block)] = value.astype(BF16)
-        gain_sum[:, pl.ds(at, block)] = sums
+            sums_d = sums_d + jnp.sum(
+                (value * hat).reshape(rows // 2 // SEGS, SEGS, block), axis=0
+            )
+            target = kept if keep else core_out
+            target[:, pl.ds(at, block)] = value.astype(BF16)
+        gain_sum[:, pl.ds(at, block)] = sums_d
         return 0
 
     lax.fori_loop(0, width // block, columns, 0)
-    core_copy = remote(core_out, core_in, tp_sem, 0, {"tp": near})
-    core_copy.start()
     gain_copy = remote(gain_sum, gain_core, gain_sem, 0, {"tp": near})
     gain_copy.start()
-
-    ticks(0, 1)
-
-    core_copy.wait_recv()
-    give = pl.multiple_of((1 - x_bit) * quarter, quarter)
-    have = pl.multiple_of(x_bit * quarter, quarter)
-    x_out[...] = (
-        kept[pl.ds(give, quarter), :] + core_in[pl.ds(give, quarter), :].astype(F32)
-    ).astype(BF16)
-    x_copy = remote(x_out, x_in, tp_sem, 1, {"tp": across})
-    x_copy.start()
     gain_copy.wait_recv()
+    core_again = remote(core_out, core_in, tp_sem, 2, {"tp": near})
+    core_again.start()
     gain_out[...] = gain_sum[...] + gain_core[...]
     gain_across = remote(gain_out, gain_x, gain_sem, 1, {"tp": across})
     gain_across.start()
 
-    ticks(1, 2)
-
-    small_rows = small_send_ref.shape[0]
+    ticks(12, 14)
+
+    core_again.wait_recv()
+    to_across()
     gain_across.wait_recv()
+    x_again = remote(x_out, x_in, tp_sem, 3, {"tp": across})
+    x_again.start()
+
+    ticks(14, 16)
+
     both = gain_out[...] + gain_x[...]
-    quarter_w = half // 2
-    s_out[0:small_rows, :] = small_send_ref[...].astype(BF16)
-    s_out[small_rows:, :] = jnp.concatenate(
-        [both[:, half : half + quarter_w], both[:, half + quarter_w :]], axis=0
-    ).astype(BF16)
+    fine = half // 2
+    steps_half = g_step_ref.shape[0] // 2
+    base = 4 * SEGS + R + 2 * N
+    pack[K + 1 : SEGS, :] = jnp.zeros((SEGS - K - 1, 2 * fine), F32)
+    pack[SEGS : 4 * SEGS, :] = misc_ref[...]
+
+    def small_rows(index, lanes):
+        column = pl.multiple_of(index * fine, fine)
+        row = pl.multiple_of(index * steps_half, steps_half)
+        return jnp.concatenate(
+            [
+                pack[:, pl.ds(column, fine)],
+                g_step_ref[pl.ds(row, steps_half), :fine],
+                g_step_ref[pl.ds(row, steps_half), fine:],
+                both[:, lanes : lanes + fine],
+                both[:, lanes + fine : lanes + 2 * fine],
+            ],
+            axis=0,
+        )
+
+    s_out[...] = small_rows(1 - dp, half).astype(BF16)
     small_y = remote(s_out, s_in, small_sem, 0, {"dp": 1 - dp})
     small_y.start()
-
-    ticks(2, 4)
-
-    x_copy.wait_recv()
+    out_last = forward(out_hbm, out_copies, 0)
+
+    ticks(16, 18)
+
+    x_again.wait_recv()
     r_own = rms_ref[pl.ds(own_row, quarter), :]
-    d_normed = (
-        kept[pl.ds(have, quarter), :]
-        + core_in[pl.ds(have, quarter), :].astype(F32)
-        + x_in[...].astype(F32)
-    )
-    hat = rows_x_wait(loads, rows_x) * r_own
+    d_normed = summed_rows()
+    hat = rows_x[...].astype(F32) * r_own
     d_hat = d_normed * gain_ref[...]
     mean = jnp.sum(d_hat * hat, axis=1, keepdims=True) * (1.0 / width)
-    final[...] = (rows_dy[...].astype(F32) + r_own * (d_hat - hat * mean)).astype(BF16)
-    gathers = []
-    for side in range(2):
-        place = pl.multiple_of((dp + side - 2 * dp * side) * half, half)
-        spot = grad_hbm.at[pl.ds(own_row, quarter), pl.ds(place, half)]
-        source = final.at[:, pl.ds(side * half, half)]
-        for p, peer in enumerate((near, across, diagonal)):
-            gathers.append(remote(source, spot, final_sem, 2 * p + side, {"tp": peer}))
-        local = pltpu.make_async_copy(source, spot, load_sem.at[9 + side])
-        local.start()
-        loads.append(local)
-    for copy in gathers:
-        copy.start()
+    rows_dy[...] = (rows_dy[...].astype(F32) + r_own * (d_hat - hat * mean)).astype(BF16)
+    grad_copies = gather(grad_hbm, rows_dy, 6)
+
+    ticks(18, 20)
 
     small_y.wait_recv()
-    s_keep = jnp.concatenate(
-        [
-            small_keep_ref[...],
-            both[:, :quarter_w],
-            both[:, quarter_w:half],
-        ],
-        axis=0,
-    ) + s_in[...].astype(F32)
+    s_keep = small_rows(dp, 0) + s_in[...].astype(F32)
     small_a = remote(s_line, s_a, small_sem, 1, {"ctx": inward})
     small_b = remote(s_line, s_b, small_sem, 2, {"ctx": twin})
     small_c = remote(small_ref, small_ref, small_sem, 3, {"ctx": outward})
@@ -752,7 +1048,10 @@
         s_line[...] = (s_keep + s_a[...].astype(F32)).astype(BF16)
         small_b.start()
 
-    ticks(4, 6)
+    ticks(20, 22)
+
+    finished(out_copies, out_last)
+    grad_last = forward(grad_hbm, grad_copies, 6)
 
     @pl.when(middle)
     def _():
@@ -760,17 +1059,17 @@
         small_ref[...] = (s_line[...].astype(F32) + s_b[...].astype(F32)).astype(BF16)
         small_c.start()
 
-    ticks(6, parts + 2)
-
-    for k in range(parts - 4, parts):
+    ticks(22, parts + 2 * LAG)
+
+    for k in range(parts - 6, parts):
         y_copy(k).wait_send()
 
     @pl.when(ends)
     def _():
         for k in range(parts - 4, parts):
             a_copy(k).wait_send()
-        for k in range(parts):
-            c_copy(k).wait_recv()
+        for k in range(parts - 10, parts):
+            wait_c(k)
         small_a.wait_send()
         small_c.wait_recv()
 
@@ -778,99 +1077,127 @@
     def _():
         for k in range(parts - 4, parts):
             b_copy(k).wait_send()
-            c_copy(k).wait_send()
-            own_copy(k).wait()
+            far_copy(k, sums_x).wait_send()
+            own_copy(k, sums_x).wait()
         small_b.wait_send()
         small_c.wait_send()
 
-    core_copy.wait_send()
-    x_copy.wait_send()
+    @pl.when(z > 0)
+    def _():
+        halo_copy.wait_send()
+
+    q_copy.wait_send()
+    core_again.wait_send()
+    x_again.wait_send()
     gain_copy.wait_send()
     gain_across.wait_send()
     small_y.wait_send()
-    for copy in gathers:
-        copy.wait()
-    for local in loads[9:]:
-        local.wait()
-
-
-def rows_x_wait(loads, ref):
-    loads[7].wait()
-    loads[8].wait()
-    return ref[...].astype(F32)
-
-
-def finish(gated, normed, d_gate, d_inner, w_inx, w_inz, x_all, dy_all, rms, gain, small_send, small_keep):
+    finished(grad_copies, grad_last)
+
+
+def finish(
+    gated_t, gated, normed_t, d_gate, d_pre, drive, inner, halo, w_inx, w_inz, w_out, x_all, dy_all,
+    rms, gain, masks, taps, w_step, w_proj, d_bc, misc, g_step,
+):
     rows, width = x_all.shape
     channels = w_inx.shape[1]
     parts = 3 * (channels // CHUNK)
     half = width // 2
-    small = small_send.shape[0] + 2 * SEGS
+    small = 4 * SEGS + R + 2 * N + g_step.shape[0] + 2 * SEGS
+    fine = half // 2
     block = 512
     hbm = pl.BlockSpec(memory_space=pl.ANY)
     vmem = pl.BlockSpec(memory_space=pltpu.VMEM)
     dma = pltpu.SemaphoreType.DMA
     piece = (half, CHUNK)
     quarter = rows // 4
+
+    def low(*shape):
+        return pltpu.VMEM(shape, BF16)
+
+    def full(*shape):
+        return pltpu.VMEM(shape, F32)
+
     return pl.pallas_call(
         lambda *refs: finish_kernel(parts, *refs),
-        in_specs=[hbm] * 8 + [vmem] * 4,
-        out_specs=[hbm, vmem, hbm],
-        out_shape=[
-            jax.ShapeDtypeStruct((3, half, channels), BF16),
-            jax.ShapeDtypeStruct((small, small_send.shape[1]), BF16),
+        in_specs=[hbm] * 13 + [vmem] * 9,
+        out_specs=[hbm, hbm, hbm, vmem, hbm, hbm],
+        out_shape=[jax.ShapeDtypeStruct((half, channels), BF16)] * 3
+        + [
+            jax.ShapeDtypeStruct((small, fine), BF16),
+            jax.ShapeDtypeStruct((rows, width), BF16),
             jax.ShapeDtypeStruct((rows, width), BF16),
         ],
         scratch_shapes=[
-            pltpu.VMEM((3, half, rows), BF16),
-            pltpu.VMEM((4, rows, channels), BF16),
-            pltpu.VMEM((block, channels), BF16),
-            pltpu.VMEM((block, channels), BF16),
-            pltpu.VMEM((rows, block), BF16),
-            pltpu.VMEM((4,) + piece, BF16),
-            pltpu.VMEM((6,) + piece, BF16),
-            pltpu.VMEM((parts,) + piece, BF16),
-            pltpu.VMEM((4,) + piece, BF16),
-            pltpu.VMEM((4,) + piece, BF16),
-            pltpu.VMEM((2,) + piece, F32),
-            pltpu.VMEM((4,) + piece, BF16),
-            pltpu.VMEM((rows // 2, width), BF16),
-            pltpu.VMEM((rows // 2, width), BF16),
-            pltpu.VMEM((rows // 2, width), F32),
-            pltpu.VMEM((quarter, width), BF16),
-            pltpu.VMEM((quarter, width), BF16),
-            pltpu.VMEM((quarter, width), BF16),
-            pltpu.VMEM((quarter, width), BF16),
-            pltpu.VMEM((quarter, width), BF16),
-            pltpu.VMEM((SEGS, width), F32),
-            pltpu.VMEM((SEGS, width), F32),
-            pltpu.VMEM((SEGS, width), F32),
-            pltpu.VMEM((SEGS, width), F32),
-            pltpu.VMEM((small, small_send.shape[1]), BF16),
-            pltpu.VMEM((small, small_send.shape[1]), BF16),
-            pltpu.VMEM((small, small_send.shape[1]), BF16),
-            pltpu.VMEM((small, small_send.shape[1]), BF16),
-            pltpu.VMEM((small, small_send.shape[1]), BF16),
-            dma((11,)),
+            low(3, half, rows),
+            low(4, rows, channels),
+            low(block, channels),
+            low(block, channels),
+            low(rows, block),
+            low(6, *piece),
+            low(8, *piece),
+            low(10, *piece),
+            low(4, *piece),
+            low(4, *piece),
+            full(2, *piece),
+            low(4, *piece),
+            low(rows // 2, width),
+            low(rows // 2, width),
+            low(rows // 2, width),
+            low(quarter, width),
+            low(quarter, width),
+            low(quarter, width),
+            low(quarter, width),
+            low(quarter, width),
+            low(quarter, width),
+            full(SEGS, width),
+            full(SEGS, width),
+            full(SEGS, width),
+            full(SEGS, width),
+            low(small, fine),
+            low(small, fine),
+            low(small, fine),
+            low(small, fine),
+            low(small, fine),
+            low(rows, 2 * LANES),
+            low(rows, 2 * LANES),
+            low(rows, 2 * LANES),
+            low(rows, 2 * LANES),
+            low(2 * LANES, rows),
+            full(rows + 2 * SEGS, WIDE),
+            low(rows + 2 * SEGS, WIDE),
+            full(rows + 2 * SEGS, WIDE),
+            low(rows, WIDE),
+            full(4 * SEGS + R + 2 * N, channels),
+            full(2 * SEGS, channels),
+            full(SEGS, channels),
+            full(SEGS, channels),
+            dma((16,)),
             dma((3,)),
             dma((2, parts)),
             dma((2, parts)),
             dma((2, parts)),
             dma((2, parts)),
             dma((parts,)),
+            dma((2, 4)),
             dma((2, 2)),
+            dma((2, 11)),
+            dma((2, 4)),
+            dma((3,)),
             dma((2, 2)),
-            dma((2, 6)),
-            dma((2, 4)),
+            dma((2, 1)),
         ],
         compiler_params=pltpu.CompilerParams(
-            collective_id=0, has_side_effects=True, vmem_limit_bytes=63000 << 10
+            collective_id=0, has_side_effects=True, vmem_limit_bytes=63900 << 10
         ),
         cost_estimate=pl.CostEstimate(
-            flops=150_000_000_000, bytes_accessed=60_000_000, transcendentals=0
+            flops=200_000_000_000, bytes_accessed=60_000_000, transcendentals=0
         ),
         name="finish",
-    )(gated, normed, d_gate, d_inner, w_inx, w_inz, x_all, dy_all, rms, gain, small_send, small_keep)
+    )(
+        gated_t, gated, normed_t, d_gate, d_pre, drive, inner, halo, w_inx, w_inz, w_out, x_all, dy_all,
+        rms, gain, masks, taps, w_step, w_proj, d_bc, misc, g_step,
+    )
 
 
 def swap_pairs(value, axis, distance):
@@ -941,7 +1268,7 @@
     dp_index, ctx_index, tp_index = (lax.axis_index(a) for a in ("dp", "ctx", "tp"))
     paired = dp_count == 2
     half = width // dp_count
-    groups, splits = 2, 1
+    groups = 2
     fused = paired and ctx_count == 4 and tp_count == 4 and half == channels == length
 
     def turned(value, axis):
@@ -979,7 +1306,7 @@
     gain_full = joined(norm_gain, 0).astype(F32)
     w_proj = joined(x_weight, 0)
     w_step = joined(dt_weight, 0)
-    w_inx, sent = weight(in_x_weight, 0, small)
+    w_inx, sent = weight(in_x_weight, 0, None)
     w_inz, sent = weight(in_z_weight, 0, sent)
     w_out, sent = weight(out_weight, 1, sent)
     gain_full = turned(gain_full, 0)
@@ -1012,8 +1339,6 @@
     projected = tp_sum(jnp.dot(activated, w_proj, preferred_element_type=F32))
     gate_z = jnp.dot(normed, w_inz, preferred_element_type=F32)
     d_gated = contract_last(grad_all, w_out)
-    gate_sig = jax.nn.sigmoid(gate_z)
-    dy_scan = d_gated * gate_z * gate_sig
 
     step_low = projected[:, :R].astype(BF16)
     step_pre = jnp.dot(step_low, w_step, preferred_element_type=F32) + step_bias
@@ -1027,7 +1352,6 @@
         axis=1,
     )
     rate2 = decay_rate * LOG2E
-    share = channels // splits
 
     def entering(whole, rate):
         state, back, spent = whole[:N], whole[N : 2 * N], whole[2 * N : 2 * N + 1]
@@ -1053,11 +1377,23 @@
             distance *= 2
         return h_in, c_in
 
-    totals = [
-        scan_totals(step_size, activated, dy_scan, rate2, table, groups, k * share, share)
-        for k in range(splits)
-    ]
-    drive_in = activated.astype(F32)
+    *segs, whole = scan_totals(step_size, activated, d_gated, gate_z, rate2, table, groups)
+    gated_t, gated, d_gate, d_pre, d_drive, rates_d, d_bc = scan_grads(
+        step_size,
+        step_pre,
+        activated,
+        d_gated,
+        gate_z,
+        skip_full[None],
+        rate2,
+        table,
+        segs,
+        entering(whole, rate2),
+        groups,
+    )
+    rates_d = jnp.sum(rates_d, axis=0)
+    g_log, g_skip, g_bias = rates_d[:N] * decay_rate, rates_d[N], rates_d[N + 1]
+    g_step = contract_first(step_low, d_pre)
 
     def input_sum(cotangent):
         value = contract_first(normed, cotangent)
@@ -1073,41 +1409,68 @@
         value = lax.psum_scatter(value.astype(BF16), "dp", scatter_dimension=1, tiled=True)
         return lax.psum(value, "ctx").astype(F32)
 
-    branch, d_low = None, None
-    gates, pres, acts, rates_d, gateds = [], [], [], [], []
-    for k in range(splits):
-        cut = slice(k * share, (k + 1) * share)
-        seg_s, seg_h, seg_c, whole = totals[k]
-        scan, d_step, d_act, d_rate, d_bc = scan_grads(
-            step_size,
-            activated,
-            dy_scan,
-            rate2,
-            table,
-            (seg_s, seg_h, seg_c),
-            entering(whole, rate2[:, cut]),
-            groups,
-            k * share,
-            share,
+    if fused:
+        padded = jnp.pad(jnp.stack(masks, axis=1), ((SEGS, SEGS), (0, 1)))
+        before = jnp.pad(halo, ((2 * SEGS - (K - 1), 0), (0, 0)))
+        taps = jnp.pad(jnp.concatenate([taps_full, conv_shift[None]]), ((0, SEGS - K - 1), (0, 0)))
+        misc = jnp.pad(
+            jnp.concatenate([g_bias[None], g_skip[None], g_log]), ((0, 3 * SEGS - N - 2), (0, 0))
         )
-        sig, z = gate_sig[:, cut], gate_z[:, cut]
-        scan_out = scan + skip_full[cut] * drive_in[:, cut]
-        gated = (scan_out * z * sig).astype(BF16)
-        d_gate = (d_gated[:, cut] * scan_out * sig * (1.0 + z * (1.0 - sig))).astype(BF16)
-        d_pre = (d_step * jax.nn.sigmoid(step_pre[:, cut])).astype(BF16)
-        low = jnp.concatenate([contract_last(d_pre, w_step[:, cut]), d_bc[:, : 2 * N]], axis=1)
-        product = jnp.dot(gated, w_out[cut], preferred_element_type=F32)
-        gateds.append(gated)
-        branch = product if branch is None else branch + product
-        d_low = low if d_low is None else d_low + low
-        gates.append(d_gate)
-        pres.append(d_pre)
-        acts.append(d_act)
-        rates_d.append(d_rate)
-    d_gate, d_pre, d_act, d_rate, gated_out = (
-        jnp.concatenate(v, axis=-1) for v in (gates, pres, acts, rates_d, gateds)
-    )
-    d_proj = tp_sum(d_low).astype(BF16)
+        s_out, s_z, s_x, small_sum, out_natural, grad_natural = finish(
+            gated_t,
+            gated,
+            normed.T,
+            d_gate,
+            d_pre,
+            d_drive,
+            inner_x,
+            before,
+            w_inx,
+            w_inz,
+            w_out,
+            rows_all,
+            grad_all,
+            inv_rms,
+            gain_full[None],
+            padded,
+            taps,
+            w_step,
+            jnp.pad(w_proj, ((0, 0), (0, 2 * LANES - R - 2 * N))),
+            d_bc,
+            misc,
+            g_step,
+        )
+        small_sum = small_sum.astype(F32)
+        steps_half = g_step.shape[0] // 2
+        at = 4 * SEGS + R + 2 * N
+        end = at + 2 * steps_half
+        return (
+            out_natural,
+            grad_natural,
+            jnp.concatenate(
+                [
+                    jnp.sum(small_sum[end : end + SEGS], axis=0),
+                    jnp.sum(small_sum[end + SEGS :], axis=0),
+                ]
+            ),
+            s_x.astype(F32),
+            s_z.astype(F32),
+            small_sum[:K],
+            small_sum[K],
+            small_sum[4 * SEGS : at].T,
+            jnp.concatenate(
+                [small_sum[at : at + steps_half], small_sum[at + steps_half : end]], axis=1
+            ),
+            small_sum[SEGS],
+            small_sum[SEGS + 2 : SEGS + 2 + N].T,
+            small_sum[SEGS + 1],
+            s_out.astype(F32),
+        )
+
+    branch = jnp.dot(gated, w_out, preferred_element_type=F32)
+    d_proj = tp_sum(
+        jnp.concatenate([contract_last(d_pre, w_step), d_bc[:, : 2 * N]], axis=1)
+    ).astype(BF16)
 
     quarter = length // tp_count
     own_row = tp_rows() * quarter
@@ -1127,13 +1490,8 @@
 
     out_natural = whole_rows((own_in + tp_scatter(branch)).astype(BF16))
 
-    g_skip = jnp.sum(dy_scan * drive_in, axis=0)
-    g_bias = jnp.sum(d_pre.astype(F32), axis=0)
-    g_step = contract_first(step_low, d_pre)
-    g_log = jnp.sum(d_rate, axis=0) * decay_rate
-
     g_proj = contract_first(d_proj, activated)
-    d_total = d_act + dy_scan * skip_full + contract_last(d_proj, w_proj)
+    d_total = d_drive + contract_last(d_proj, w_proj)
     conv_sig = jax.nn.sigmoid(conv_pre)
     d_conv = d_total * conv_sig * (1.0 + conv_pre * (1.0 - conv_sig))
     g_shift = jnp.sum(d_conv, axis=0)
@@ -1157,60 +1515,18 @@
     packed = jnp.concatenate(
         [g_taps, g_shift[None], g_bias[None], g_skip[None], g_log, g_proj], axis=0
     )
-    if fused:
-
-        def side(index):
-            piece = half_of(packed, index, 1)
-            steps = half_of(g_step, index)
-            cut = piece.shape[1]
-            rows = [piece, steps[:, :cut], steps[:, cut:]]
-            count = sum(r.shape[0] for r in rows)
-            rows.append(jnp.zeros((-count % 16, cut), F32))
-            return jnp.concatenate(rows, axis=0)
-
-        small_send, small_keep = side(1 - dp_index), side(dp_index)
-        sums, small_sum, grad_natural = finish(
-            gated_out.T,
-            normed.T,
-            d_gate,
-            d_inner,
-            w_inx,
-            w_inz,
-            rows_all,
-            grad_all,
-            inv_rms,
-            gain_full[None],
-            small_send,
-            small_keep,
-        )
-        sums = sums.astype(F32)
-        small_sum = small_sum.astype(F32)
-        count, high, cut = packed.shape[0], g_step.shape[0] // 2, packed.shape[1] // 2
-        at = small_send.shape[0]
-        g_out, g_inz, g_inx = sums[0], sums[1], sums[2]
-        g_gain = jnp.concatenate(
-            [
-                jnp.sum(small_sum[at : at + SEGS], axis=0),
-                jnp.sum(small_sum[at + SEGS :], axis=0),
-            ]
-        )
-        packed = small_sum[:count]
-        g_step = jnp.concatenate(
-            [small_sum[count : count + high], small_sum[count + high : count + 2 * high]], axis=1
-        )
-    else:
-        g_inx, g_inz, g_out = input_sum(d_inner), input_sum(d_gate), output_sum(gated_out)
-        d_normed = tp_scatter(contract_last(d_inner, w_inx) + contract_last(d_gate, w_inz))
-        g_gain = jnp.sum(d_normed * own_hat, axis=0)
-        d_hat = d_normed * gain_full
-        d_rows = own_grad + own_rms * (
-            d_hat - own_hat * jnp.mean(d_hat * own_hat, axis=1, keepdims=True)
-        )
-        grad_natural = whole_rows(d_rows.astype(BF16))
-        g_gain = turned(lax.psum(g_gain, ("ctx", "tp")), 0)
-        g_gain = lax.psum_scatter(g_gain, "dp", scatter_dimension=0, tiled=True)
-        packed = lax.psum(lax.psum_scatter(packed, "dp", scatter_dimension=1, tiled=True), "ctx")
-        g_step = lax.psum(lax.psum_scatter(g_step, "dp", scatter_dimension=0, tiled=True), "ctx")
+    g_inx, g_inz, g_out = input_sum(d_inner), input_sum(d_gate), output_sum(gated)
+    d_normed = tp_scatter(contract_last(d_inner, w_inx) + contract_last(d_gate, w_inz))
+    g_gain = jnp.sum(d_normed * own_hat, axis=0)
+    d_hat = d_normed * gain_full
+    d_rows = own_grad + own_rms * (
+        d_hat - own_hat * jnp.mean(d_hat * own_hat, axis=1, keepdims=True)
+    )
+    grad_natural = whole_rows(d_rows.astype(BF16))
+    g_gain = turned(lax.psum(g_gain, ("ctx", "tp")), 0)
+    g_gain = lax.psum_scatter(g_gain, "dp", scatter_dimension=0, tiled=True)
+    packed = lax.psum(lax.psum_scatter(packed, "dp", scatter_dimension=1, tiled=True), "ctx")
+    g_step = lax.psum(lax.psum_scatter(g_step, "dp", scatter_dimension=0, tiled=True), "ctx")
     return (
         out_natural,
         grad_natural,

time: 700 us -> 536 us (0.77)
  waiting for transfers between devices: 98.1 us -> 27.8 us
  matrix products: 68.3 us -> 25.7 us
  other arithmetic: 88.1 us -> 55.2 us
  local copies, waits for them, and re-layouts: 62.7 us -> 48.8 us
  starting transfers between devices: 28.6 us -> 20.6 us
    ppermute x20 -> x14, waiting for transfers between devices: 80 us -> 27.8 us  [swap_pairs(): return lax.ppermute(value, axis, [(i, i ^ distance) for i in range(count)])]
    dot_general x3 -> x1, matrix products: 27.9 us -> 4.76 us  [contract_last(): lax.dot_general(left, right, (((1,), (1,)), ((), ())), preferred_element_...]
    ppermute x2 -> x1, waiting for transfers between devices: 18.1 us -> 0.01 us  [shifted(): lax.ppermute(value, axis, [(source, source + steps) for source in range(l...]
    dot_general x1, matrix products: 21 us -> 8.17 us  [per_device(): gate_z = jnp.dot(normed, w_inz, preferred_element_type=F32)]
    squeeze x1 -> x0, local copies, waits for them, and re-layouts: 10.1 us -> none  [per_device(): g_out, g_inz, g_inx = (sums[0], sums[1], sums[2])]
    select_n x6 -> x3, other arithmetic: 20.7 us -> 11 us  [ordered(): jnp.where(bit == 0, jnp.concatenate([mine, other], axis=axis), jnp.concat...]
    pallas_call x2, Pallas kernels: 128 us -> 137 us  [the longest x1 96 us: scan_grads(): pl.pallas_call(lambda *refs: grads_kernel(groups, steps, blocks, *refs),...]
    add x2 -> x0, other arithmetic: 9.05 us -> none  [the longest x1 5.59 us: per_device(): d_extended + jnp.pad(d_conv * masks[tap][:, None] * taps_full[tap], ((tap...]
  transfers between devices with their start and end apart: 22 -> 15, of which waited for: 11 -> 5; matrix products, arithmetic and copies ran while one was open for 24% -> 17% of each run, Pallas kernels for 31% -> 0%
where the time goes in v2:
time: 536 us; the launch traced here: 527 us
  Pallas kernels  346 us (65%)
  other arithmetic  55.2 us (10%)
  local copies, waits for them, and re-layouts  48.8 us (9%)
  waiting for transfers between devices  27.8 us (5%)
  matrix products  25.7 us (5%)
  starting transfers between devices  20.6 us (4%)
    pallas_call x1, Pallas kernels, finish(): pl.pallas_call(lambda *refs: finish_kernel(parts, *refs), in_specs=[hbm]...  208 us
    pallas_call x1, Pallas kernels, scan_grads(): pl.pallas_call(lambda *refs: grads_kernel(groups, steps, blocks, *refs),...  96 us
    pallas_call x1, Pallas kernels, scan_totals(): pl.pallas_call(lambda *refs: totals_kernel(groups, steps, *refs), grid=(b...  41.5 us
    ppermute x14, waiting for transfers between devices, swap_pairs(): return lax.ppermute(value, axis, [(i, i ^ distance) for i in range(count)])  27.8 us
    ppermute x14, starting transfers between devices, swap_pairs(): return lax.ppermute(value, axis, [(i, i ^ distance) for i in range(count)])  17.1 us
    dynamic_slice x6, local copies, waits for them, and re-layouts, half_of(): return lax.dynamic_slice_in_dim(value, index * size, size, axis)  14.8 us
    unnamed x67, local copies, waits for them, and re-layouts  11 us
    select_n x3, other arithmetic, ordered(): jnp.where(bit == 0, jnp.concatenate([mine, other], axis=axis), jnp.concat...  11 us
  transfers between devices with their start and end apart: 15, of which 5 were waited for; matrix products, arithmetic and copies ran while one was open for 17% of the time, Pallas kernels for 0%

profile of v2, /device:TPU:0, one launch (start us, length us, event | category | flops | bytes accessed | tf_op | source)
XLA Modules:
  0.0 526.9 jit_solution(16367939121290085651)
XLA Ops:
  0.7 2.3 constant_dynamic-slice_fusion.4
  2.9 3.0 collective-permute-start.2
  8.0 1.5 concatenate.89
  9.5 2.1 collective-permute-start
  11.6 1.8 copy.68
  13.4 2.0 collective-permute-start.8
  15.4 2.7 constant_dynamic-slice_fusion.6
  24.9 4.7 constant_dynamic-slice_fusion.3
  31.5 2.9 constant_dynamic-slice_fusion
  34.4 2.3 constant_dynamic-slice_fusion.1
  36.7 4.9 pad_maximum_fusion
  43.9 1.6 collective-permute-start.3
  45.6 3.9 fusion.25
  49.4 6.4 %copy.75.refs_2_ = bf16[2048,1024]{1,0:T(8,128)(2,1)} copy(bf16[2048,1024]{0,1:T(8,128)(2,1)} %fusion.25) | data formatting | bytes 8388608 | tf_op jit(solution)/shard_map/transpose | solution.py:1422
  56.5 11.2 %collective-permute-done.3 = bf16[512,1024]{1,0:T(8,128)(2,1)S(1)} collective-permute-done((bf16[512,1024]{1,0:T(8,128)(2,1)}, bf16[512,1024]{1,0:T(8,128)(2,1)S(1)}, u32[]{:S(2)}, u32[]{:S(2)}) %collective-permute-start.3) | collective-permute-done | bytes 1048608 | tf_op jit(solution)/shard_map/ppermute | solution.py:1205
  67.7 2.6 maximum_select_fusion
  70.3 4.5 convolution_convert_fusion.refs_6_
  74.9 3.5 collective-permute-start.4
  78.4 1.5 maximum_select_fusion.3
  80.5 1.6 collective-permute-start.12
  82.7 3.9 multiply_convert_fusion.refs_1_.refs_2_
  89.9 2.4 pad_maximum_fusion.1.refs_8_
  93.8 1.5 collective-permute-start.7
  95.3 1.4 copy.70
  96.8 6.1 %collective-permute-done.12 = bf16[512,1024]{1,0:T(8,128)(2,1)} collective-permute-done((bf16[512,1024]{1,0:T(8,128)(2,1)}, bf16[512,1024]{1,0:T(8,128)(2,1)}, u32[]{:S(2)}, u32[]{:S(2)}) %collective-permute-start.12) | collective-permute-done | bytes 1048608 | tf_op jit(solution)/shard_map/ppermute | solution.py:1205
  102.9 3.4 maximum_select_fusion.2
  106.3 1.7 collective-permute-start.11
  108.0 8.2 %fusion.23.refs_3_.refs_4_ = f32[1024,1024]{1,0:T(8,128)} fusion(bf16[1024,1024]{1,0:T(8,128)(2,1)S(1)} %maximum_select_fusion.2, bf16[1024,1024]{1,0:T(8,128)(2,1)} %param.20, f32[2048]{0:T(1024)S(1)} %pad_maximum_fusion.9, f32[1024]{0:T(1024)S(1)} %add_rsqrt_fusion, bf16[1024,1024]{1,0:T(8,128)(2,1)S(1)} %copy-done.10, bf16[1024,1024]{1,0:T(8,128)(2,1)S(1)} %copy-done.6), kind=kOutput, calls=%fused_computation.107 | convolution fusion | flops 4318035968 | bytes 12595200 | tf_op jit(solution)/shard_map/dot_general | solution.py:1340
  116.2 2.4 pad_maximum_fusion.4.refs_9_
  118.6 2.4 copy.71
  121.0 1.4 add.170
  122.7 4.5 compare_select_fusion
  127.9 5.1 maximum_select_fusion.1
  133.0 4.8 fusion.24.refs_2_.refs_3_
  137.8 41.5 %scan_totals.1 = (f32[16,1024]{1,0:T(8,128)S(1)}, f32[256,1024]{1,0:T(8,128)S(1)}, f32[256,1024]{1,0:T(8,128)S(1)}, f32[40,1024]{1,0:T(8,128)S(1)}) custom-call(f32[1024,1024]{1,0:T(8,128)S(1)} %get-tuple-element.88.refs_0_, bf16[1024,1024]{1,0:T(8,128)(2,1)S(1)} %multiply_convert_fusion.refs_1_.refs_2_, f32[1024,1024]{1,0:T(8,128)S(1)} %fusion.24.refs_2_.refs_3_, ...), custom_call_target="tpu_custom_call" | custom-call | flops 50331648000 | bytes 14680064 | tf_op jit(solution)/shard_map/scan_totals/pallas_call | solution.py:361
  180.2 5.7 %collective-permute-done.13 = f32[40,1024]{1,0:T(8,128)S(1)} collective-permute-done((f32[40,1024]{1,0:T(8,128)S(1)}, f32[40,1024]{1,0:T(8,128)S(1)}, u32[]{:S(2)}, u32[]{:S(2)}) %collective-permute-start.13) | collective-permute-done | bytes 163872 | tf_op jit(solution)/shard_map/ppermute | solution.py:1205
  186.0 1.5 collective-permute-start.14
  187.5 2.4 pad_maximum_fusion.3.refs_10_
  190.0 4.1 collective-permute-done.14
  194.2 96.0 %scan_grads.1 = (bf16[1024,1024]{1,0:T(8,128)(2,1)S(1)}, bf16[1024,1024]{1,0:T(8,128)(2,1)}, bf16[1024,1024]{1,0:T(8,128)(2,1)}, bf16[1024,1024]{1,0:T(8,128)(2,...) custom-call(f32[1024,1024]{1,0:T(8,128)} %copy-done.1, ...), custom_call_target="tpu_custom_call" | custom-call | flops 100663296000 | bytes 31457280 | tf_op jit(solution)/shard_map/scan_grads/pallas_call | solution.py:443
  292.3 2.9 fusion.10.refs_21_
  295.8 208.3 %finish.1 = (bf16[1024,1024]{1,0:T(8,128)(2,1)}, bf16[1024,1024]{1,0:T(8,128)(2,1)}, bf16[1024,1024]{1,0:T(8,128)(2,1)}, bf16[336,512]{1,0:T(8,128)(2,1)}, bf16[...) custom-call(bf16[1024,1024]{1,0:T(8,128)(2,1)} %copy-done.3, bf16[1024,1024]{1,0:T(8,128)(2,1)} %get-tuple-element.39.refs_1_, ...), custom_call_target="tpu_custom_call" | custom-call | flops 199999995904 | bytes 60000000 | tf_op jit(solution)/shard_map/finish/pallas_call | solution.py:1121
  510.3 4.1 convert_element_type.134
  514.3 2.5 convert_element_type.135
  516.8 2.6 convert_element_type.136
  520.7 2.1 copy.79
  522.9 1.6 copy-done.19
  524.4 2.0 copy.80
  (145 shorter events, 30.7 us)
Async XLA Ops:
  2.9 41.0 %collective-permute-start.2 = (bf16[512,1024]{1,0:T(8,128)(2,1)}, bf16[512,1024]{1,0:T(8,128)(2,1)}, u32[]{:S(2)}, u32[]{:S(2)}) collective-permute-start(bf16[512,1024]{1,0:T(8,128)(2,1)} %constant_dynamic-slice_fusion.4), channel_id=1, source_target_pairs={{0,16},{16,0},{1,17},{17,1},{2,18},{18,2},{3,19},{19,3},{4,20},{20... | collective-permute-start | bytes 3145736 | tf_op jit(solution)/shard_map/ppermute | solution.py:1205
  5.9 38.0 %collective-permute-start.1 = (bf16[1024]{0:T(1024)(128)(2,1)}, bf16[1024]{0:T(1024)(128)(2,1)S(1)}, u32[]{:S(2)}, u32[]{:S(2)}) collective-permute-start(bf16[1024]{0:T(1024)(128)(2,1)} %param.18), channel_id=1, source_target_pairs={{0,16},{16,0},{1,17},{17,1},{2,18},{18,2},{3,19},{19,3},{4,20},{20... | collective-permute-start | bytes 6152 | tf_op jit(solution)/shard_map/ppermute | solution.py:1205
  9.5 46.3 %collective-permute-start = (bf16[23,512]{1,0:T(8,128)(2,1)S(1)}, bf16[23,512]{1,0:T(8,128)(2,1)S(1)}, u32[]{:S(2)}, u32[]{:S(2)}) collective-permute-start(bf16[23,512]{1,0:T(8,128)(2,1)S(1)} %concatenate.89), channel_id=1, source_target_pairs={{0,16},{16,0},{1,17},{17,1},{2,18},{18,2},{3,19},{19,3},{4,20},{20... | collective-permute-start | bytes 70664 | tf_op jit(solution)/shard_map/ppermute | solution.py:1205
  13.3 65.0 %collective-permute-start.5 = (bf16[512,160]{1,0:T(8,128)(2,1)}, bf16[512,160]{1,0:T(8,128)(2,1)}, u32[]{:S(2)}, u32[]{:S(2)}) collective-permute-start(bf16[512,160]{1,0:T(8,128)(2,1)} %copy.68), channel_id=1, source_target_pairs={{0,16},{16,0},{1,17},{17,1},{2,18},{18,2},{3,19},{19,3},{4,20},{20... | collective-permute-start | bytes 491528 | tf_op jit(solution)/shard_map/ppermute | solution.py:1205
  13.4 74.8 %collective-permute-start.8 = (bf16[64,1024]{1,0:T(8,128)(2,1)}, bf16[64,1024]{1,0:T(8,128)(2,1)S(1)}, u32[]{:S(2)}, u32[]{:S(2)}) collective-permute-start(bf16[64,1024]{1,0:T(8,128)(2,1)} %param.24), channel_id=1, source_target_pairs={{0,16},{16,0},{1,17},{17,1},{2,18},{18,2},{3,19},{19,3},{4,20},{20... | collective-permute-start | bytes 393224 | tf_op jit(solution)/shard_map/ppermute | solution.py:1205
  18.0 1.3 copy-start.7
  18.0 52.2 %copy-start.5 = (bf16[1024,1024]{1,0:T(8,128)(2,1)}, bf16[1024,1024]{1,0:T(8,128)(2,1)S(1)}, u32[]{:S(2)}) copy-start(bf16[1024,1024]{1,0:T(8,128)(2,1)S(1)} %get-tuple-element.59) | copy-start | bytes 6291460
  18.1 2.3 copy-start.30
  18.1 2.3 copy-start.31
  30.6 6.1 %copy-start.8 = (bf16[1024,1024]{1,0:T(8,128)(2,1)S(1)}, bf16[1024,1024]{1,0:T(8,128)(2,1)}, u32[]{:S(2)}) copy-start(bf16[1024,1024]{1,0:T(8,128)(2,1)} %copy-done.7) | copy-start | bytes 6291460
  30.6 6.1 %copy-start.11 = (bf16[1024,1024]{1,0:T(8,128)(2,1)S(1)}, bf16[1024,1024]{1,0:T(8,128)(2,1)}, u32[]{:S(2)}) copy-start(bf16[1024,1024]{1,0:T(8,128)(2,1)} %get-tuple-element.57) | copy-start | bytes 6291460
  36.7 7.2 %copy-start.28 = (bf16[1024]{0:T(1024)(128)(2,1)S(1)}, bf16[1024]{0:T(1024)(128)(2,1)}, u32[]{:S(2)}) copy-start(bf16[1024]{0:T(1024)(128)(2,1)} %param.18) | copy-start | bytes 6148
  43.9 64.1 %copy-start.27 = (f32[2048]{0:T(1024)}, f32[2048]{0:T(1024)S(1)}, u32[]{:S(2)}) copy-start(f32[2048]{0:T(1024)S(1)} %pad_maximum_fusion.9) | copy-start | bytes 24580
  43.9 23.8 %collective-permute-start.3 = (bf16[512,1024]{1,0:T(8,128)(2,1)}, bf16[512,1024]{1,0:T(8,128)(2,1)S(1)}, u32[]{:S(2)}, u32[]{:S(2)}) collective-permute-start(bf16[512,1024]{1,0:T(8,128)(2,1)} %collective-permute-done.2), channel_id=1, source_target_pairs={{0,4},{4,0},{8,12},{12,8},{1,5},{5,1},{9,13},{13,9},{2,6},{6,2},{1... | collective-permute-start | bytes 3145736 | tf_op jit(solution)/shard_map/ppermute | solution.py:1205
  55.8 14.5 %copy-start.9 = (bf16[1024,1024]{1,0:T(8,128)(2,1)S(1)}, bf16[1024,1024]{1,0:T(8,128)(2,1)}, u32[]{:S(2)}) copy-start(bf16[1024,1024]{1,0:T(8,128)(2,1)} %copy-done.7) | copy-start | bytes 6291460
  55.8 14.5 %copy-start.14 = (bf16[1024,1024]{1,0:T(8,128)(2,1)S(1)}, bf16[1024,1024]{1,0:T(8,128)(2,1)}, u32[]{:S(2)}) copy-start(bf16[1024,1024]{1,0:T(8,128)(2,1)} %param.19) | copy-start | bytes 6291460
  55.9 23.9 %collective-permute-start.9 = (bf16[512,1024]{1,0:T(8,128)(2,1)}, bf16[512,1024]{1,0:T(8,128)(2,1)}, u32[]{:S(2)}, u32[]{:S(2)}) collective-permute-start(bf16[512,1024]{1,0:T(8,128)(2,1)} %constant_dynamic-slice_fusion), channel_id=1, source_target_pairs={{0,16},{16,0},{1,17},{17,1},{2,18},{18,2},{3,19},{19,3},{4,20},{20... | collective-permute-start | bytes 3145736 | tf_op jit(solution)/shard_map/ppermute | solution.py:1205
  74.9 11.7 %copy-start.21 = (bf16[1024,1024]{1,0:T(8,128)(2,1)}, bf16[1024,1024]{1,0:T(8,128)(2,1)S(1)}, u32[]{:S(2)}) copy-start(bf16[1024,1024]{1,0:T(8,128)(2,1)S(1)} %convolution_convert_fusion.refs_6_) | copy-start | bytes 6291460
  74.9 7.1 %collective-permute-start.4 = (bf16[3,1024]{1,0:T(4,128)(2,1)S(1)}, bf16[3,1024]{1,0:T(4,128)(2,1)S(1)}, u32[]{:S(2)}, u32[]{:S(2)}) collective-permute-start(bf16[3,1024]{1,0:T(4,128)(2,1)S(1)} %slice.165), channel_id=1, source_target_pairs={{0,4},{4,8},{8,12},{1,5},{5,9},{9,13},{2,6},{6,10},{10,14},{3,7},{... | collective-permute-start | bytes 18440 | tf_op jit(solution)/shard_map/ppermute | solution.py:35
  79.9 26.4 %collective-permute-start.10 = (bf16[512,1024]{1,0:T(8,128)(2,1)}, bf16[512,1024]{1,0:T(8,128)(2,1)}, u32[]{:S(2)}, u32[]{:S(2)}) collective-permute-start(bf16[512,1024]{1,0:T(8,128)(2,1)} %constant_dynamic-slice_fusion.1), channel_id=1, source_target_pairs={{0,16},{16,0},{1,17},{17,1},{2,18},{18,2},{3,19},{19,3},{4,20},{20... | collective-permute-start | bytes 3145736 | tf_op jit(solution)/shard_map/ppermute | solution.py:1205
  80.5 22.4 %collective-permute-start.12 = (bf16[512,1024]{1,0:T(8,128)(2,1)}, bf16[512,1024]{1,0:T(8,128)(2,1)}, u32[]{:S(2)}, u32[]{:S(2)}) collective-permute-start(bf16[512,1024]{1,0:T(8,128)(2,1)} %collective-permute-done.9), channel_id=1, source_target_pairs={{0,4},{4,0},{8,12},{12,8},{1,5},{5,1},{9,13},{13,9},{2,6},{6,2},{1... | collective-permute-start | bytes 3145736 | tf_op jit(solution)/shard_map/ppermute | solution.py:1205
  82.7 4.8 copy-start.29
  82.7 5.5 %copy-start.26 = (bf16[64,1024]{1,0:T(8,128)(2,1)S(1)}, bf16[64,1024]{1,0:T(8,128)(2,1)}, u32[]{:S(2)}) copy-start(bf16[64,1024]{1,0:T(8,128)(2,1)} %param.24) | copy-start | bytes 393220
  86.5 51.2 %copy-start = (bf16[1024,1024]{1,0:T(8,128)(2,1)}, bf16[1024,1024]{1,0:T(8,128)(2,1)S(1)}, u32[]{:S(2)}) copy-start(bf16[1024,1024]{1,0:T(8,128)(2,1)S(1)} %multiply_convert_fusion.refs_1_.refs_2_) | copy-start | bytes 6291460
  87.4 5.5 %collective-permute-start.6 = (f32[1024,160]{0,1:T(8,128)S(1)}, f32[1024,160]{0,1:T(8,128)S(1)}, u32[]{:S(2)}, u32[]{:S(2)}) collective-permute-start(f32[1024,160]{0,1:T(8,128)S(1)} %fusion.33), channel_id=1, source_target_pairs={{0,1},{1,0},{2,3},{3,2},{4,5},{5,4},{6,7},{7,6},{8,9},{9,8},{10,11... | collective-permute-start | bytes 1966088 | tf_op jit(solution)/shard_map/ppermute | solution.py:1205
  93.8 24.7 %collective-permute-start.7 = (f32[1024,160]{0,1:T(8,128)}, f32[1024,160]{0,1:T(8,128)}, u32[]{:S(2)}, u32[]{:S(2)}) collective-permute-start(f32[1024,160]{0,1:T(8,128)} %add.169), channel_id=1, source_target_pairs={{0,2},{1,3},{2,0},{3,1},{4,6},{5,7},{6,4},{7,5},{8,10},{9,11},{10,... | collective-permute-start | bytes 1966088 | tf_op jit(solution)/shard_map/ppermute | solution.py:1205
  96.8 11.2 %copy-start.6 = (bf16[1024,1024]{1,0:T(8,128)(2,1)S(1)}, bf16[1024,1024]{1,0:T(8,128)(2,1)}, u32[]{:S(2)}) copy-start(bf16[1024,1024]{1,0:T(8,128)(2,1)} %copy-done.5) | copy-start | bytes 6291460
  96.8 11.2 %copy-start.10 = (bf16[1024,1024]{1,0:T(8,128)(2,1)S(1)}, bf16[1024,1024]{1,0:T(8,128)(2,1)}, u32[]{:S(2)}) copy-start(bf16[1024,1024]{1,0:T(8,128)(2,1)} %copy-done.7) | copy-start | bytes 6291460
  106.2 9.9 %copy-start.15 = (bf16[1024,1024]{1,0:T(8,128)(2,1)S(1)}, bf16[1024,1024]{1,0:T(8,128)(2,1)}, u32[]{:S(2)}) copy-start(bf16[1024,1024]{1,0:T(8,128)(2,1)} %param.20) | copy-start | bytes 6291460
  106.3 21.6 %collective-permute-start.11 = (bf16[512,1024]{1,0:T(8,128)(2,1)}, bf16[512,1024]{1,0:T(8,128)(2,1)}, u32[]{:S(2)}, u32[]{:S(2)}) collective-permute-start(bf16[512,1024]{1,0:T(8,128)(2,1)} %collective-permute-done.10), channel_id=1, source_target_pairs={{0,4},{4,0},{8,12},{12,8},{1,5},{5,1},{9,13},{13,9},{2,6},{6,2},{1... | collective-permute-start | bytes 3145736 | tf_op jit(solution)/shard_map/ppermute | solution.py:1205
  120.9 1.5 copy-start.24
  121.0 1.7 copy-start.25
  122.4 4.8 copy-start.17
  122.7 10.3 %copy-start.16 = (bf16[1024,1024]{1,0:T(8,128)(2,1)S(1)}, bf16[1024,1024]{1,0:T(8,128)(2,1)}, u32[]{:S(2)}) copy-start(bf16[1024,1024]{1,0:T(8,128)(2,1)} %param.28) | copy-start | bytes 6291460
  127.2 10.5 %copy-start.1 = (f32[1024,1024]{1,0:T(8,128)}, f32[1024,1024]{1,0:T(8,128)S(1)}, u32[]{:S(2)}) copy-start(f32[1024,1024]{1,0:T(8,128)S(1)} %get-tuple-element.88.refs_0_) | copy-start | bytes 12582916
  127.2 5.7 %copy-start.12 = (bf16[1024,1024]{1,0:T(8,128)(2,1)S(1)}, bf16[1024,1024]{1,0:T(8,128)(2,1)}, u32[]{:S(2)}) copy-start(bf16[1024,1024]{1,0:T(8,128)(2,1)} %get-tuple-element.57) | copy-start | bytes 6291460
  127.2 5.7 %copy-start.13 = (bf16[1024,1024]{1,0:T(8,128)(2,1)S(1)}, bf16[1024,1024]{1,0:T(8,128)(2,1)}, u32[]{:S(2)}) copy-start(bf16[1024,1024]{1,0:T(8,128)(2,1)} %get-tuple-element.58) | copy-start | bytes 6291460
  137.7 41.5 %copy-start.2 = (f32[1024,1024]{1,0:T(8,128)}, f32[1024,1024]{1,0:T(8,128)S(1)}, u32[]{:S(2)}) copy-start(f32[1024,1024]{1,0:T(8,128)S(1)} %fusion.24.refs_2_.refs_3_) | copy-start | bytes 12582916
  179.3 6.6 %collective-permute-start.13 = (f32[40,1024]{1,0:T(8,128)S(1)}, f32[40,1024]{1,0:T(8,128)S(1)}, u32[]{:S(2)}, u32[]{:S(2)}) collective-permute-start(f32[40,1024]{1,0:T(8,128)S(1)} %pad_maximum_fusion.6), channel_id=1, source_target_pairs={{0,4},{4,0},{8,12},{12,8},{1,5},{5,1},{9,13},{13,9},{2,6},{6,2},{1... | collective-permute-start | bytes 491528 | tf_op jit(solution)/shard_map/ppermute | solution.py:1205
  186.0 8.0 %collective-permute-start.14 = (f32[40,1024]{1,0:T(8,128)S(1)}, f32[40,1024]{1,0:T(8,128)S(1)}, u32[]{:S(2)}, u32[]{:S(2)}) collective-permute-start(f32[40,1024]{1,0:T(8,128)S(1)} %pad_maximum_fusion.7), channel_id=1, source_target_pairs={{0,8},{4,12},{8,0},{12,4},{1,9},{5,13},{9,1},{13,5},{2,10},{6,14},... | collective-permute-start | bytes 491528 | tf_op jit(solution)/shard_map/ppermute | solution.py:1205
  194.1 98.1 %copy-start.18 = (f32[1024,160]{1,0:T(8,128)S(1)}, f32[1024,160]{1,0:T(8,128)}, u32[]{:S(2)}) copy-start(f32[1024,160]{1,0:T(8,128)} %copy-done.17) | copy-start | bytes 1966084
  290.1 1.3 copy-start.3
  291.4 0.8 copy-start.4
  504.1 10.2 %copy-start.23 = (bf16[1024,1024]{1,0:T(8,128)(2,1)S(1)}, bf16[1024,1024]{1,0:T(8,128)(2,1)}, u32[]{:S(2)}) copy-start(bf16[1024,1024]{1,0:T(8,128)(2,1)} %get-tuple-element.49) | copy-start | bytes 6291460
  514.3 2.5 copy-start.22
  516.8 3.9 copy-start.20
  520.7 3.7 copy-start.19
